TPU v7x, 32 devices: a whole 2x2x4 slice. The times are simulated.
32 devices in a mesh: pair: 8 (over z, x), aux: 4 (over y, core).
Axes of the slice: x: 2, y: 2, z: 4, core: 2. Of those that a mesh axis runs over, the one named last changes fastest.
Arguments:
- panels: bfloat16 [16, 120, 9216], P('pair', None, 'aux'), may hold values from -1.5 to 1.5
- amplitudes: bfloat16 [16, 2, 120, 120], P('pair'), may hold values from -0.5 to 0.5
- drive: float32 [16, 2, 14400], P('pair', None, 'aux'), may hold values from -6 to 6
- pno_energy: float32 [16, 120], P('pair'), may hold values from 1 to 3
- occ_energy: float32 [32], replicated, may hold values from -2 to -0.5
- frequency: float32 [1], replicated, may hold values from 0.2 to 2
- pair_lmo: int32 [16, 2], replicated, may hold values from 0 to 31
- neighbours: int32 [16, 8], P('pair'), may hold values from 0 to 15
- pno_ranks: int32 [16], P('pair'), may hold values from 60 to 120
- fock_off: float32 [32, 32], replicated, may hold values from -1.8 to 1.8
Outputs:
- residual: float32 [16, 2, 14400], P('pair', None, 'aux')
Inputs may be any that keep to these rules, and one draw needn't show every extreme that they name: `neighbours`: neighbour pairs; a pair may be listed more than once and may list itself. `pno_ranks`: rows of a pair's panel from its rank on are padding.
All inputs are finite; a program needn't handle non-finite values.
Results may differ from a plain program's by a relative error of at most 0.0033.
Values may be sent and summed in bfloat16 or wider, within the bound.
No kernel may reach another device: no remote copies, remote signals or barrier semaphores. Data moves between devices by JAX's collectives and lax.ppermute only.
A program may use at most 128 MiB of HBM per device.

v0:
```python
import functools

import jax
import jax.numpy as jnp
from jax import lax
from jax.experimental import pallas as pl
from jax.experimental.pallas import tpu as pltpu
from jax.sharding import PartitionSpec as P


LANES = 128
BF = jnp.bfloat16
F32 = jnp.float32


def round_up(value, unit):
    return -(-value // unit) * unit


def flip(count, bits):
    return [(i, i ^ bits) for i in range(count)]


def prep_kernel(n_pair, blocks, rows, sides, *refs):
    inputs, chunks, share_ref = refs[:6], refs[6 : 6 + n_pair], refs[6 + n_pair]
    buffers, (turned, sems) = refs[7 + n_pair : 13 + n_pair], refs[13 + n_pair :]
    copies = [
        pltpu.make_async_copy(src, dst, sems.at[i])
        for i, (src, dst) in enumerate(zip(inputs, buffers))
    ]
    for copy in copies:
        copy.start()
    panels, amps, lmo, near, ranks, fock = buffers
    local, rank, width = panels.shape
    depth = turned.shape[2]
    rows_pad = depth // blocks
    part = width // n_pair
    me = lax.axis_index("pair")
    freq = lax.axis_index("aux") % 2 if sides == 2 else 0
    slots = near.shape[1]
    for copy in copies:
        copy.wait()

    def spread_rows(x, lanes):
        pieces = []
        for h in range(blocks):
            pieces.append(x[h * rows : (h + 1) * rows])
            if rows_pad > rows:
                pieces.append(jnp.zeros((rows_pad - rows, lanes), x.dtype))
        return jnp.concatenate(pieces, axis=0) if len(pieces) > 1 else pieces[0]

    tile = 256 if width % 256 == 0 else LANES
    for lp in range(local):
        keep = lax.broadcasted_iota(jnp.int32, (rank, tile), 0) < ranks[lp]
        for t in range(width // tile):
            x = panels[lp, :, t * tile : (t + 1) * tile].astype(F32)
            x = spread_rows(jnp.where(keep, x, 0.0), tile)
            turned[lp, t * tile : (t + 1) * tile, :] = x.T.astype(BF)
    for k in range(n_pair):
        start = pl.multiple_of((me ^ k) * part, 16)
        for lp in range(local):
            chunks[k][lp] = turned[lp, pl.ds(start, part), :]

    share_rows = share_ref.shape[0]
    freqs = amps.shape[1] * depth * local // (share_rows - 16)
    take = amps.shape[1] // freqs
    for lp in range(local):
        for s in range(take):
            a = amps[lp, freq * take + s].astype(F32)
            a = spread_rows(a, rank)
            a = jnp.concatenate([a, jnp.zeros((depth, LANES - rank), F32)], axis=1)
            first = (lp * take + s) * depth
            share_ref[first : first + depth, :] = a.astype(BF)

    row = lax.broadcasted_iota(jnp.int32, (16, LANES), 0)
    lane = lax.broadcasted_iota(jnp.int32, (16, LANES), 1)
    tail = jnp.zeros((16, LANES), F32)
    for lp in range(local):
        left, right = lmo[0, me * local + lp], lmo[1, me * local + lp]
        ids = [near[lp, k] for k in range(slots)]
        values = [fock[left, lmo[0, i]] + fock[right, lmo[1, i]] for i in ids]
        for k in range(slots):
            total = jnp.float32(0.0)
            fresh = jnp.float32(1.0)
            for j in range(slots):
                same = (ids[j] == ids[k]).astype(F32) if j != k else jnp.float32(1.0)
                total = total + same * values[j]
                if j < k:
                    fresh = fresh * (1.0 - same)
            here = lane == lp * slots + k
            tail = jnp.where(here & (row == 0), ids[k].astype(F32), tail)
            tail = jnp.where(here & (row == 1), total * fresh, tail)
    share_ref[share_rows - 16 :, :] = tail.astype(BF)


def couple_kernel(n_pair, blocks, sides, where, ids_ref, w_ref, *refs):
    half = n_pair // 2
    panels, mats = refs[:n_pair], refs[n_pair : n_pair + half * sides]
    out_ref, proj, mixed = refs[n_pair + half * sides :]
    local, part, depth = panels[0].shape
    freqs = proj.shape[2] // LANES
    rows = depth // blocks
    slots = ids_ref.shape[2]
    me, my_core = where[0], where[1]
    take = freqs // sides

    for k in range(n_pair):
        for lp in range(local):
            for s in range(freqs):
                slot, inner = s // take, s % take
                first = (lp * take + inner) * depth
                mat = mats[slot * half + k % half][k // half, first : first + depth, :]
                proj[k * local + lp, :, s * LANES : (s + 1) * LANES] = jnp.dot(
                    panels[k][lp], mat, preferred_element_type=F32
                )

    tile = 32 if part % 32 == 0 else 16
    for k in range(n_pair):
        for lp in range(local):
            source = []
            for j in range(slots):
                i = ids_ref[k, lp, j]
                source.append(((i // local) ^ me) * local + i % local)
            scale = [w_ref[k, lp, j] for j in range(slots)]
            for t in range(part // tile):
                span = slice(t * tile, (t + 1) * tile)
                acc = scale[0] * proj[source[0], span, :]
                for j in range(1, slots):
                    acc = acc + scale[j] * proj[source[j], span, :]
                mixed[span, :] = acc.astype(BF)
            got = lax.dot_general(
                panels[k][lp], mixed[...], (((0,), (0,)), ((), ())), preferred_element_type=F32
            )
            for h in range(blocks):
                side = my_core ^ (h % 2) if blocks > 1 else 0
                for s in range(freqs):
                    freq = (s // take ^ my_core) * take + s % take if sides == 2 else s
                    out_ref[side, me ^ k, h // 2, lp, freq] = got[
                        h * rows : (h + 1) * rows, s * LANES : (s + 1) * LANES
                    ].astype(out_ref.dtype)


def body(sizes, panels, amplitudes, drive, pno_energy, occ_energy, frequency, pair_lmo,
         neighbours, pno_ranks, fock_off):
    n_pair, n_aux = sizes
    local, rank, width = panels.shape
    freqs = amplitudes.shape[1]
    total = pair_lmo.shape[0]
    slots = neighbours.shape[1]
    even = rank % n_aux == 0 and n_aux % 2 == 0
    blocks = n_aux if even else 1
    rows = rank // blocks
    rows_pad = round_up(rows, 16)
    depth = round_up(blocks * rows_pad, LANES)
    rows_pad = depth // blocks
    part = width // n_pair
    me_pair = lax.axis_index("pair")
    me_aux = lax.axis_index("aux")
    sides = 2 if n_aux % 2 == 0 and freqs % 2 == 0 else 1
    my_core = me_aux % 2 if sides == 2 else jnp.int32(0)
    where = jnp.stack([me_pair, my_core]).astype(jnp.int32)
    vmem = pl.BlockSpec(memory_space=pltpu.VMEM)
    smem = pl.BlockSpec(memory_space=pltpu.SMEM)

    share_rows = local * (freqs // sides) * depth + 16
    given = (panels, amplitudes, pair_lmo.T, neighbours, pno_ranks, fock_off)
    spaces = [pltpu.VMEM] * 2 + [pltpu.SMEM] * 4
    outs = pl.pallas_call(
        functools.partial(prep_kernel, n_pair, blocks, rows, sides),
        out_shape=[jax.ShapeDtypeStruct((local, part, depth), BF)] * n_pair
        + [jax.ShapeDtypeStruct((share_rows, LANES), BF)],
        in_specs=[pl.BlockSpec(memory_space=pltpu.HBM)] * 6,
        out_specs=[vmem] * (n_pair + 1),
        scratch_shapes=[space(a.shape, a.dtype) for space, a in zip(spaces, given)]
        + [pltpu.VMEM((local, width, depth), BF), pltpu.SemaphoreType.DMA((6,))],
        cost_estimate=pl.CostEstimate(flops=0, bytes_accessed=4 * 2**20, transcendentals=0),
    )(*given)
    chunks, share = outs[:n_pair], outs[n_pair]

    far = n_pair // 2
    other = lax.ppermute(share, "pair", flip(n_pair, far))
    pieces = [jnp.concatenate([share[None], other[None]], axis=0)] + [None] * (far - 1)
    received = [chunks[0]] + [None] * (n_pair - 1)
    for k in range(1, n_pair):
        if k < far:
            pieces[k] = lax.ppermute(pieces[0], "pair", flip(n_pair, k))
        received[k] = lax.ppermute(chunks[k], "pair", flip(n_pair, k))
    tail = jnp.stack([piece[:, share_rows - 16 :] for piece in pieces], axis=1)
    tail = tail.reshape(n_pair, 16, LANES)
    ids = tail[:, 0, : local * slots].reshape(n_pair, local, slots).astype(jnp.int32)
    scale = tail[:, 1, : local * slots].reshape(n_pair, local, slots).astype(F32)
    if sides == 2:
        for k in range(far):
            pieces.append(lax.ppermute(pieces[k], "aux", flip(n_aux, 1)))

    out_dims = (2 if even else 1, n_pair, max(blocks // 2, 1), local, freqs, rows_pad, LANES)
    flops = 4 * total * part * depth * freqs * LANES
    coupled = pl.pallas_call(
        functools.partial(couple_kernel, n_pair, blocks, sides),
        out_shape=jax.ShapeDtypeStruct(out_dims, BF if even else F32),
        in_specs=[smem] * 3 + [vmem] * (n_pair + far * sides),
        out_specs=vmem,
        scratch_shapes=[
            pltpu.VMEM((total, part, freqs * LANES), F32),
            pltpu.VMEM((part, freqs * LANES), BF),
        ],
        compiler_params=pltpu.CompilerParams(vmem_limit_bytes=40 * 2**20),
        cost_estimate=pl.CostEstimate(flops=flops, bytes_accessed=4 * 2**20, transcendentals=0),
    )(where, ids, scale, *received, *pieces)

    if even:
        other = lax.ppermute(coupled[1], "aux", flip(n_aux, 1))
        mine = (coupled[0].astype(F32) + other.astype(F32)).astype(BF)
        mine = mine.reshape((n_pair * (n_aux // 2),) + out_dims[3:])
        groups = [
            [g * n_aux + 2 * h + c for g in range(n_pair) for h in range(n_aux // 2)]
            for c in range(2)
        ]
        parts = lax.all_to_all(
            mine, ("pair", "aux"), 0, 0, axis_index_groups=groups, tiled=True
        )
        coupled_share = jnp.sum(parts.astype(F32), axis=0)[:, :, :rows, :rank].reshape(
            local, freqs, rows * rank
        )
    else:
        flat = coupled.reshape(total, freqs, depth, LANES)[:, :, :rank, :rank]
        flat = flat.reshape(total, freqs, rank * rank)
        share_aux = lax.psum_scatter(flat, "aux", scatter_dimension=2, tiled=True)
        coupled_share = lax.psum_scatter(share_aux, "pair", scatter_dimension=0, tiled=True)

    share_width = drive.shape[2]
    start = me_aux * share_width
    lmo_ids = jnp.arange(occ_energy.shape[0], dtype=jnp.int32)
    own_lmo = lax.dynamic_slice_in_dim(pair_lmo, me_pair * local, local, 0)
    own_table = (own_lmo[:, :, None] == lmo_ids[None, None, :]).astype(F32)
    occ_pair = jnp.sum(own_table * occ_energy[None, None, :], axis=(1, 2))
    signs = jnp.array([1.0, -1.0], F32)
    if even:
        energy_rows = lax.dynamic_slice_in_dim(pno_energy, me_aux * rows, rows, 1)
        shift = energy_rows[:, :, None] + pno_energy[:, None, :] - occ_pair[:, None, None]
        factor = shift[:, None] - signs[None, :, None, None] * frequency[0]
        amp_rows_own = lax.dynamic_slice_in_dim(amplitudes, me_aux * rows, rows, 2)
        diagonal = (factor * amp_rows_own.astype(F32)).reshape(local, freqs, share_width)
    else:
        shift = pno_energy[:, :, None] + pno_energy[:, None, :] - occ_pair[:, None, None]
        factor = shift[:, None] - signs[None, :, None, None] * frequency[0]
        diagonal = (factor * amplitudes.astype(F32)).reshape(local, freqs, rank * rank)
        diagonal = lax.dynamic_slice_in_dim(diagonal, start, share_width, 2)
    return drive + diagonal + coupled_share


def solution(mesh):
    placed = (
        P("pair", None, "aux"),
        P("pair", None, None, None),
        P("pair", None, "aux"),
        P("pair", None),
        P(),
        P(),
        P(),
        P("pair", None),
        P("pair"),
        P(),
    )
    sizes = (mesh.shape["pair"], mesh.shape["aux"])

    def layer(*args):
        return body(sizes, *args)

    return jax.shard_map(
        layer,
        mesh=mesh,
        in_specs=placed,
        out_specs=P("pair", None, "aux"),
        check_vma=False,
    )
```

profile of v0, /device:TPU:0, one launch (start us, length us, event | category | flops | bytes accessed | tf_op | source)
XLA Modules:
  0.0 82.2 jit_solution(16041178505615791137)
XLA Ops:
  0.0 2.9 %shard_map.109 = (bf16[2,288,128]{2,1,0:T(8,128)(2,1)}, bf16[2,288,128]{2,1,0:T(8,128)(2,1)}, bf16[2,288,128]{2,1,0:T(8,128)(2,1)}, bf16[2,288,128]{2,1,0:T(8,12...) custom-call(bf16[2,120,2304]{2,1,0:T(8,128)(2,1)} %refs_0_.1, ...), custom_call_target="tpu_custom_call" | custom-call | bytes 4194304 | tf_op jit(solution)/shard_map/pallas_call | solution.py:168
  2.9 4.1 %collective-permute-start = (bf16[272,128]{1,0:T(8,128)(2,1)}, bf16[272,128]{1,0:T(8,128)(2,1)S(1)}, u32[]{:S(2)}, u32[]{:S(2)}) collective-permute-start(bf16[272,128]{1,0:T(8,128)(2,1)} %get-tuple-element.14), channel_id=1, source_target_pairs={{0,16},{4,20},{8,24},{12,28},{16,0},{20,4},{24,8},{28,12},{1,17},{... | collective-permute-start | bytes 208904 | tf_op jit(solution)/shard_map/ppermute | solution.py:181
  7.1 2.3 %collective-permute-start.10 = (bf16[2,288,128]{2,1,0:T(8,128)(2,1)}, bf16[2,288,128]{2,1,0:T(8,128)(2,1)S(1)}, u32[]{:S(2)}, u32[]{:S(2)}) collective-permute-start(bf16[2,288,128]{2,1,0:T(8,128)(2,1)} %get-tuple-element.22), channel_id=1, source_target_pairs={{0,28},{4,24},{8,20},{12,16},{16,12},{20,8},{24,4},{28,0},{1,29},{... | collective-permute-start | bytes 442376 | tf_op jit(solution)/shard_map/ppermute | solution.py:187
  9.3 0.5 collective-permute-start.4
  9.9 0.3 collective-permute-start.5
  10.1 2.7 %collective-permute-start.6 = (bf16[2,288,128]{2,1,0:T(8,128)(2,1)}, bf16[2,288,128]{2,1,0:T(8,128)(2,1)S(1)}, u32[]{:S(2)}, u32[]{:S(2)}) collective-permute-start(bf16[2,288,128]{2,1,0:T(8,128)(2,1)} %get-tuple-element.18), channel_id=1, source_target_pairs={{0,12},{4,8},{8,4},{12,0},{16,28},{20,24},{24,20},{28,16},{1,13},{... | collective-permute-start | bytes 442376 | tf_op jit(solution)/shard_map/ppermute | solution.py:187
  12.8 0.0 collective-permute-done
  12.8 0.9 %pad_maximum_fusion.refs_8_ = bf16[2,272,128]{2,1,0:T(8,128)(2,1)S(1)} fusion(bf16[1,272,128]{2,1,0:T(8,128)(2,1)S(1)} %bitcast.27, bf16[1,272,128]{2,1,0:T(8,128)(2,1)} %bitcast.25), kind=kLoop, calls=%fused_computation.6 | loop fusion | flops 69632 | bytes 278528 | tf_op jit(solution)/shard_map/concatenate | solution.py:182
  13.7 3.3 %collective-permute-start.3 = (bf16[2,272,128]{2,1,0:T(8,128)(2,1)S(1)}, bf16[2,272,128]{2,1,0:T(8,128)(2,1)S(1)}, u32[]{:S(2)}, u32[]{:S(2)}) collective-permute-start(bf16[2,272,128]{2,1,0:T(8,128)(2,1)S(1)} %pad_maximum_fusion.refs_8_), channel_id=1, source_target_pairs={{0,12},{4,8},{8,4},{12,0},{16,28},{20,24},{24,20},{28,16},{1,13},{... | collective-permute-start | bytes 417800 | tf_op jit(solution)/shard_map/ppermute | solution.py:186
  17.0 0.1 pad_add_fusion.where
  17.1 0.7 fusion.2
  17.8 7.0 %collective-permute-done.3.refs_11_ = bf16[2,272,128]{2,1,0:T(8,128)(2,1)S(1)} collective-permute-done((bf16[2,272,128]{2,1,0:T(8,128)(2,1)S(1)}, bf16[2,272,128]{2,1,0:T(8,128)(2,1)S(1)}, u32[]{:S(2)}, u32[]{:S(2)}) %collective-permute-start.3) | collective-permute-done | bytes 139296 | tf_op jit(solution)/shard_map/ppermute | solution.py:186
  24.8 0.4 collective-permute-start.2
  25.2 5.1 %collective-permute-done.2.refs_10_ = bf16[2,272,128]{2,1,0:T(8,128)(2,1)S(1)} collective-permute-done((bf16[2,272,128]{2,1,0:T(8,128)(2,1)S(1)}, bf16[2,272,128]{2,1,0:T(8,128)(2,1)S(1)}, u32[]{:S(2)}, u32[]{:S(2)}) %collective-permute-start.2) | collective-permute-done | bytes 139296 | tf_op jit(solution)/shard_map/ppermute | solution.py:186
  30.3 0.4 collective-permute-start.1
  30.7 0.0 collective-permute-done.10.refs_7_
  30.7 2.1 %collective-permute-start.7 = (bf16[2,288,128]{2,1,0:T(8,128)(2,1)}, bf16[2,288,128]{2,1,0:T(8,128)(2,1)S(1)}, u32[]{:S(2)}, u32[]{:S(2)}) collective-permute-start(bf16[2,288,128]{2,1,0:T(8,128)(2,1)} %get-tuple-element.19), channel_id=1, source_target_pairs={{0,16},{4,20},{8,24},{12,28},{16,0},{20,4},{24,8},{28,12},{1,17},{... | collective-permute-start | bytes 442376 | tf_op jit(solution)/shard_map/ppermute | solution.py:187
  32.8 2.5 %collective-permute-done.1.refs_9_ = bf16[2,272,128]{2,1,0:T(8,128)(2,1)S(1)} collective-permute-done((bf16[2,272,128]{2,1,0:T(8,128)(2,1)S(1)}, bf16[2,272,128]{2,1,0:T(8,128)(2,1)S(1)}, u32[]{:S(2)}, u32[]{:S(2)}) %collective-permute-start.1) | collective-permute-done | bytes 139296 | tf_op jit(solution)/shard_map/ppermute | solution.py:186
  35.4 1.9 %collective-permute-start.8 = (bf16[2,288,128]{2,1,0:T(8,128)(2,1)}, bf16[2,288,128]{2,1,0:T(8,128)(2,1)S(1)}, u32[]{:S(2)}, u32[]{:S(2)}) collective-permute-start(bf16[2,288,128]{2,1,0:T(8,128)(2,1)} %get-tuple-element.20), channel_id=1, source_target_pairs={{0,20},{4,16},{8,28},{12,24},{16,4},{20,0},{24,12},{28,8},{1,21},{... | collective-permute-start | bytes 442376 | tf_op jit(solution)/shard_map/ppermute | solution.py:187
  37.3 0.0 collective-permute-done.4.refs_1_
  37.4 1.3 %collective-permute-start.9 = (bf16[2,288,128]{2,1,0:T(8,128)(2,1)}, bf16[2,288,128]{2,1,0:T(8,128)(2,1)S(1)}, u32[]{:S(2)}, u32[]{:S(2)}) collective-permute-start(bf16[2,288,128]{2,1,0:T(8,128)(2,1)} %get-tuple-element.21), channel_id=1, source_target_pairs={{0,24},{4,28},{8,16},{12,20},{16,8},{20,12},{24,0},{28,4},{1,25},{... | collective-permute-start | bytes 442376 | tf_op jit(solution)/shard_map/ppermute | solution.py:187
  38.6 0.0 collective-permute-done.5.refs_2_
  38.6 0.0 collective-permute-start.11
  38.6 0.0 collective-permute-done.6.refs_3_
  38.6 0.5 collective-permute-start.12
  39.1 7.5 %collective-permute-done.7.refs_4_ = bf16[2,288,128]{2,1,0:T(8,128)(2,1)S(1)} collective-permute-done((bf16[2,288,128]{2,1,0:T(8,128)(2,1)}, bf16[2,288,128]{2,1,0:T(8,128)(2,1)S(1)}, u32[]{:S(2)}, u32[]{:S(2)}) %collective-permute-start.7) | collective-permute-done | bytes 147488 | tf_op jit(solution)/shard_map/ppermute | solution.py:187
  46.7 4.1 %collective-permute-done.8.refs_5_ = bf16[2,288,128]{2,1,0:T(8,128)(2,1)S(1)} collective-permute-done((bf16[2,288,128]{2,1,0:T(8,128)(2,1)}, bf16[2,288,128]{2,1,0:T(8,128)(2,1)S(1)}, u32[]{:S(2)}, u32[]{:S(2)}) %collective-permute-start.8) | collective-permute-done | bytes 147488 | tf_op jit(solution)/shard_map/ppermute | solution.py:187
  50.8 0.0 collective-permute-start.14
  50.8 0.1 reshape.31.ids_ref
  50.9 0.1 reshape.32.w_ref
  51.0 1.1 %collective-permute-done.14.refs_15_ = bf16[2,272,128]{2,1,0:T(8,128)(2,1)S(1)} collective-permute-done((bf16[2,272,128]{2,1,0:T(8,128)(2,1)S(1)}, bf16[2,272,128]{2,1,0:T(8,128)(2,1)S(1)}, u32[]{:S(2)}, u32[]{:S(2)}) %collective-permute-start.14) | collective-permute-done | bytes 139296 | tf_op jit(solution)/shard_map/ppermute | solution.py:194
  52.1 0.9 %copy-done = bf16[2,288,128]{2,1,0:T(8,128)(2,1)S(1)} copy-done((bf16[2,288,128]{2,1,0:T(8,128)(2,1)S(1)}, bf16[2,288,128]{2,1,0:T(8,128)(2,1)}, u32[]{:S(2)}) %copy-start) | copy-done | bytes 147480
  53.0 4.3 %shard_map.110 = bf16[2,8,2,2,2,32,128]{6,5,4,3,2,1,0:T(8,128)(2,1)S(1)} custom-call(s32[2]{0:T(128)S(1)} %pad_add_fusion.where, s32[8,2,8]{2,1,0:T(2,128)S(1)} %reshape.31.ids_ref, f32[8,2,8]{2,1,0:T(2,128)S(1)} %reshape.32.w_ref, bf16[2,288,128]{2,1,0:T(8,128)(2,1)S(1)} %copy-done, bf16[2,288,128]{2,1,0:T(8,128)(2,1)S(1)} %collective-permute-done.4.refs_1_, ...), custom_call_target="tpu_custom_call" | custom-call | flops 603979776 | bytes 4194304 | tf_op jit(solution)/shard_map/pallas_call | solution.py:198
  57.4 0.2 collective-permute-start.15
  57.6 1.8 %collective-permute-done.15 = bf16[8,2,2,2,32,128]{5,4,3,2,1,0:T(8,128)(2,1)S(1)} collective-permute-done((bf16[8,2,2,2,32,128]{5,4,3,2,1,0:T(8,128)(2,1)S(1)}, bf16[8,2,2,2,32,128]{5,4,3,2,1,0:T(8,128)(2,1)S(1)}, u32[]{:S(2)}, u32[]{:S(2)}) %collective-permute-start.15) | collective-permute-done | bytes 524320 | tf_op jit(solution)/shard_map/ppermute | solution.py:212
  59.4 1.0 %fusion = bf16[8,2,2,2,32,128]{5,4,3,2,1,0:T(8,128)(2,1)} fusion(bf16[8,2,2,2,32,128]{5,4,3,2,1,0:T(8,128)(2,1)S(1)} %collective-permute-done.15, bf16[2,8,2,2,2,32,128]{6,5,4,3,2,1,0:T(8,128)(2,1)S(1)} %shard_map.110), kind=kLoop, calls=%fused_computation.1 | loop fusion | flops 1048576 | bytes 1572864 | tf_op jit(solution)/shard_map/convert_element_type | solution.py:213
  60.4 5.6 %all-to-all-start = ((bf16[16,2,2,32,128]{4,3,2,1,0:T(8,128)(2,1)}), bf16[16,2,2,32,128]{4,3,2,1,0:T(8,128)(2,1)S(1)}, u32[]{:S(2)}, u32[]{:S(2)}) async-start(bf16[16,2,2,32,128]{4,3,2,1,0:T(8,128)(2,1)} %bitcast.13), calls=%async_computation | async-start | bytes 1048576 | tf_op jit(solution)/shard_map/all_to_all | solution.py:219
  66.0 0.1 constant_dynamic-slice_fusion
  66.0 0.1 copy.15
  66.8 0.1 constant_dynamic-slice_fusion.1
  66.9 0.2 fusion.5
  67.0 0.1 add_subtract_fusion
  67.1 0.9 %convert_multiply_fusion = f32[2,2,30,120]{3,2,1,0:T(8,128)S(1)} fusion(bf16[2,2,120,120]{3,2,1,0:T(8,128)(2,1)} %refs_1_.1, s32[]{:T(128)S(6)} %select_n.14, f32[2]{0:T(128)S(1)} %broadcast_multiply_fusion, f32[2,30,120]{2,1,0:T(8,128)S(1)} %add_subtract_fusion), kind=kLoop, calls=%fused_computation.8 | loop fusion | flops 43200 | bytes 115212 | tf_op jit(solution)/shard_map/mul | solution.py:243
  68.0 0.1 reshape.27
  68.1 13.2 %all-to-all-done = bf16[16,2,2,32,128]{4,3,2,1,0:T(8,128)(2,1)S(1)} async-done(((bf16[16,2,2,32,128]{4,3,2,1,0:T(8,128)(2,1)}), bf16[16,2,2,32,128]{4,3,2,1,0:T(8,128)(2,1)S(1)}, u32[]{:S(2)}, u32[]{:S(2)}) %all-to-all-start) | async-done | bytes 524320 | tf_op jit(solution)/shard_map/all_to_all | solution.py:219
  81.3 0.1 convert_reduce_fusion
  81.4 0.1 reshape.30
  81.5 0.7 add_add_fusion
  (25 shorter events, 0.1 us)
Async XLA Ops:
  2.9 9.9 %collective-permute-start = (bf16[272,128]{1,0:T(8,128)(2,1)}, bf16[272,128]{1,0:T(8,128)(2,1)S(1)}, u32[]{:S(2)}, u32[]{:S(2)}) collective-permute-start(bf16[272,128]{1,0:T(8,128)(2,1)} %get-tuple-element.14), channel_id=1, source_target_pairs={{0,16},{4,20},{8,24},{12,28},{16,0},{20,4},{24,8},{28,12},{1,17},{... | collective-permute-start | bytes 208904 | tf_op jit(solution)/shard_map/ppermute | solution.py:181
  7.1 23.7 %collective-permute-start.10 = (bf16[2,288,128]{2,1,0:T(8,128)(2,1)}, bf16[2,288,128]{2,1,0:T(8,128)(2,1)S(1)}, u32[]{:S(2)}, u32[]{:S(2)}) collective-permute-start(bf16[2,288,128]{2,1,0:T(8,128)(2,1)} %get-tuple-element.22), channel_id=1, source_target_pairs={{0,28},{4,24},{8,20},{12,16},{16,12},{20,8},{24,4},{28,0},{1,29},{... | collective-permute-start | bytes 442376 | tf_op jit(solution)/shard_map/ppermute | solution.py:187
  9.3 28.0 %collective-permute-start.4 = (bf16[2,288,128]{2,1,0:T(8,128)(2,1)}, bf16[2,288,128]{2,1,0:T(8,128)(2,1)S(1)}, u32[]{:S(2)}, u32[]{:S(2)}) collective-permute-start(bf16[2,288,128]{2,1,0:T(8,128)(2,1)} %get-tuple-element.16), channel_id=1, source_target_pairs={{0,4},{4,0},{8,12},{12,8},{16,20},{20,16},{24,28},{28,24},{1,5},{5... | collective-permute-start | bytes 442376 | tf_op jit(solution)/shard_map/ppermute | solution.py:187
  9.9 28.8 %collective-permute-start.5 = (bf16[2,288,128]{2,1,0:T(8,128)(2,1)}, bf16[2,288,128]{2,1,0:T(8,128)(2,1)S(1)}, u32[]{:S(2)}, u32[]{:S(2)}) collective-permute-start(bf16[2,288,128]{2,1,0:T(8,128)(2,1)} %get-tuple-element.17), channel_id=1, source_target_pairs={{0,8},{4,12},{8,0},{12,4},{16,24},{20,28},{24,16},{28,20},{1,9},{5... | collective-permute-start | bytes 442376 | tf_op jit(solution)/shard_map/ppermute | solution.py:187
  10.1 28.5 %collective-permute-start.6 = (bf16[2,288,128]{2,1,0:T(8,128)(2,1)}, bf16[2,288,128]{2,1,0:T(8,128)(2,1)S(1)}, u32[]{:S(2)}, u32[]{:S(2)}) collective-permute-start(bf16[2,288,128]{2,1,0:T(8,128)(2,1)} %get-tuple-element.18), channel_id=1, source_target_pairs={{0,12},{4,8},{8,4},{12,0},{16,28},{20,24},{24,20},{28,16},{1,13},{... | collective-permute-start | bytes 442376 | tf_op jit(solution)/shard_map/ppermute | solution.py:187
  13.7 11.1 %collective-permute-start.3 = (bf16[2,272,128]{2,1,0:T(8,128)(2,1)S(1)}, bf16[2,272,128]{2,1,0:T(8,128)(2,1)S(1)}, u32[]{:S(2)}, u32[]{:S(2)}) collective-permute-start(bf16[2,272,128]{2,1,0:T(8,128)(2,1)S(1)} %pad_maximum_fusion.refs_8_), channel_id=1, source_target_pairs={{0,12},{4,8},{8,4},{12,0},{16,28},{20,24},{24,20},{28,16},{1,13},{... | collective-permute-start | bytes 417800 | tf_op jit(solution)/shard_map/ppermute | solution.py:186
  24.8 5.5 %collective-permute-start.2 = (bf16[2,272,128]{2,1,0:T(8,128)(2,1)S(1)}, bf16[2,272,128]{2,1,0:T(8,128)(2,1)S(1)}, u32[]{:S(2)}, u32[]{:S(2)}) collective-permute-start(bf16[2,272,128]{2,1,0:T(8,128)(2,1)S(1)} %pad_maximum_fusion.refs_8_), channel_id=1, source_target_pairs={{0,8},{4,12},{8,0},{12,4},{16,24},{20,28},{24,16},{28,20},{1,9},{5... | collective-permute-start | bytes 417800 | tf_op jit(solution)/shard_map/ppermute | solution.py:186
  30.3 5.1 %collective-permute-start.1 = (bf16[2,272,128]{2,1,0:T(8,128)(2,1)S(1)}, bf16[2,272,128]{2,1,0:T(8,128)(2,1)S(1)}, u32[]{:S(2)}, u32[]{:S(2)}) collective-permute-start(bf16[2,272,128]{2,1,0:T(8,128)(2,1)S(1)} %pad_maximum_fusion.refs_8_), channel_id=1, source_target_pairs={{0,4},{4,0},{8,12},{12,8},{16,20},{20,16},{24,28},{28,24},{1,5},{5... | collective-permute-start | bytes 417800 | tf_op jit(solution)/shard_map/ppermute | solution.py:186
  30.7 16.0 %collective-permute-start.7 = (bf16[2,288,128]{2,1,0:T(8,128)(2,1)}, bf16[2,288,128]{2,1,0:T(8,128)(2,1)S(1)}, u32[]{:S(2)}, u32[]{:S(2)}) collective-permute-start(bf16[2,288,128]{2,1,0:T(8,128)(2,1)} %get-tuple-element.19), channel_id=1, source_target_pairs={{0,16},{4,20},{8,24},{12,28},{16,0},{20,4},{24,8},{28,12},{1,17},{... | collective-permute-start | bytes 442376 | tf_op jit(solution)/shard_map/ppermute | solution.py:187
  35.4 15.4 %collective-permute-start.8 = (bf16[2,288,128]{2,1,0:T(8,128)(2,1)}, bf16[2,288,128]{2,1,0:T(8,128)(2,1)S(1)}, u32[]{:S(2)}, u32[]{:S(2)}) collective-permute-start(bf16[2,288,128]{2,1,0:T(8,128)(2,1)} %get-tuple-element.20), channel_id=1, source_target_pairs={{0,20},{4,16},{8,28},{12,24},{16,4},{20,0},{24,12},{28,8},{1,21},{... | collective-permute-start | bytes 442376 | tf_op jit(solution)/shard_map/ppermute | solution.py:187
  37.4 13.6 %collective-permute-start.9 = (bf16[2,288,128]{2,1,0:T(8,128)(2,1)}, bf16[2,288,128]{2,1,0:T(8,128)(2,1)S(1)}, u32[]{:S(2)}, u32[]{:S(2)}) collective-permute-start(bf16[2,288,128]{2,1,0:T(8,128)(2,1)} %get-tuple-element.21), channel_id=1, source_target_pairs={{0,24},{4,28},{8,16},{12,20},{16,8},{20,12},{24,0},{28,4},{1,25},{... | collective-permute-start | bytes 442376 | tf_op jit(solution)/shard_map/ppermute | solution.py:187
  38.6 12.4 %collective-permute-start.11 = (bf16[2,272,128]{2,1,0:T(8,128)(2,1)S(1)}, bf16[2,272,128]{2,1,0:T(8,128)(2,1)S(1)}, u32[]{:S(2)}, u32[]{:S(2)}) collective-permute-start(bf16[2,272,128]{2,1,0:T(8,128)(2,1)S(1)} %pad_maximum_fusion.refs_8_), channel_id=1, source_target_pairs={{0,1},{1,0},{2,3},{3,2},{4,5},{5,4},{6,7},{7,6},{8,9},{9,8},{10,11... | collective-permute-start | bytes 417800 | tf_op jit(solution)/shard_map/ppermute | solution.py:194
  38.6 12.3 %collective-permute-start.12 = (bf16[2,272,128]{2,1,0:T(8,128)(2,1)S(1)}, bf16[2,272,128]{2,1,0:T(8,128)(2,1)S(1)}, u32[]{:S(2)}, u32[]{:S(2)}) collective-permute-start(bf16[2,272,128]{2,1,0:T(8,128)(2,1)S(1)} %collective-permute-done.1.refs_9_), channel_id=1, source_target_pairs={{0,1},{1,0},{2,3},{3,2},{4,5},{5,4},{6,7},{7,6},{8,9},{9,8},{10,11... | collective-permute-start | bytes 417800 | tf_op jit(solution)/shard_map/ppermute | solution.py:194
  46.7 4.3 %collective-permute-start.13 = (bf16[2,272,128]{2,1,0:T(8,128)(2,1)S(1)}, bf16[2,272,128]{2,1,0:T(8,128)(2,1)S(1)}, u32[]{:S(2)}, u32[]{:S(2)}) collective-permute-start(bf16[2,272,128]{2,1,0:T(8,128)(2,1)S(1)} %collective-permute-done.2.refs_10_), channel_id=1, source_target_pairs={{0,1},{1,0},{2,3},{3,2},{4,5},{5,4},{6,7},{7,6},{8,9},{9,8},{10,11... | collective-permute-start | bytes 417800 | tf_op jit(solution)/shard_map/ppermute | solution.py:194
  50.8 1.4 %collective-permute-start.14 = (bf16[2,272,128]{2,1,0:T(8,128)(2,1)S(1)}, bf16[2,272,128]{2,1,0:T(8,128)(2,1)S(1)}, u32[]{:S(2)}, u32[]{:S(2)}) collective-permute-start(bf16[2,272,128]{2,1,0:T(8,128)(2,1)S(1)} %collective-permute-done.3.refs_11_), channel_id=1, source_target_pairs={{0,1},{1,0},{2,3},{3,2},{4,5},{5,4},{6,7},{7,6},{8,9},{9,8},{10,11... | collective-permute-start | bytes 417800 | tf_op jit(solution)/shard_map/ppermute | solution.py:194
  52.1 0.9 %copy-start = (bf16[2,288,128]{2,1,0:T(8,128)(2,1)S(1)}, bf16[2,288,128]{2,1,0:T(8,128)(2,1)}, u32[]{:S(2)}) copy-start(bf16[2,288,128]{2,1,0:T(8,128)(2,1)} %get-tuple-element.15.refs_0_) | copy-start | bytes 442372
  57.4 2.0 %collective-permute-start.15 = (bf16[8,2,2,2,32,128]{5,4,3,2,1,0:T(8,128)(2,1)S(1)}, bf16[8,2,2,2,32,128]{5,4,3,2,1,0:T(8,128)(2,1)S(1)}, u32[]{:S(2)}, u32[]{:S(2)}) collective-permute-start(bf16[8,2,2,2,32,128]{5,4,3,2,1,0:T(8,128)(2,1)S(1)} %slice_bitcast_fusion), channel_id=1, source_target_pairs={{0,1},{1,0},{2,3},{3,2},{4,5},{5,4},{6,7},{7,6},{8,9},{9,8},{10,11... | collective-permute-start | bytes 1572872 | tf_op jit(solution)/shard_map/ppermute | solution.py:212
  57.6 8.3 %copy-start.2 = (s32[16,2]{0,1:T(2,128)S(1)}, s32[16,2]{0,1:T(2,128)}, u32[]{:S(2)}) copy-start(s32[16,2]{0,1:T(2,128)} %param.17) | copy-start | bytes 388
  57.6 9.2 %copy-start.3 = (f32[2,120]{1,0:T(2,128)S(1)}, f32[2,120]{1,0:T(2,128)}, u32[]{:S(2)}) copy-start(f32[2,120]{1,0:T(2,128)} %param.14) | copy-start | bytes 2884
  57.6 9.3 %copy-start.4 = (f32[32]{0:T(128)S(1)}, f32[32]{0:T(128)}, u32[]{:S(2)}) copy-start(f32[32]{0:T(128)} %param.15) | copy-start | bytes 388
  57.6 9.4 %copy-start.5 = (f32[2]{0:T(128)S(1)}, f32[2]{0:T(128)}, u32[]{:S(2)}) copy-start(f32[2]{0:T(128)} %constant.34.clone) | copy-start | bytes 28
  60.4 21.2 %copy-start.1 = (f32[2,2,3600]{2,1,0:T(2,128)S(1)}, f32[2,2,3600]{2,1,0:T(2,128)}, u32[]{:S(2)}) copy-start(f32[2,2,3600]{2,1,0:T(2,128)} %param.13) | copy-start | bytes 172804
  60.4 20.9 %all-to-all-start = ((bf16[16,2,2,32,128]{4,3,2,1,0:T(8,128)(2,1)}), bf16[16,2,2,32,128]{4,3,2,1,0:T(8,128)(2,1)S(1)}, u32[]{:S(2)}, u32[]{:S(2)}) async-start(bf16[16,2,2,32,128]{4,3,2,1,0:T(8,128)(2,1)} %bitcast.13), calls=%async_computation | async-start | bytes 1048576 | tf_op jit(solution)/shard_map/all_to_all | solution.py:219
where the time goes:
time: 82.7 us; the launch traced here: 82.2 us
  waiting for transfers between devices  42.4 us (51%)
  starting transfers between devices  25.6 us (31%)
  Pallas kernels  7.22 us (9%)
  other arithmetic  4.57 us (6%)
  local copies, waits for them, and re-layouts  1.64 us (2%)
    ppermute x3, waiting for transfers between devices, body(): pieces[k] = lax.ppermute(pieces[0], 'pair', flip(n_pair, k))  14.6 us
    all_to_all x1, waiting for transfers between devices, body(): lax.all_to_all(mine, ('pair', 'aux'), 0, 0, axis_index_groups=groups, til...  13.2 us
    ppermute x7, waiting for transfers between devices, body(): received[k] = lax.ppermute(chunks[k], 'pair', flip(n_pair, k))  11.6 us
    ppermute x7, starting transfers between devices, body(): received[k] = lax.ppermute(chunks[k], 'pair', flip(n_pair, k))  11.1 us
    all_to_all x1, starting transfers between devices, body(): lax.all_to_all(mine, ('pair', 'aux'), 0, 0, axis_index_groups=groups, til...  5.55 us
    pallas_call x1, Pallas kernels, body(): pl.pallas_call(functools.partial(couple_kernel, n_pair, blocks, sides), o...  4.3 us
    ppermute x1, starting transfers between devices, body(): other = lax.ppermute(share, 'pair', flip(n_pair, far))  4.13 us
    ppermute x3, starting transfers between devices, body(): pieces[k] = lax.ppermute(pieces[0], 'pair', flip(n_pair, k))  4.11 us
  transfers between devices with their start and end apart: 17, of which 8 were waited for; matrix products, arithmetic and copies ran while one was open for 4% of the time, Pallas kernels for 0%

commit v1 on v0

--- a/solution.py
+++ b/solution.py
@@ -21,7 +21,11 @@
     return [(i, i ^ bits) for i in range(count)]
 
 
-def prep_kernel(n_pair, blocks, rows, sides, *refs):
+def member(aux, sides):
+    return (aux // 2 % 2 if sides[1] == 2 else 0, aux % 2 if sides[0] == 2 else 0)
+
+
+def prep_kernel(n_pair, sides, *refs):
     inputs, chunks, share_ref = refs[:6], refs[6 : 6 + n_pair], refs[6 + n_pair]
     buffers, (turned, sems) = refs[7 + n_pair : 13 + n_pair], refs[13 + n_pair :]
     copies = [
@@ -32,46 +36,16 @@
         copy.start()
     panels, amps, lmo, near, ranks, fock = buffers
     local, rank, width = panels.shape
-    depth = turned.shape[2]
-    rows_pad = depth // blocks
     part = width // n_pair
+    wide = part // LANES
+    rest = part - wide * LANES
     me = lax.axis_index("pair")
-    freq = lax.axis_index("aux") % 2 if sides == 2 else 0
+    aux = lax.axis_index("aux")
     slots = near.shape[1]
-    for copy in copies:
+    for copy in copies[2:]:
         copy.wait()
 
-    def spread_rows(x, lanes):
-        pieces = []
-        for h in range(blocks):
-            pieces.append(x[h * rows : (h + 1) * rows])
-            if rows_pad > rows:
-                pieces.append(jnp.zeros((rows_pad - rows, lanes), x.dtype))
-        return jnp.concatenate(pieces, axis=0) if len(pieces) > 1 else pieces[0]
-
-    tile = 256 if width % 256 == 0 else LANES
-    for lp in range(local):
-        keep = lax.broadcasted_iota(jnp.int32, (rank, tile), 0) < ranks[lp]
-        for t in range(width // tile):
-            x = panels[lp, :, t * tile : (t + 1) * tile].astype(F32)
-            x = spread_rows(jnp.where(keep, x, 0.0), tile)
-            turned[lp, t * tile : (t + 1) * tile, :] = x.T.astype(BF)
-    for k in range(n_pair):
-        start = pl.multiple_of((me ^ k) * part, 16)
-        for lp in range(local):
-            chunks[k][lp] = turned[lp, pl.ds(start, part), :]
-
     share_rows = share_ref.shape[0]
-    freqs = amps.shape[1] * depth * local // (share_rows - 16)
-    take = amps.shape[1] // freqs
-    for lp in range(local):
-        for s in range(take):
-            a = amps[lp, freq * take + s].astype(F32)
-            a = spread_rows(a, rank)
-            a = jnp.concatenate([a, jnp.zeros((depth, LANES - rank), F32)], axis=1)
-            first = (lp * take + s) * depth
-            share_ref[first : first + depth, :] = a.astype(BF)
-
     row = lax.broadcasted_iota(jnp.int32, (16, LANES), 0)
     lane = lax.broadcasted_iota(jnp.int32, (16, LANES), 1)
     tail = jnp.zeros((16, LANES), F32)
@@ -92,30 +66,82 @@
             tail = jnp.where(here & (row == 1), total * fresh, tail)
     share_ref[share_rows - 16 :, :] = tail.astype(BF)
 
-
-def couple_kernel(n_pair, blocks, sides, where, ids_ref, w_ref, *refs):
+    freqs = amps.shape[1]
+    many, take = local // sides[1], freqs // sides[0]
+    lp_first, s_first = member(aux, sides)
+    copies[1].wait()
+    for i in range(many):
+        for j in range(take):
+            a = amps[lp_first * many + i, s_first * take + j].astype(F32)
+            a = jnp.concatenate([a, jnp.zeros((rank, LANES - rank), F32)], axis=1)
+            first = (i * take + j) * rank
+            share_ref[first : first + rank, :] = a.astype(BF)
+
+    copies[0].wait()
+    for lp in range(local):
+        keep = lax.broadcasted_iota(jnp.int32, (rank, LANES), 0) < ranks[lp]
+        for k in range(n_pair):
+            for w in range(wide):
+                start = pl.multiple_of(((me ^ k) * wide + w) * LANES, LANES)
+                x = panels[lp, :, pl.ds(start, LANES)].astype(F32)
+                chunks[k][lp, w * rank : (w + 1) * rank, :] = jnp.where(keep, x, 0.0).astype(BF)
+        if rest:
+            for t in range(n_pair * rest // LANES):
+                start = n_pair * wide * LANES + t * LANES
+                x = panels[lp, :, start : start + LANES].astype(F32)
+                x = jnp.where(keep, x, 0.0)
+                x = jnp.concatenate([x, jnp.zeros((LANES - rank, LANES), F32)], axis=0)
+                turned[t * LANES : (t + 1) * LANES, :] = x.T.astype(BF)
+            for k in range(n_pair):
+                start = pl.multiple_of((me ^ k) * rest, 16)
+                chunks[k][lp, wide * rank :, :] = turned[pl.ds(start, rest), :]
+
+
+def couple_kernel(n_pair, blocks, sides, shape, where, ids_ref, w_ref, *refs):
     half = n_pair // 2
-    panels, mats = refs[:n_pair], refs[n_pair : n_pair + half * sides]
-    out_ref, proj, mixed = refs[n_pair + half * sides :]
-    local, part, depth = panels[0].shape
-    freqs = proj.shape[2] // LANES
-    rows = depth // blocks
+    members = sides[0] * sides[1]
+    panels, mats = list(refs[:n_pair]), refs[n_pair : n_pair + half * members]
+    out_ref, proj, mixed, mat, own, sem = refs[n_pair + half * members :]
+    local, rank, part, freqs = shape
+    wide = part // LANES
+    rest = part - wide * LANES
+    rows = rank // blocks
     slots = ids_ref.shape[2]
-    me, my_core = where[0], where[1]
-    take = freqs // sides
-
-    for k in range(n_pair):
-        for lp in range(local):
-            for s in range(freqs):
-                slot, inner = s // take, s % take
-                first = (lp * take + inner) * depth
-                mat = mats[slot * half + k % half][k // half, first : first + depth, :]
-                proj[k * local + lp, :, s * LANES : (s + 1) * LANES] = jnp.dot(
-                    panels[k][lp], mat, preferred_element_type=F32
-                )
+    me, aux = where[0], where[1]
+    many, take = local // sides[1], freqs // sides[0]
+    copy = pltpu.make_async_copy(panels[0], own, sem)
+    copy.start()
+    panels[0] = own
+    order = list(range(1, n_pair)) + [0]
+
+    for k in order:
+        if k == 0:
+            copy.wait()
+        for pair_slot in range(sides[1]):
+            for i in range(many):
+                lp = member(aux ^ (pair_slot * 2), sides)[0] * many + i
+                for s in range(freqs):
+                    slot, inner = s // take, s % take
+                    first = (i * take + inner) * rank
+                    piece = mats[(pair_slot * sides[0] + slot) * half + k % half]
+                    mat[:, s * LANES : (s + 1) * LANES] = piece[k // half, first : first + rank, :]
+                index = k * local + lp
+                for w in range(wide):
+                    proj[index, w * LANES : (w + 1) * LANES, :] = lax.dot_general(
+                        panels[k][lp, w * rank : (w + 1) * rank, :],
+                        mat[...],
+                        (((0,), (0,)), ((), ())),
+                        preferred_element_type=F32,
+                    )
+                if rest:
+                    proj[index, wide * LANES :, :] = jnp.dot(
+                        panels[k][lp, wide * rank :, :][:, :rank],
+                        mat[...],
+                        preferred_element_type=F32,
+                    )
 
     tile = 32 if part % 32 == 0 else 16
-    for k in range(n_pair):
+    for k in order:
         for lp in range(local):
             source = []
             for j in range(slots):
@@ -128,14 +154,25 @@
                 for j in range(1, slots):
                     acc = acc + scale[j] * proj[source[j], span, :]
                 mixed[span, :] = acc.astype(BF)
-            got = lax.dot_general(
-                panels[k][lp], mixed[...], (((0,), (0,)), ((), ())), preferred_element_type=F32
-            )
+            got = None
+            if wide:
+                x = jnp.concatenate(
+                    [panels[k][lp, w * rank : (w + 1) * rank, :] for w in range(wide)], axis=1
+                )
+                got = jnp.dot(x, mixed[: wide * LANES, :], preferred_element_type=F32)
+            if rest:
+                more = lax.dot_general(
+                    panels[k][lp, wide * rank :, :],
+                    mixed[wide * LANES :, :],
+                    (((0,), (0,)), ((), ())),
+                    preferred_element_type=F32,
+                )[:rank]
+                got = more if got is None else got + more
             for h in range(blocks):
-                side = my_core ^ (h % 2) if blocks > 1 else 0
+                side = aux % 2 ^ (h % 2) if blocks > 1 else 0
                 for s in range(freqs):
-                    freq = (s // take ^ my_core) * take + s % take if sides == 2 else s
-                    out_ref[side, me ^ k, h // 2, lp, freq] = got[
+                    freq = member(aux ^ (s // take), sides)[1] * take + s % take
+                    out_ref[side, me ^ k, h // 2, lp, freq, :rows, :] = got[
                         h * rows : (h + 1) * rows, s * LANES : (s + 1) * LANES
                     ].astype(out_ref.dtype)
 
@@ -151,28 +188,34 @@
     blocks = n_aux if even else 1
     rows = rank // blocks
     rows_pad = round_up(rows, 16)
-    depth = round_up(blocks * rows_pad, LANES)
-    rows_pad = depth // blocks
     part = width // n_pair
     me_pair = lax.axis_index("pair")
     me_aux = lax.axis_index("aux")
-    sides = 2 if n_aux % 2 == 0 and freqs % 2 == 0 else 1
-    my_core = me_aux % 2 if sides == 2 else jnp.int32(0)
-    where = jnp.stack([me_pair, my_core]).astype(jnp.int32)
+    wide = part // LANES
+    rest = part - wide * LANES
+    chunk_rows = wide * rank + rest
+    sides = (
+        2 if n_aux % 2 == 0 and freqs % 2 == 0 else 1,
+        2 if n_aux % 4 == 0 and freqs % 2 == 0 and local % 2 == 0 else 1,
+    )
+    where = jnp.stack([me_pair, me_aux]).astype(jnp.int32)
     vmem = pl.BlockSpec(memory_space=pltpu.VMEM)
     smem = pl.BlockSpec(memory_space=pltpu.SMEM)
 
-    share_rows = local * (freqs // sides) * depth + 16
+    share_rows = (local // sides[1]) * (freqs // sides[0]) * rank + 16
     given = (panels, amplitudes, pair_lmo.T, neighbours, pno_ranks, fock_off)
     spaces = [pltpu.VMEM] * 2 + [pltpu.SMEM] * 4
     outs = pl.pallas_call(
-        functools.partial(prep_kernel, n_pair, blocks, rows, sides),
-        out_shape=[jax.ShapeDtypeStruct((local, part, depth), BF)] * n_pair
+        functools.partial(prep_kernel, n_pair, sides),
+        out_shape=[jax.ShapeDtypeStruct((local, chunk_rows, LANES), BF)] * n_pair
         + [jax.ShapeDtypeStruct((share_rows, LANES), BF)],
         in_specs=[pl.BlockSpec(memory_space=pltpu.HBM)] * 6,
         out_specs=[vmem] * (n_pair + 1),
         scratch_shapes=[space(a.shape, a.dtype) for space, a in zip(spaces, given)]
-        + [pltpu.VMEM((local, width, depth), BF), pltpu.SemaphoreType.DMA((6,))],
+        + [
+            pltpu.VMEM((max(n_pair * rest, 16), LANES), BF),
+            pltpu.SemaphoreType.DMA((6,)),
+        ],
         cost_estimate=pl.CostEstimate(flops=0, bytes_accessed=4 * 2**20, transcendentals=0),
     )(*given)
     chunks, share = outs[:n_pair], outs[n_pair]
@@ -189,20 +232,34 @@
     tail = tail.reshape(n_pair, 16, LANES)
     ids = tail[:, 0, : local * slots].reshape(n_pair, local, slots).astype(jnp.int32)
     scale = tail[:, 1, : local * slots].reshape(n_pair, local, slots).astype(F32)
-    if sides == 2:
+    if sides[1] == 2:
         for k in range(far):
-            pieces.append(lax.ppermute(pieces[k], "aux", flip(n_aux, 1)))
+            pieces.append(lax.ppermute(pieces[k], "aux", flip(n_aux, 2)))
+    if sides[0] == 2:
+        held, pieces = pieces, []
+        for slot in range(sides[1]):
+            block = held[slot * far : (slot + 1) * far]
+            pieces += block
+            for k in range(far):
+                pieces.append(lax.ppermute(block[k], "aux", flip(n_aux, 1)))
 
     out_dims = (2 if even else 1, n_pair, max(blocks // 2, 1), local, freqs, rows_pad, LANES)
-    flops = 4 * total * part * depth * freqs * LANES
+    flops = 4 * total * part * rank * freqs * LANES
     coupled = pl.pallas_call(
-        functools.partial(couple_kernel, n_pair, blocks, sides),
+        functools.partial(
+            couple_kernel, n_pair, blocks, sides, (local, rank, part, freqs)
+        ),
         out_shape=jax.ShapeDtypeStruct(out_dims, BF if even else F32),
-        in_specs=[smem] * 3 + [vmem] * (n_pair + far * sides),
+        in_specs=[smem] * 3
+        + [pl.BlockSpec(memory_space=pltpu.HBM)]
+        + [vmem] * (n_pair - 1 + far * sides[0] * sides[1]),
         out_specs=vmem,
         scratch_shapes=[
             pltpu.VMEM((total, part, freqs * LANES), F32),
             pltpu.VMEM((part, freqs * LANES), BF),
+            pltpu.VMEM((rank, freqs * LANES), BF),
+            pltpu.VMEM((local, chunk_rows, LANES), BF),
+            pltpu.SemaphoreType.DMA,
         ],
         compiler_params=pltpu.CompilerParams(vmem_limit_bytes=40 * 2**20),
         cost_estimate=pl.CostEstimate(flops=flops, bytes_accessed=4 * 2**20, transcendentals=0),
@@ -223,7 +280,7 @@
             local, freqs, rows * rank
         )
     else:
-        flat = coupled.reshape(total, freqs, depth, LANES)[:, :, :rank, :rank]
+        flat = coupled.reshape(total, freqs, rows_pad, LANES)[:, :, :rank, :rank]
         flat = flat.reshape(total, freqs, rank * rank)
         share_aux = lax.psum_scatter(flat, "aux", scatter_dimension=2, tiled=True)
         coupled_share = lax.psum_scatter(share_aux, "pair", scatter_dimension=0, tiled=True)

time: 82.7 us -> 78.2 us (0.946)
  waiting for transfers between devices: 42.4 us -> 30 us
  starting transfers between devices: 25.6 us -> 32.8 us
    ppermute x3, waiting for transfers between devices: 14.6 us -> 2.44 us  [body(): pieces[k] = lax.ppermute(pieces[0], 'pair', flip(n_pair, k))]
    ppermute x4 -> x12, starting transfers between devices: 0.51 us -> 6.55 us  [the longest x4 4.95 us: body(): pieces.append(lax.ppermute(pieces[k], 'aux', flip(n_aux, 2)))]
    ppermute x7, starting transfers between devices: 11.1 us -> 12.7 us  [body(): received[k] = lax.ppermute(chunks[k], 'pair', flip(n_pair, k))]
    all_to_all x1, starting transfers between devices: 5.55 us -> 4.16 us  [body(): lax.all_to_all(mine, ('pair', 'aux'), 0, 0, axis_index_groups=groups, til...]
    ppermute x7, waiting for transfers between devices: 11.6 us -> 10.6 us  [body(): received[k] = lax.ppermute(chunks[k], 'pair', flip(n_pair, k))]
    ppermute x3, starting transfers between devices: 4.11 us -> 5.01 us  [body(): pieces[k] = lax.ppermute(pieces[0], 'pair', flip(n_pair, k))]
    ppermute x4 -> x12, waiting for transfers between devices: 1.13 us -> 1.98 us  [the longest x8 1.09 us: body(): pieces.append(lax.ppermute(block[k], 'aux', flip(n_aux, 1)))]
  transfers between devices with their start and end apart: 17 -> 25, of which waited for: 8 -> 13; matrix products, arithmetic and copies ran while one was open for 4% -> 4% of each run, Pallas kernels for 0% -> 0%
where the time goes in v1:
time: 78.2 us; the launch traced here: 77.7 us
  starting transfers between devices  32.8 us (42%)
  waiting for transfers between devices  30 us (38%)
  Pallas kernels  8 us (10%)
  other arithmetic  4.46 us (6%)
  local copies, waits for them, and re-layouts  1.64 us (2%)
  between operations  0.79 us (1%)
    all_to_all x1, waiting for transfers between devices, body(): lax.all_to_all(mine, ('pair', 'aux'), 0, 0, axis_index_groups=groups, til...  13.2 us
    ppermute x7, starting transfers between devices, body(): received[k] = lax.ppermute(chunks[k], 'pair', flip(n_pair, k))  12.7 us
    ppermute x7, waiting for transfers between devices, body(): received[k] = lax.ppermute(chunks[k], 'pair', flip(n_pair, k))  10.6 us
    pallas_call x1, Pallas kernels, body(): pl.pallas_call(functools.partial(couple_kernel, n_pair, blocks, sides, (l...  5.04 us
    ppermute x3, starting transfers between devices, body(): pieces[k] = lax.ppermute(pieces[0], 'pair', flip(n_pair, k))  5.01 us
    ppermute x4, starting transfers between devices, body(): pieces.append(lax.ppermute(pieces[k], 'aux', flip(n_aux, 2)))  4.95 us
    all_to_all x1, starting transfers between devices, body(): lax.all_to_all(mine, ('pair', 'aux'), 0, 0, axis_index_groups=groups, til...  4.16 us
    ppermute x1, starting transfers between devices, body(): other = lax.ppermute(share, 'pair', flip(n_pair, far))  4.13 us
  transfers between devices with their start and end apart: 25, of which 13 were waited for; matrix products, arithmetic and copies ran while one was open for 4% of the time, Pallas kernels for 0%

profile of v1, /device:TPU:0, one launch (start us, length us, event | category | flops | bytes accessed | tf_op | source)
XLA Modules:
  0.0 77.7 jit_solution(10969359085794616736)
XLA Ops:
  0.0 3.0 %shard_map.109 = (bf16[2,272,128]{2,1,0:T(8,128)(2,1)}, bf16[2,272,128]{2,1,0:T(8,128)(2,1)}, bf16[2,272,128]{2,1,0:T(8,128)(2,1)}, bf16[2,272,128]{2,1,0:T(8,12...) custom-call(bf16[2,120,2304]{2,1,0:T(8,128)(2,1)} %refs_0_.1, ...), custom_call_target="tpu_custom_call" | custom-call | bytes 4194304 | tf_op jit(solution)/shard_map/pallas_call | solution.py:208
  3.0 4.1 %collective-permute-start = (bf16[136,128]{1,0:T(8,128)(2,1)}, bf16[136,128]{1,0:T(8,128)(2,1)S(1)}, u32[]{:S(2)}, u32[]{:S(2)}) collective-permute-start(bf16[136,128]{1,0:T(8,128)(2,1)} %get-tuple-element.14), channel_id=1, source_target_pairs={{0,16},{4,20},{8,24},{12,28},{16,0},{20,4},{24,8},{28,12},{1,17},{... | collective-permute-start | bytes 104456 | tf_op jit(solution)/shard_map/ppermute | solution.py:224
  7.1 2.3 %collective-permute-start.10 = (bf16[2,272,128]{2,1,0:T(8,128)(2,1)}, bf16[2,272,128]{2,1,0:T(8,128)(2,1)S(1)}, u32[]{:S(2)}, u32[]{:S(2)}) collective-permute-start(bf16[2,272,128]{2,1,0:T(8,128)(2,1)} %get-tuple-element.22), channel_id=1, source_target_pairs={{0,28},{4,24},{8,20},{12,16},{16,12},{20,8},{24,4},{28,0},{1,29},{... | collective-permute-start | bytes 417800 | tf_op jit(solution)/shard_map/ppermute | solution.py:230
  9.4 0.5 collective-permute-start.4
  10.0 0.8 pad_maximum_fusion.refs_8_
  10.8 4.4 %collective-permute-start.3 = (bf16[2,136,128]{2,1,0:T(8,128)(2,1)S(1)}, bf16[2,136,128]{2,1,0:T(8,128)(2,1)S(1)}, u32[]{:S(2)}, u32[]{:S(2)}) collective-permute-start(bf16[2,136,128]{2,1,0:T(8,128)(2,1)S(1)} %pad_maximum_fusion.refs_8_), channel_id=1, source_target_pairs={{0,12},{4,8},{8,4},{12,0},{16,28},{20,24},{24,20},{28,16},{1,13},{... | collective-permute-start | bytes 208904 | tf_op jit(solution)/shard_map/ppermute | solution.py:229
  15.1 0.6 collective-permute-start.1
  15.8 0.7 fusion.2
  16.5 1.1 %collective-permute-done.3.refs_11_ = bf16[2,136,128]{2,1,0:T(8,128)(2,1)S(1)} collective-permute-done((bf16[2,136,128]{2,1,0:T(8,128)(2,1)S(1)}, bf16[2,136,128]{2,1,0:T(8,128)(2,1)S(1)}, u32[]{:S(2)}, u32[]{:S(2)}) %collective-permute-start.3) | collective-permute-done | bytes 69664 | tf_op jit(solution)/shard_map/ppermute | solution.py:229
  17.6 1.5 %collective-permute-start.15 = (bf16[2,136,128]{2,1,0:T(8,128)(2,1)S(1)}, bf16[2,136,128]{2,1,0:T(8,128)(2,1)S(1)}, u32[]{:S(2)}, u32[]{:S(2)}) collective-permute-start(bf16[2,136,128]{2,1,0:T(8,128)(2,1)S(1)} %pad_maximum_fusion.refs_8_), channel_id=1, source_target_pairs={{0,2},{1,3},{2,0},{3,1},{4,6},{5,7},{6,4},{7,5},{8,10},{9,11},{10,... | collective-permute-start | bytes 208904 | tf_op jit(solution)/shard_map/ppermute | solution.py:237
  19.1 0.3 collective-permute-done.2.refs_10_
  19.5 1.0 %collective-permute-done.1.refs_9_ = bf16[2,136,128]{2,1,0:T(8,128)(2,1)S(1)} collective-permute-done((bf16[2,136,128]{2,1,0:T(8,128)(2,1)S(1)}, bf16[2,136,128]{2,1,0:T(8,128)(2,1)S(1)}, u32[]{:S(2)}, u32[]{:S(2)}) %collective-permute-start.1) | collective-permute-done | bytes 69664 | tf_op jit(solution)/shard_map/ppermute | solution.py:229
  20.4 1.0 %collective-permute-start.5 = (bf16[2,272,128]{2,1,0:T(8,128)(2,1)}, bf16[2,272,128]{2,1,0:T(8,128)(2,1)S(1)}, u32[]{:S(2)}, u32[]{:S(2)}) collective-permute-start(bf16[2,272,128]{2,1,0:T(8,128)(2,1)} %get-tuple-element.17), channel_id=1, source_target_pairs={{0,8},{4,12},{8,0},{12,4},{16,24},{20,28},{24,16},{28,20},{1,9},{5... | collective-permute-start | bytes 417800 | tf_op jit(solution)/shard_map/ppermute | solution.py:230
  21.5 0.4 collective-permute-done.15.refs_16_
  21.9 2.8 %collective-permute-start.6 = (bf16[2,272,128]{2,1,0:T(8,128)(2,1)}, bf16[2,272,128]{2,1,0:T(8,128)(2,1)S(1)}, u32[]{:S(2)}, u32[]{:S(2)}) collective-permute-start(bf16[2,272,128]{2,1,0:T(8,128)(2,1)} %get-tuple-element.18), channel_id=1, source_target_pairs={{0,12},{4,8},{8,4},{12,0},{16,28},{20,24},{24,20},{28,16},{1,13},{... | collective-permute-start | bytes 417800 | tf_op jit(solution)/shard_map/ppermute | solution.py:230
  24.7 3.8 %collective-permute-start.7 = (bf16[2,272,128]{2,1,0:T(8,128)(2,1)}, bf16[2,272,128]{2,1,0:T(8,128)(2,1)S(1)}, u32[]{:S(2)}, u32[]{:S(2)}) collective-permute-start(bf16[2,272,128]{2,1,0:T(8,128)(2,1)} %get-tuple-element.19), channel_id=1, source_target_pairs={{0,16},{4,20},{8,24},{12,28},{16,0},{20,4},{24,8},{28,12},{1,17},{... | collective-permute-start | bytes 417800 | tf_op jit(solution)/shard_map/ppermute | solution.py:230
  28.4 2.4 %collective-permute-start.9 = (bf16[2,272,128]{2,1,0:T(8,128)(2,1)}, bf16[2,272,128]{2,1,0:T(8,128)(2,1)S(1)}, u32[]{:S(2)}, u32[]{:S(2)}) collective-permute-start(bf16[2,272,128]{2,1,0:T(8,128)(2,1)} %get-tuple-element.21), channel_id=1, source_target_pairs={{0,24},{4,28},{8,16},{12,20},{16,8},{20,12},{24,0},{28,4},{1,25},{... | collective-permute-start | bytes 417800 | tf_op jit(solution)/shard_map/ppermute | solution.py:230
  30.8 1.6 %collective-permute-start.16 = (bf16[2,136,128]{2,1,0:T(8,128)(2,1)S(1)}, bf16[2,136,128]{2,1,0:T(8,128)(2,1)S(1)}, u32[]{:S(2)}, u32[]{:S(2)}) collective-permute-start(bf16[2,136,128]{2,1,0:T(8,128)(2,1)S(1)} %collective-permute-done.1.refs_9_), channel_id=1, source_target_pairs={{0,2},{1,3},{2,0},{3,1},{4,6},{5,7},{6,4},{7,5},{8,10},{9,11},{10,... | collective-permute-start | bytes 208904 | tf_op jit(solution)/shard_map/ppermute | solution.py:237
  32.4 1.1 %collective-permute-done.6.refs_3_ = bf16[2,272,128]{2,1,0:T(8,128)(2,1)S(1)} collective-permute-done((bf16[2,272,128]{2,1,0:T(8,128)(2,1)}, bf16[2,272,128]{2,1,0:T(8,128)(2,1)S(1)}, u32[]{:S(2)}, u32[]{:S(2)}) %collective-permute-start.6) | collective-permute-done | bytes 139296 | tf_op jit(solution)/shard_map/ppermute | solution.py:230
  33.5 0.4 collective-permute-start.17
  33.8 8.3 %collective-permute-done.7.refs_4_ = bf16[2,272,128]{2,1,0:T(8,128)(2,1)S(1)} collective-permute-done((bf16[2,272,128]{2,1,0:T(8,128)(2,1)}, bf16[2,272,128]{2,1,0:T(8,128)(2,1)S(1)}, u32[]{:S(2)}, u32[]{:S(2)}) %collective-permute-start.7) | collective-permute-done | bytes 139296 | tf_op jit(solution)/shard_map/ppermute | solution.py:230
  42.2 1.5 %collective-permute-start.18 = (bf16[2,136,128]{2,1,0:T(8,128)(2,1)S(1)}, bf16[2,136,128]{2,1,0:T(8,128)(2,1)S(1)}, u32[]{:S(2)}, u32[]{:S(2)}) collective-permute-start(bf16[2,136,128]{2,1,0:T(8,128)(2,1)S(1)} %collective-permute-done.3.refs_11_), channel_id=1, source_target_pairs={{0,2},{1,3},{2,0},{3,1},{4,6},{5,7},{6,4},{7,5},{8,10},{9,11},{10,... | collective-permute-start | bytes 208904 | tf_op jit(solution)/shard_map/ppermute | solution.py:237
  43.7 1.2 %collective-permute-done.8.refs_5_ = bf16[2,272,128]{2,1,0:T(8,128)(2,1)S(1)} collective-permute-done((bf16[2,272,128]{2,1,0:T(8,128)(2,1)}, bf16[2,272,128]{2,1,0:T(8,128)(2,1)S(1)}, u32[]{:S(2)}, u32[]{:S(2)}) %collective-permute-start.8) | collective-permute-done | bytes 139296 | tf_op jit(solution)/shard_map/ppermute | solution.py:230
  44.9 0.5 collective-permute-start.13
  45.4 0.1 reshape.31.ids_ref
  45.5 0.5 collective-permute-start.19
  46.0 0.5 collective-permute-done.18.refs_19_
  46.5 0.5 collective-permute-start.21
  47.1 0.1 reshape.32.w_ref
  47.2 0.6 collective-permute-done.20.refs_21_
  47.7 0.2 collective-permute-done.21.refs_22_
  47.9 0.4 collective-permute-done.22.refs_23_
  48.3 0.9 %copy-done = bf16[2,272,128]{2,1,0:T(8,128)(2,1)S(1)} copy-done((bf16[2,272,128]{2,1,0:T(8,128)(2,1)S(1)}, bf16[2,272,128]{2,1,0:T(8,128)(2,1)}, u32[]{:S(2)}) %copy-start) | copy-done | bytes 139288
  49.2 5.0 %shard_map.110 = bf16[2,8,2,2,2,32,128]{6,5,4,3,2,1,0:T(8,128)(2,1)S(1)} custom-call(s32[2]{0:T(128)S(1)} %pad_add_fusion.where, s32[8,2,8]{2,1,0:T(2,128)S(1)} %reshape.31.ids_ref, f32[8,2,8]{2,1,0:T(2,128)S(1)} %reshape.32.w_ref, bf16[2,272,128]{2,1,0:T(8,128)(2,1)S(1)} %copy-done, bf16[2,272,128]{2,1,0:T(8,128)(2,1)S(1)} %collective-permute-done.4.refs_1_, ...), custom_call_target="tpu_custom_call" | custom-call | flops 566231040 | bytes 4194304 | tf_op jit(solution)/shard_map/pallas_call | solution.py:248
  54.3 0.2 collective-permute-start.23
  54.5 1.7 %collective-permute-done.23 = bf16[8,2,2,2,32,128]{5,4,3,2,1,0:T(8,128)(2,1)S(1)} collective-permute-done((bf16[8,2,2,2,32,128]{5,4,3,2,1,0:T(8,128)(2,1)S(1)}, bf16[8,2,2,2,32,128]{5,4,3,2,1,0:T(8,128)(2,1)S(1)}, u32[]{:S(2)}, u32[]{:S(2)}) %collective-permute-start.23) | collective-permute-done | bytes 524320 | tf_op jit(solution)/shard_map/ppermute | solution.py:269
  56.2 1.0 %fusion = bf16[8,2,2,2,32,128]{5,4,3,2,1,0:T(8,128)(2,1)} fusion(bf16[8,2,2,2,32,128]{5,4,3,2,1,0:T(8,128)(2,1)S(1)} %collective-permute-done.23, bf16[2,8,2,2,2,32,128]{6,5,4,3,2,1,0:T(8,128)(2,1)S(1)} %shard_map.110), kind=kLoop, calls=%fused_computation.1 | loop fusion | flops 1048576 | bytes 1572864 | tf_op jit(solution)/shard_map/convert_element_type | solution.py:270
  57.2 4.2 %all-to-all-start = ((bf16[16,2,2,32,128]{4,3,2,1,0:T(8,128)(2,1)}), bf16[16,2,2,32,128]{4,3,2,1,0:T(8,128)(2,1)S(1)}, u32[]{:S(2)}, u32[]{:S(2)}) async-start(bf16[16,2,2,32,128]{4,3,2,1,0:T(8,128)(2,1)} %bitcast.13), calls=%async_computation | async-start | bytes 1048576 | tf_op jit(solution)/shard_map/all_to_all | solution.py:276
  61.4 0.1 constant_dynamic-slice_fusion
  61.5 0.1 copy.15
  62.3 0.1 constant_dynamic-slice_fusion.1
  62.3 0.2 fusion.5
  62.6 0.9 %convert_multiply_fusion = f32[2,2,30,120]{3,2,1,0:T(8,128)S(1)} fusion(bf16[2,2,120,120]{3,2,1,0:T(8,128)(2,1)} %refs_1_.1, s32[]{:T(128)S(6)} %select_n.7, f32[2]{0:T(128)S(1)} %broadcast_multiply_fusion, f32[2,30,120]{2,1,0:T(8,128)S(1)} %add_subtract_fusion), kind=kLoop, calls=%fused_computation.8 | loop fusion | flops 43200 | bytes 115212 | tf_op jit(solution)/shard_map/mul | solution.py:300
  63.4 0.1 reshape.27
  63.6 13.2 %all-to-all-done = bf16[16,2,2,32,128]{4,3,2,1,0:T(8,128)(2,1)S(1)} async-done(((bf16[16,2,2,32,128]{4,3,2,1,0:T(8,128)(2,1)}), bf16[16,2,2,32,128]{4,3,2,1,0:T(8,128)(2,1)S(1)}, u32[]{:S(2)}, u32[]{:S(2)}) %all-to-all-start) | async-done | bytes 524320 | tf_op jit(solution)/shard_map/all_to_all | solution.py:276
  76.8 0.1 convert_reduce_fusion
  76.9 0.1 reshape.30
  77.0 0.7 add_add_fusion
  (41 shorter events, 0.4 us)
Async XLA Ops:
  3.0 7.0 %collective-permute-start = (bf16[136,128]{1,0:T(8,128)(2,1)}, bf16[136,128]{1,0:T(8,128)(2,1)S(1)}, u32[]{:S(2)}, u32[]{:S(2)}) collective-permute-start(bf16[136,128]{1,0:T(8,128)(2,1)} %get-tuple-element.14), channel_id=1, source_target_pairs={{0,16},{4,20},{8,24},{12,28},{16,0},{20,4},{24,8},{28,12},{1,17},{... | collective-permute-start | bytes 104456 | tf_op jit(solution)/shard_map/ppermute | solution.py:224
  7.1 21.3 %collective-permute-start.10 = (bf16[2,272,128]{2,1,0:T(8,128)(2,1)}, bf16[2,272,128]{2,1,0:T(8,128)(2,1)S(1)}, u32[]{:S(2)}, u32[]{:S(2)}) collective-permute-start(bf16[2,272,128]{2,1,0:T(8,128)(2,1)} %get-tuple-element.22), channel_id=1, source_target_pairs={{0,28},{4,24},{8,20},{12,16},{16,12},{20,8},{24,4},{28,0},{1,29},{... | collective-permute-start | bytes 417800 | tf_op jit(solution)/shard_map/ppermute | solution.py:230
  9.4 19.1 %collective-permute-start.4 = (bf16[2,272,128]{2,1,0:T(8,128)(2,1)}, bf16[2,272,128]{2,1,0:T(8,128)(2,1)S(1)}, u32[]{:S(2)}, u32[]{:S(2)}) collective-permute-start(bf16[2,272,128]{2,1,0:T(8,128)(2,1)} %get-tuple-element.16), channel_id=1, source_target_pairs={{0,4},{4,0},{8,12},{12,8},{16,20},{20,16},{24,28},{28,24},{1,5},{5... | collective-permute-start | bytes 417800 | tf_op jit(solution)/shard_map/ppermute | solution.py:230
  10.8 6.8 %collective-permute-start.3 = (bf16[2,136,128]{2,1,0:T(8,128)(2,1)S(1)}, bf16[2,136,128]{2,1,0:T(8,128)(2,1)S(1)}, u32[]{:S(2)}, u32[]{:S(2)}) collective-permute-start(bf16[2,136,128]{2,1,0:T(8,128)(2,1)S(1)} %pad_maximum_fusion.refs_8_), channel_id=1, source_target_pairs={{0,12},{4,8},{8,4},{12,0},{16,28},{20,24},{24,20},{28,16},{1,13},{... | collective-permute-start | bytes 208904 | tf_op jit(solution)/shard_map/ppermute | solution.py:229
  15.1 4.3 %collective-permute-start.2 = (bf16[2,136,128]{2,1,0:T(8,128)(2,1)S(1)}, bf16[2,136,128]{2,1,0:T(8,128)(2,1)S(1)}, u32[]{:S(2)}, u32[]{:S(2)}) collective-permute-start(bf16[2,136,128]{2,1,0:T(8,128)(2,1)S(1)} %pad_maximum_fusion.refs_8_), channel_id=1, source_target_pairs={{0,8},{4,12},{8,0},{12,4},{16,24},{20,28},{24,16},{28,20},{1,9},{5... | collective-permute-start | bytes 208904 | tf_op jit(solution)/shard_map/ppermute | solution.py:229
  15.1 5.3 %collective-permute-start.1 = (bf16[2,136,128]{2,1,0:T(8,128)(2,1)S(1)}, bf16[2,136,128]{2,1,0:T(8,128)(2,1)S(1)}, u32[]{:S(2)}, u32[]{:S(2)}) collective-permute-start(bf16[2,136,128]{2,1,0:T(8,128)(2,1)S(1)} %pad_maximum_fusion.refs_8_), channel_id=1, source_target_pairs={{0,4},{4,0},{8,12},{12,8},{16,20},{20,16},{24,28},{28,24},{1,5},{5... | collective-permute-start | bytes 208904 | tf_op jit(solution)/shard_map/ppermute | solution.py:229
  17.6 4.3 %collective-permute-start.15 = (bf16[2,136,128]{2,1,0:T(8,128)(2,1)S(1)}, bf16[2,136,128]{2,1,0:T(8,128)(2,1)S(1)}, u32[]{:S(2)}, u32[]{:S(2)}) collective-permute-start(bf16[2,136,128]{2,1,0:T(8,128)(2,1)S(1)} %pad_maximum_fusion.refs_8_), channel_id=1, source_target_pairs={{0,2},{1,3},{2,0},{3,1},{4,6},{5,7},{6,4},{7,5},{8,10},{9,11},{10,... | collective-permute-start | bytes 208904 | tf_op jit(solution)/shard_map/ppermute | solution.py:237
  19.4 5.2 %collective-permute-start.11 = (bf16[2,136,128]{2,1,0:T(8,128)(2,1)S(1)}, bf16[2,136,128]{2,1,0:T(8,128)(2,1)S(1)}, u32[]{:S(2)}, u32[]{:S(2)}) collective-permute-start(bf16[2,136,128]{2,1,0:T(8,128)(2,1)S(1)} %pad_maximum_fusion.refs_8_), channel_id=1, source_target_pairs={{0,1},{1,0},{2,3},{3,2},{4,5},{5,4},{6,7},{7,6},{8,9},{9,8},{10,11... | collective-permute-start | bytes 208904 | tf_op jit(solution)/shard_map/ppermute | solution.py:244
  20.4 10.4 %collective-permute-start.5 = (bf16[2,272,128]{2,1,0:T(8,128)(2,1)}, bf16[2,272,128]{2,1,0:T(8,128)(2,1)S(1)}, u32[]{:S(2)}, u32[]{:S(2)}) collective-permute-start(bf16[2,272,128]{2,1,0:T(8,128)(2,1)} %get-tuple-element.17), channel_id=1, source_target_pairs={{0,8},{4,12},{8,0},{12,4},{16,24},{20,28},{24,16},{28,20},{1,9},{5... | collective-permute-start | bytes 417800 | tf_op jit(solution)/shard_map/ppermute | solution.py:230
  21.9 11.6 %collective-permute-start.6 = (bf16[2,272,128]{2,1,0:T(8,128)(2,1)}, bf16[2,272,128]{2,1,0:T(8,128)(2,1)S(1)}, u32[]{:S(2)}, u32[]{:S(2)}) collective-permute-start(bf16[2,272,128]{2,1,0:T(8,128)(2,1)} %get-tuple-element.18), channel_id=1, source_target_pairs={{0,12},{4,8},{8,4},{12,0},{16,28},{20,24},{24,20},{28,16},{1,13},{... | collective-permute-start | bytes 417800 | tf_op jit(solution)/shard_map/ppermute | solution.py:230
  24.7 17.5 %collective-permute-start.7 = (bf16[2,272,128]{2,1,0:T(8,128)(2,1)}, bf16[2,272,128]{2,1,0:T(8,128)(2,1)S(1)}, u32[]{:S(2)}, u32[]{:S(2)}) collective-permute-start(bf16[2,272,128]{2,1,0:T(8,128)(2,1)} %get-tuple-element.19), channel_id=1, source_target_pairs={{0,16},{4,20},{8,24},{12,28},{16,0},{20,4},{24,8},{28,12},{1,17},{... | collective-permute-start | bytes 417800 | tf_op jit(solution)/shard_map/ppermute | solution.py:230
  28.4 16.4 %collective-permute-start.8 = (bf16[2,272,128]{2,1,0:T(8,128)(2,1)}, bf16[2,272,128]{2,1,0:T(8,128)(2,1)S(1)}, u32[]{:S(2)}, u32[]{:S(2)}) collective-permute-start(bf16[2,272,128]{2,1,0:T(8,128)(2,1)} %get-tuple-element.20), channel_id=1, source_target_pairs={{0,20},{4,16},{8,28},{12,24},{16,4},{20,0},{24,12},{28,8},{1,21},{... | collective-permute-start | bytes 417800 | tf_op jit(solution)/shard_map/ppermute | solution.py:230
  28.4 16.4 %collective-permute-start.9 = (bf16[2,272,128]{2,1,0:T(8,128)(2,1)}, bf16[2,272,128]{2,1,0:T(8,128)(2,1)S(1)}, u32[]{:S(2)}, u32[]{:S(2)}) collective-permute-start(bf16[2,272,128]{2,1,0:T(8,128)(2,1)} %get-tuple-element.21), channel_id=1, source_target_pairs={{0,24},{4,28},{8,16},{12,20},{16,8},{20,12},{24,0},{28,4},{1,25},{... | collective-permute-start | bytes 417800 | tf_op jit(solution)/shard_map/ppermute | solution.py:230
  30.8 14.6 %collective-permute-start.16 = (bf16[2,136,128]{2,1,0:T(8,128)(2,1)S(1)}, bf16[2,136,128]{2,1,0:T(8,128)(2,1)S(1)}, u32[]{:S(2)}, u32[]{:S(2)}) collective-permute-start(bf16[2,136,128]{2,1,0:T(8,128)(2,1)S(1)} %collective-permute-done.1.refs_9_), channel_id=1, source_target_pairs={{0,2},{1,3},{2,0},{3,1},{4,6},{5,7},{6,4},{7,5},{8,10},{9,11},{10,... | collective-permute-start | bytes 208904 | tf_op jit(solution)/shard_map/ppermute | solution.py:237
  33.5 12.0 %collective-permute-start.17 = (bf16[2,136,128]{2,1,0:T(8,128)(2,1)S(1)}, bf16[2,136,128]{2,1,0:T(8,128)(2,1)S(1)}, u32[]{:S(2)}, u32[]{:S(2)}) collective-permute-start(bf16[2,136,128]{2,1,0:T(8,128)(2,1)S(1)} %collective-permute-done.2.refs_10_), channel_id=1, source_target_pairs={{0,2},{1,3},{2,0},{3,1},{4,6},{5,7},{6,4},{7,5},{8,10},{9,11},{10,... | collective-permute-start | bytes 208904 | tf_op jit(solution)/shard_map/ppermute | solution.py:237
  42.2 4.3 %collective-permute-start.18 = (bf16[2,136,128]{2,1,0:T(8,128)(2,1)S(1)}, bf16[2,136,128]{2,1,0:T(8,128)(2,1)S(1)}, u32[]{:S(2)}, u32[]{:S(2)}) collective-permute-start(bf16[2,136,128]{2,1,0:T(8,128)(2,1)S(1)} %collective-permute-done.3.refs_11_), channel_id=1, source_target_pairs={{0,2},{1,3},{2,0},{3,1},{4,6},{5,7},{6,4},{7,5},{8,10},{9,11},{10,... | collective-permute-start | bytes 208904 | tf_op jit(solution)/shard_map/ppermute | solution.py:237
  44.9 1.6 %collective-permute-start.12 = (bf16[2,136,128]{2,1,0:T(8,128)(2,1)S(1)}, bf16[2,136,128]{2,1,0:T(8,128)(2,1)S(1)}, u32[]{:S(2)}, u32[]{:S(2)}) collective-permute-start(bf16[2,136,128]{2,1,0:T(8,128)(2,1)S(1)} %collective-permute-done.1.refs_9_), channel_id=1, source_target_pairs={{0,1},{1,0},{2,3},{3,2},{4,5},{5,4},{6,7},{7,6},{8,9},{9,8},{10,11... | collective-permute-start | bytes 208904 | tf_op jit(solution)/shard_map/ppermute | solution.py:244
  44.9 2.1 %collective-permute-start.13 = (bf16[2,136,128]{2,1,0:T(8,128)(2,1)S(1)}, bf16[2,136,128]{2,1,0:T(8,128)(2,1)S(1)}, u32[]{:S(2)}, u32[]{:S(2)}) collective-permute-start(bf16[2,136,128]{2,1,0:T(8,128)(2,1)S(1)} %collective-permute-done.2.refs_10_), channel_id=1, source_target_pairs={{0,1},{1,0},{2,3},{3,2},{4,5},{5,4},{6,7},{7,6},{8,9},{9,8},{10,11... | collective-permute-start | bytes 208904 | tf_op jit(solution)/shard_map/ppermute | solution.py:244
  45.5 1.7 %collective-permute-start.14 = (bf16[2,136,128]{2,1,0:T(8,128)(2,1)S(1)}, bf16[2,136,128]{2,1,0:T(8,128)(2,1)S(1)}, u32[]{:S(2)}, u32[]{:S(2)}) collective-permute-start(bf16[2,136,128]{2,1,0:T(8,128)(2,1)S(1)} %collective-permute-done.3.refs_11_), channel_id=1, source_target_pairs={{0,1},{1,0},{2,3},{3,2},{4,5},{5,4},{6,7},{7,6},{8,9},{9,8},{10,11... | collective-permute-start | bytes 208904 | tf_op jit(solution)/shard_map/ppermute | solution.py:244
  45.5 1.6 %collective-permute-start.19 = (bf16[2,136,128]{2,1,0:T(8,128)(2,1)S(1)}, bf16[2,136,128]{2,1,0:T(8,128)(2,1)S(1)}, u32[]{:S(2)}, u32[]{:S(2)}) collective-permute-start(bf16[2,136,128]{2,1,0:T(8,128)(2,1)S(1)} %collective-permute-done.15.refs_16_), channel_id=1, source_target_pairs={{0,1},{1,0},{2,3},{3,2},{4,5},{5,4},{6,7},{7,6},{8,9},{9,8},{10,11... | collective-permute-start | bytes 208904 | tf_op jit(solution)/shard_map/ppermute | solution.py:244
  46.5 1.3 %collective-permute-start.20 = (bf16[2,136,128]{2,1,0:T(8,128)(2,1)S(1)}, bf16[2,136,128]{2,1,0:T(8,128)(2,1)S(1)}, u32[]{:S(2)}, u32[]{:S(2)}) collective-permute-start(bf16[2,136,128]{2,1,0:T(8,128)(2,1)S(1)} %collective-permute-done.16.refs_17_), channel_id=1, source_target_pairs={{0,1},{1,0},{2,3},{3,2},{4,5},{5,4},{6,7},{7,6},{8,9},{9,8},{10,11... | collective-permute-start | bytes 208904 | tf_op jit(solution)/shard_map/ppermute | solution.py:244
  46.5 1.4 %collective-permute-start.21 = (bf16[2,136,128]{2,1,0:T(8,128)(2,1)S(1)}, bf16[2,136,128]{2,1,0:T(8,128)(2,1)S(1)}, u32[]{:S(2)}, u32[]{:S(2)}) collective-permute-start(bf16[2,136,128]{2,1,0:T(8,128)(2,1)S(1)} %collective-permute-done.17.refs_18_), channel_id=1, source_target_pairs={{0,1},{1,0},{2,3},{3,2},{4,5},{5,4},{6,7},{7,6},{8,9},{9,8},{10,11... | collective-permute-start | bytes 208904 | tf_op jit(solution)/shard_map/ppermute | solution.py:244
  47.0 1.3 %collective-permute-start.22 = (bf16[2,136,128]{2,1,0:T(8,128)(2,1)S(1)}, bf16[2,136,128]{2,1,0:T(8,128)(2,1)S(1)}, u32[]{:S(2)}, u32[]{:S(2)}) collective-permute-start(bf16[2,136,128]{2,1,0:T(8,128)(2,1)S(1)} %collective-permute-done.18.refs_19_), channel_id=1, source_target_pairs={{0,1},{1,0},{2,3},{3,2},{4,5},{5,4},{6,7},{7,6},{8,9},{9,8},{10,11... | collective-permute-start | bytes 208904 | tf_op jit(solution)/shard_map/ppermute | solution.py:244
  48.2 0.9 %copy-start = (bf16[2,272,128]{2,1,0:T(8,128)(2,1)S(1)}, bf16[2,272,128]{2,1,0:T(8,128)(2,1)}, u32[]{:S(2)}) copy-start(bf16[2,272,128]{2,1,0:T(8,128)(2,1)} %get-tuple-element.15.refs_0_) | copy-start | bytes 417796
  54.3 2.0 %collective-permute-start.23 = (bf16[8,2,2,2,32,128]{5,4,3,2,1,0:T(8,128)(2,1)S(1)}, bf16[8,2,2,2,32,128]{5,4,3,2,1,0:T(8,128)(2,1)S(1)}, u32[]{:S(2)}, u32[]{:S(2)}) collective-permute-start(bf16[8,2,2,2,32,128]{5,4,3,2,1,0:T(8,128)(2,1)S(1)} %slice_bitcast_fusion), channel_id=1, source_target_pairs={{0,1},{1,0},{2,3},{3,2},{4,5},{5,4},{6,7},{7,6},{8,9},{9,8},{10,11... | collective-permute-start | bytes 1572872 | tf_op jit(solution)/shard_map/ppermute | solution.py:269
  54.5 6.9 %copy-start.2 = (s32[16,2]{0,1:T(2,128)S(1)}, s32[16,2]{0,1:T(2,128)}, u32[]{:S(2)}) copy-start(s32[16,2]{0,1:T(2,128)} %param.17) | copy-start | bytes 388
  54.5 7.8 %copy-start.3 = (f32[2,120]{1,0:T(2,128)S(1)}, f32[2,120]{1,0:T(2,128)}, u32[]{:S(2)}) copy-start(f32[2,120]{1,0:T(2,128)} %param.14) | copy-start | bytes 2884
  54.5 7.9 %copy-start.4 = (f32[32]{0:T(128)S(1)}, f32[32]{0:T(128)}, u32[]{:S(2)}) copy-start(f32[32]{0:T(128)} %param.15) | copy-start | bytes 388
  54.5 8.0 %copy-start.5 = (f32[2]{0:T(128)S(1)}, f32[2]{0:T(128)}, u32[]{:S(2)}) copy-start(f32[2]{0:T(128)} %constant.24.clone) | copy-start | bytes 28
  57.2 19.8 %copy-start.1 = (f32[2,2,3600]{2,1,0:T(2,128)S(1)}, f32[2,2,3600]{2,1,0:T(2,128)}, u32[]{:S(2)}) copy-start(f32[2,2,3600]{2,1,0:T(2,128)} %param.13) | copy-start | bytes 172804
  57.2 19.6 %all-to-all-start = ((bf16[16,2,2,32,128]{4,3,2,1,0:T(8,128)(2,1)}), bf16[16,2,2,32,128]{4,3,2,1,0:T(8,128)(2,1)S(1)}, u32[]{:S(2)}, u32[]{:S(2)}) async-start(bf16[16,2,2,32,128]{4,3,2,1,0:T(8,128)(2,1)} %bitcast.13), calls=%async_computation | async-start | bytes 1048576 | tf_op jit(solution)/shard_map/all_to_all | solution.py:276

commit v2 on v1

--- a/solution.py
+++ b/solution.py
@@ -26,8 +26,8 @@
 
 
 def prep_kernel(n_pair, sides, *refs):
-    inputs, chunks, share_ref = refs[:6], refs[6 : 6 + n_pair], refs[6 + n_pair]
-    buffers, (turned, sems) = refs[7 + n_pair : 13 + n_pair], refs[13 + n_pair :]
+    inputs, chunks, share_ref = refs[:6], refs[6], refs[7]
+    buffers, (turned, sems) = refs[8:14], refs[14:]
     copies = [
         pltpu.make_async_copy(src, dst, sems.at[i])
         for i, (src, dst) in enumerate(zip(inputs, buffers))
@@ -84,7 +84,7 @@
             for w in range(wide):
                 start = pl.multiple_of(((me ^ k) * wide + w) * LANES, LANES)
                 x = panels[lp, :, pl.ds(start, LANES)].astype(F32)
-                chunks[k][lp, w * rank : (w + 1) * rank, :] = jnp.where(keep, x, 0.0).astype(BF)
+                chunks[me ^ k, lp, w * rank : (w + 1) * rank, :] = jnp.where(keep, x, 0.0).astype(BF)
         if rest:
             for t in range(n_pair * rest // LANES):
                 start = n_pair * wide * LANES + t * LANES
@@ -94,14 +94,14 @@
                 turned[t * LANES : (t + 1) * LANES, :] = x.T.astype(BF)
             for k in range(n_pair):
                 start = pl.multiple_of((me ^ k) * rest, 16)
-                chunks[k][lp, wide * rank :, :] = turned[pl.ds(start, rest), :]
+                chunks[me ^ k, lp, wide * rank :, :] = turned[pl.ds(start, rest), :]
 
 
 def couple_kernel(n_pair, blocks, sides, shape, where, ids_ref, w_ref, *refs):
     half = n_pair // 2
     members = sides[0] * sides[1]
-    panels, mats = list(refs[:n_pair]), refs[n_pair : n_pair + half * members]
-    out_ref, proj, mixed, mat, own, sem = refs[n_pair + half * members :]
+    panels, mats = refs[0], refs[1 : 1 + half * members]
+    out_ref, proj, mixed, mat = refs[1 + half * members :]
     local, rank, part, freqs = shape
     wide = part // LANES
     rest = part - wide * LANES
@@ -109,14 +109,9 @@
     slots = ids_ref.shape[2]
     me, aux = where[0], where[1]
     many, take = local // sides[1], freqs // sides[0]
-    copy = pltpu.make_async_copy(panels[0], own, sem)
-    copy.start()
-    panels[0] = own
-    order = list(range(1, n_pair)) + [0]
+    order = list(range(n_pair))
 
     for k in order:
-        if k == 0:
-            copy.wait()
         for pair_slot in range(sides[1]):
             for i in range(many):
                 lp = member(aux ^ (pair_slot * 2), sides)[0] * many + i
@@ -128,14 +123,14 @@
                 index = k * local + lp
                 for w in range(wide):
                     proj[index, w * LANES : (w + 1) * LANES, :] = lax.dot_general(
-                        panels[k][lp, w * rank : (w + 1) * rank, :],
+                        panels[me ^ k, lp, w * rank : (w + 1) * rank, :],
                         mat[...],
                         (((0,), (0,)), ((), ())),
                         preferred_element_type=F32,
                     )
                 if rest:
                     proj[index, wide * LANES :, :] = jnp.dot(
-                        panels[k][lp, wide * rank :, :][:, :rank],
+                        panels[me ^ k, lp, wide * rank :, :][:, :rank],
                         mat[...],
                         preferred_element_type=F32,
                     )
@@ -157,12 +152,12 @@
             got = None
             if wide:
                 x = jnp.concatenate(
-                    [panels[k][lp, w * rank : (w + 1) * rank, :] for w in range(wide)], axis=1
+                    [panels[me ^ k, lp, w * rank : (w + 1) * rank, :] for w in range(wide)], axis=1
                 )
                 got = jnp.dot(x, mixed[: wide * LANES, :], preferred_element_type=F32)
             if rest:
                 more = lax.dot_general(
-                    panels[k][lp, wide * rank :, :],
+                    panels[me ^ k, lp, wide * rank :, :],
                     mixed[wide * LANES :, :],
                     (((0,), (0,)), ((), ())),
                     preferred_element_type=F32,
@@ -196,7 +191,7 @@
     chunk_rows = wide * rank + rest
     sides = (
         2 if n_aux % 2 == 0 and freqs % 2 == 0 else 1,
-        2 if n_aux % 4 == 0 and freqs % 2 == 0 and local % 2 == 0 else 1,
+        1,
     )
     where = jnp.stack([me_pair, me_aux]).astype(jnp.int32)
     vmem = pl.BlockSpec(memory_space=pltpu.VMEM)
@@ -207,10 +202,10 @@
     spaces = [pltpu.VMEM] * 2 + [pltpu.SMEM] * 4
     outs = pl.pallas_call(
         functools.partial(prep_kernel, n_pair, sides),
-        out_shape=[jax.ShapeDtypeStruct((local, chunk_rows, LANES), BF)] * n_pair
+        out_shape=[jax.ShapeDtypeStruct((n_pair, local, chunk_rows, LANES), BF)]
         + [jax.ShapeDtypeStruct((share_rows, LANES), BF)],
         in_specs=[pl.BlockSpec(memory_space=pltpu.HBM)] * 6,
-        out_specs=[vmem] * (n_pair + 1),
+        out_specs=[vmem] * 2,
         scratch_shapes=[space(a.shape, a.dtype) for space, a in zip(spaces, given)]
         + [
             pltpu.VMEM((max(n_pair * rest, 16), LANES), BF),
@@ -218,16 +213,15 @@
         ],
         cost_estimate=pl.CostEstimate(flops=0, bytes_accessed=4 * 2**20, transcendentals=0),
     )(*given)
-    chunks, share = outs[:n_pair], outs[n_pair]
+    chunks, share = outs
 
     far = n_pair // 2
     other = lax.ppermute(share, "pair", flip(n_pair, far))
     pieces = [jnp.concatenate([share[None], other[None]], axis=0)] + [None] * (far - 1)
-    received = [chunks[0]] + [None] * (n_pair - 1)
+    received = lax.all_to_all(chunks, "pair", 0, 0, tiled=True)
     for k in range(1, n_pair):
         if k < far:
             pieces[k] = lax.ppermute(pieces[0], "pair", flip(n_pair, k))
-        received[k] = lax.ppermute(chunks[k], "pair", flip(n_pair, k))
     tail = jnp.stack([piece[:, share_rows - 16 :] for piece in pieces], axis=1)
     tail = tail.reshape(n_pair, 16, LANES)
     ids = tail[:, 0, : local * slots].reshape(n_pair, local, slots).astype(jnp.int32)
@@ -251,19 +245,16 @@
         ),
         out_shape=jax.ShapeDtypeStruct(out_dims, BF if even else F32),
         in_specs=[smem] * 3
-        + [pl.BlockSpec(memory_space=pltpu.HBM)]
-        + [vmem] * (n_pair - 1 + far * sides[0] * sides[1]),
+        + [vmem] * (1 + far * sides[0] * sides[1]),
         out_specs=vmem,
         scratch_shapes=[
             pltpu.VMEM((total, part, freqs * LANES), F32),
             pltpu.VMEM((part, freqs * LANES), BF),
             pltpu.VMEM((rank, freqs * LANES), BF),
-            pltpu.VMEM((local, chunk_rows, LANES), BF),
-            pltpu.SemaphoreType.DMA,
         ],
         compiler_params=pltpu.CompilerParams(vmem_limit_bytes=40 * 2**20),
         cost_estimate=pl.CostEstimate(flops=flops, bytes_accessed=4 * 2**20, transcendentals=0),
-    )(where, ids, scale, *received, *pieces)
+    )(where, ids, scale, received, *pieces)
 
     if even:
         other = lax.ppermute(coupled[1], "aux", flip(n_aux, 1))

time: 78.2 us -> 80.7 us (1.032)
  waiting for transfers between devices: 30 us -> 47.8 us
  starting transfers between devices: 32.8 us -> 20.4 us
  other arithmetic: 4.46 us -> 3 us
  local copies, waits for them, and re-layouts: 1.64 us -> 0.73 us
    ppermute x1, waiting for transfers between devices: 0.01 us -> 27.1 us  [body(): other = lax.ppermute(share, 'pair', flip(n_pair, far))]
    ppermute x11 -> x0, starting transfers between devices: 17.7 us -> none  [the longest x7 12.7 us: body(): received[k] = lax.ppermute(chunks[k], 'pair', flip(n_pair, k))]
    ppermute x11 -> x0, waiting for transfers between devices: 11.5 us -> none  [the longest x7 10.6 us: body(): received[k] = lax.ppermute(chunks[k], 'pair', flip(n_pair, k))]
    all_to_all x0 -> x1, starting transfers between devices: none -> 7.43 us  [body(): received = lax.all_to_all(chunks, 'pair', 0, 0, tiled=True)]
    ppermute x3, waiting for transfers between devices: 2.44 us -> 4.74 us  [body(): pieces[k] = lax.ppermute(pieces[0], 'pair', flip(n_pair, k))]
    all_to_all x1, starting transfers between devices: 4.16 us -> 5.64 us  [body(): lax.all_to_all(mine, ('pair', 'aux'), 0, 0, axis_index_groups=groups, til...]
    ppermute x3, starting transfers between devices: 5.01 us -> 3.54 us  [body(): pieces[k] = lax.ppermute(pieces[0], 'pair', flip(n_pair, k))]
    ppermute x1, starting transfers between devices: 4.13 us -> 2.92 us  [body(): other = lax.ppermute(share, 'pair', flip(n_pair, far))]
  transfers between devices with their start and end apart: 25 -> 11, of which waited for: 13 -> 9; matrix products, arithmetic and copies ran while one was open for 4% -> 2% of each run, Pallas kernels for 0% -> 0%
where the time goes in v2:
time: 80.7 us; the launch traced here: 80.3 us
  waiting for transfers between devices  47.8 us (59%)
  starting transfers between devices  20.4 us (25%)
  Pallas kernels  7.54 us (9%)
  other arithmetic  3 us (4%)
    ppermute x1, waiting for transfers between devices, body(): other = lax.ppermute(share, 'pair', flip(n_pair, far))  27.1 us
    all_to_all x1, waiting for transfers between devices, body(): lax.all_to_all(mine, ('pair', 'aux'), 0, 0, axis_index_groups=groups, til...  13.9 us
    all_to_all x1, starting transfers between devices, body(): received = lax.all_to_all(chunks, 'pair', 0, 0, tiled=True)  7.43 us
    all_to_all x1, starting transfers between devices, body(): lax.all_to_all(mine, ('pair', 'aux'), 0, 0, axis_index_groups=groups, til...  5.64 us
    ppermute x3, waiting for transfers between devices, body(): pieces[k] = lax.ppermute(pieces[0], 'pair', flip(n_pair, k))  4.74 us
    pallas_call x1, Pallas kernels, body(): pl.pallas_call(functools.partial(couple_kernel, n_pair, blocks, sides, (l...  4.56 us
    ppermute x3, starting transfers between devices, body(): pieces[k] = lax.ppermute(pieces[0], 'pair', flip(n_pair, k))  3.54 us
    pallas_call x1, Pallas kernels, body(): pl.pallas_call(functools.partial(prep_kernel, n_pair, sides), out_shape=[...  2.97 us
  transfers between devices with their start and end apart: 11, of which 9 were waited for; matrix products, arithmetic and copies ran while one was open for 2% of the time, Pallas kernels for 0%

profile of v2, /device:TPU:0, one launch (start us, length us, event | category | flops | bytes accessed | tf_op | source)
XLA Modules:
  0.0 80.3 jit_solution(456962556359866447)
XLA Ops:
  0.0 3.0 %shard_map.109 = (bf16[8,2,272,128]{3,2,1,0:T(8,128)(2,1)}, bf16[256,128]{1,0:T(8,128)(2,1)}) custom-call(bf16[2,120,2304]{2,1,0:T(8,128)(2,1)} %refs_0_.1, bf16[2,2,120,120]{3,2,1,0:T(8,128)(2,1)} %refs_1_.1, s32[2,16]{1,0:T(2,128)} %bitcast.32, s32[2,8]{1,0:T(2,128)} %refs_3_.1, s32[2]{0:T(128)} %refs_4_.1, f32[32,32]{1,0:T(8,128)} %refs_5_.1), custom_call_target="tpu_custom_call" | custom-call | bytes 4194304 | tf_op jit(solution)/shard_map/pallas_call | solution.py:203
  3.0 0.0 copy-start
  3.0 7.4 %all-to-all-start = ((bf16[8,2,272,128]{3,2,1,0:T(8,128)(2,1)}), bf16[8,2,272,128]{3,2,1,0:T(8,128)(2,1)S(1)}, u32[]{:S(2)}, u32[]{:S(2)}) async-start(bf16[8,2,272,128]{3,2,1,0:T(8,128)(2,1)} %get-tuple-element.8), calls=%async_computation | async-start | bytes 2228224 | tf_op jit(solution)/shard_map/all_to_all | solution.py:221
  10.4 0.0 copy-done
  10.4 2.9 %collective-permute-start = (bf16[256,128]{1,0:T(8,128)(2,1)S(1)}, bf16[256,128]{1,0:T(8,128)(2,1)S(1)}, u32[]{:S(2)}, u32[]{:S(2)}) collective-permute-start(bf16[256,128]{1,0:T(8,128)(2,1)S(1)} %copy-done), channel_id=1, source_target_pairs={{0,16},{4,20},{8,24},{12,28},{16,0},{20,4},{24,8},{28,12},{1,17},{... | collective-permute-start | bytes 196616 | tf_op jit(solution)/shard_map/ppermute | solution.py:219
  13.3 27.1 %collective-permute-done = bf16[256,128]{1,0:T(8,128)(2,1)S(1)} collective-permute-done((bf16[256,128]{1,0:T(8,128)(2,1)S(1)}, bf16[256,128]{1,0:T(8,128)(2,1)S(1)}, u32[]{:S(2)}, u32[]{:S(2)}) %collective-permute-start) | collective-permute-done | bytes 65568 | tf_op jit(solution)/shard_map/ppermute | solution.py:219
  40.4 0.1 collective-permute-start.3
  40.5 0.1 pad_add_fusion.where
  40.6 2.9 %collective-permute-start.2 = (bf16[2,256,128]{2,1,0:T(8,128)(2,1)S(1)}, bf16[2,256,128]{2,1,0:T(8,128)(2,1)S(1)}, u32[]{:S(2)}, u32[]{:S(2)}) collective-permute-start(bf16[2,256,128]{2,1,0:T(8,128)(2,1)S(1)} %pad_maximum_fusion.refs_1_), channel_id=1, source_target_pairs={{0,8},{4,12},{8,0},{12,4},{16,24},{20,28},{24,16},{28,20},{1,9},{5... | collective-permute-start | bytes 393224 | tf_op jit(solution)/shard_map/ppermute | solution.py:224
  43.4 0.6 collective-permute-start.1
  44.0 0.0 collective-permute-start.4
  44.1 3.0 %collective-permute-done.3.refs_4_ = bf16[2,256,128]{2,1,0:T(8,128)(2,1)S(1)} collective-permute-done((bf16[2,256,128]{2,1,0:T(8,128)(2,1)S(1)}, bf16[2,256,128]{2,1,0:T(8,128)(2,1)S(1)}, u32[]{:S(2)}, u32[]{:S(2)}) %collective-permute-start.3) | collective-permute-done | bytes 131104 | tf_op jit(solution)/shard_map/ppermute | solution.py:224
  47.0 1.6 %collective-permute-done.2.refs_3_ = bf16[2,256,128]{2,1,0:T(8,128)(2,1)S(1)} collective-permute-done((bf16[2,256,128]{2,1,0:T(8,128)(2,1)S(1)}, bf16[2,256,128]{2,1,0:T(8,128)(2,1)S(1)}, u32[]{:S(2)}, u32[]{:S(2)}) %collective-permute-start.2) | collective-permute-done | bytes 131104 | tf_op jit(solution)/shard_map/ppermute | solution.py:224
  48.7 0.1 collective-permute-done.1.refs_2_
  48.8 0.1 collective-permute-start.5
  48.9 0.5 collective-permute-start.6
  49.4 0.1 collective-permute-start.7
  49.5 0.1 reshape.31.ids_ref
  49.6 0.1 reshape.32.w_ref
  49.7 0.0 collective-permute-done.4.refs_5_
  49.7 0.6 collective-permute-done.5.refs_6_
  50.2 0.2 collective-permute-done.6.refs_7_
  50.4 0.3 collective-permute-done.7.refs_8_
  50.7 0.0 all-to-all-done.refs_0_
  50.8 4.6 %shard_map.110 = bf16[2,8,2,2,2,32,128]{6,5,4,3,2,1,0:T(8,128)(2,1)S(1)} custom-call(s32[2]{0:T(128)S(1)} %pad_add_fusion.where, s32[8,2,8]{2,1,0:T(2,128)S(1)} %reshape.31.ids_ref, f32[8,2,8]{2,1,0:T(2,128)S(1)} %reshape.32.w_ref, bf16[8,2,272,128]{3,2,1,0:T(8,128)(2,1)S(1)} %all-to-all-done.refs_0_, bf16[2,256,128]{2,1,0:T(8,128)(2,1)S(1)} %pad_maximum_fusion.refs_1_, ...), custom_call_target="tpu_custom_call" | custom-call | flops 566231040 | bytes 4194304 | tf_op jit(solution)/shard_map/pallas_call | solution.py:242
  55.4 0.3 collective-permute-start.8
  56.3 0.0 copy-start.2
  56.3 0.0 copy-start.3
  56.3 0.0 copy-start.4
  56.3 0.0 copy-start.5
  56.3 1.0 %collective-permute-done.8 = bf16[8,2,2,2,32,128]{5,4,3,2,1,0:T(8,128)(2,1)S(1)} collective-permute-done((bf16[8,2,2,2,32,128]{5,4,3,2,1,0:T(8,128)(2,1)S(1)}, bf16[8,2,2,2,32,128]{5,4,3,2,1,0:T(8,128)(2,1)S(1)}, u32[]{:S(2)}, u32[]{:S(2)}) %collective-permute-start.8) | collective-permute-done | bytes 524320 | tf_op jit(solution)/shard_map/ppermute | solution.py:260
  57.3 1.0 %fusion = bf16[8,2,2,2,32,128]{5,4,3,2,1,0:T(8,128)(2,1)} fusion(bf16[8,2,2,2,32,128]{5,4,3,2,1,0:T(8,128)(2,1)S(1)} %collective-permute-done.8, bf16[2,8,2,2,2,32,128]{6,5,4,3,2,1,0:T(8,128)(2,1)S(1)} %shard_map.110), kind=kLoop, calls=%fused_computation.1 | loop fusion | flops 1048576 | bytes 1572864 | tf_op jit(solution)/shard_map/convert_element_type | solution.py:261
  58.3 5.6 %all-to-all-start.1 = ((bf16[16,2,2,32,128]{4,3,2,1,0:T(8,128)(2,1)}), bf16[16,2,2,32,128]{4,3,2,1,0:T(8,128)(2,1)S(1)}, u32[]{:S(2)}, u32[]{:S(2)}) async-start(bf16[16,2,2,32,128]{4,3,2,1,0:T(8,128)(2,1)} %bitcast.13), calls=%async_computation.1 | async-start | bytes 1048576 | tf_op jit(solution)/shard_map/all_to_all | solution.py:267
  64.0 0.0 copy-done.2
  64.0 0.1 constant_dynamic-slice_fusion
  64.1 0.1 copy.15
  64.2 0.0 copy-done.3
  64.2 0.1 constant_dynamic-slice_fusion.1
  64.2 0.0 copy-done.4
  64.2 0.2 fusion.5
  64.4 0.0 copy-done.5
  64.4 0.1 add_subtract_fusion
  64.5 0.9 %convert_multiply_fusion = f32[2,2,30,120]{3,2,1,0:T(8,128)S(1)} fusion(bf16[2,2,120,120]{3,2,1,0:T(8,128)(2,1)} %refs_1_.1, s32[]{:T(128)S(6)} %select_n.7, f32[2]{0:T(128)S(1)} %broadcast_multiply_fusion, f32[2,30,120]{2,1,0:T(8,128)S(1)} %add_subtract_fusion), kind=kLoop, calls=%fused_computation.8 | loop fusion | flops 43200 | bytes 115212 | tf_op jit(solution)/shard_map/mul | solution.py:291
  65.4 0.1 reshape.27
  65.5 13.9 %all-to-all-done.1 = bf16[16,2,2,32,128]{4,3,2,1,0:T(8,128)(2,1)S(1)} async-done(((bf16[16,2,2,32,128]{4,3,2,1,0:T(8,128)(2,1)}), bf16[16,2,2,32,128]{4,3,2,1,0:T(8,128)(2,1)S(1)}, u32[]{:S(2)}, u32[]{:S(2)}) %all-to-all-start.1) | async-done | bytes 524320 | tf_op jit(solution)/shard_map/all_to_all | solution.py:267
  79.4 0.1 convert_reduce_fusion
  79.5 0.1 reshape.30
  79.6 0.7 add_add_fusion
  (13 shorter events, 0.1 us)
Async XLA Ops:
  3.0 7.4 %copy-start = (bf16[256,128]{1,0:T(8,128)(2,1)S(1)}, bf16[256,128]{1,0:T(8,128)(2,1)}, u32[]{:S(2)}) copy-start(bf16[256,128]{1,0:T(8,128)(2,1)} %get-tuple-element.7) | copy-start | bytes 196612
  3.0 47.8 %all-to-all-start = ((bf16[8,2,272,128]{3,2,1,0:T(8,128)(2,1)}), bf16[8,2,272,128]{3,2,1,0:T(8,128)(2,1)S(1)}, u32[]{:S(2)}, u32[]{:S(2)}) async-start(bf16[8,2,272,128]{3,2,1,0:T(8,128)(2,1)} %get-tuple-element.8), calls=%async_computation | async-start | bytes 2228224 | tf_op jit(solution)/shard_map/all_to_all | solution.py:221
  10.4 30.0 %collective-permute-start = (bf16[256,128]{1,0:T(8,128)(2,1)S(1)}, bf16[256,128]{1,0:T(8,128)(2,1)S(1)}, u32[]{:S(2)}, u32[]{:S(2)}) collective-permute-start(bf16[256,128]{1,0:T(8,128)(2,1)S(1)} %copy-done), channel_id=1, source_target_pairs={{0,16},{4,20},{8,24},{12,28},{16,0},{20,4},{24,8},{28,12},{1,17},{... | collective-permute-start | bytes 196616 | tf_op jit(solution)/shard_map/ppermute | solution.py:219
  40.4 6.6 %collective-permute-start.3 = (bf16[2,256,128]{2,1,0:T(8,128)(2,1)S(1)}, bf16[2,256,128]{2,1,0:T(8,128)(2,1)S(1)}, u32[]{:S(2)}, u32[]{:S(2)}) collective-permute-start(bf16[2,256,128]{2,1,0:T(8,128)(2,1)S(1)} %pad_maximum_fusion.refs_1_), channel_id=1, source_target_pairs={{0,12},{4,8},{8,4},{12,0},{16,28},{20,24},{24,20},{28,16},{1,13},{... | collective-permute-start | bytes 393224 | tf_op jit(solution)/shard_map/ppermute | solution.py:224
  40.6 8.1 %collective-permute-start.2 = (bf16[2,256,128]{2,1,0:T(8,128)(2,1)S(1)}, bf16[2,256,128]{2,1,0:T(8,128)(2,1)S(1)}, u32[]{:S(2)}, u32[]{:S(2)}) collective-permute-start(bf16[2,256,128]{2,1,0:T(8,128)(2,1)S(1)} %pad_maximum_fusion.refs_1_), channel_id=1, source_target_pairs={{0,8},{4,12},{8,0},{12,4},{16,24},{20,28},{24,16},{28,20},{1,9},{5... | collective-permute-start | bytes 393224 | tf_op jit(solution)/shard_map/ppermute | solution.py:224
  43.4 5.4 %collective-permute-start.1 = (bf16[2,256,128]{2,1,0:T(8,128)(2,1)S(1)}, bf16[2,256,128]{2,1,0:T(8,128)(2,1)S(1)}, u32[]{:S(2)}, u32[]{:S(2)}) collective-permute-start(bf16[2,256,128]{2,1,0:T(8,128)(2,1)S(1)} %pad_maximum_fusion.refs_1_), channel_id=1, source_target_pairs={{0,4},{4,0},{8,12},{12,8},{16,20},{20,16},{24,28},{28,24},{1,5},{5... | collective-permute-start | bytes 393224 | tf_op jit(solution)/shard_map/ppermute | solution.py:224
  44.0 5.6 %collective-permute-start.4 = (bf16[2,256,128]{2,1,0:T(8,128)(2,1)S(1)}, bf16[2,256,128]{2,1,0:T(8,128)(2,1)S(1)}, u32[]{:S(2)}, u32[]{:S(2)}) collective-permute-start(bf16[2,256,128]{2,1,0:T(8,128)(2,1)S(1)} %pad_maximum_fusion.refs_1_), channel_id=1, source_target_pairs={{0,1},{1,0},{2,3},{3,2},{4,5},{5,4},{6,7},{7,6},{8,9},{9,8},{10,11... | collective-permute-start | bytes 393224 | tf_op jit(solution)/shard_map/ppermute | solution.py:238
  48.8 1.4 %collective-permute-start.5 = (bf16[2,256,128]{2,1,0:T(8,128)(2,1)S(1)}, bf16[2,256,128]{2,1,0:T(8,128)(2,1)S(1)}, u32[]{:S(2)}, u32[]{:S(2)}) collective-permute-start(bf16[2,256,128]{2,1,0:T(8,128)(2,1)S(1)} %collective-permute-done.1.refs_2_), channel_id=1, source_target_pairs={{0,1},{1,0},{2,3},{3,2},{4,5},{5,4},{6,7},{7,6},{8,9},{9,8},{10,11... | collective-permute-start | bytes 393224 | tf_op jit(solution)/shard_map/ppermute | solution.py:238
  48.9 1.5 %collective-permute-start.6 = (bf16[2,256,128]{2,1,0:T(8,128)(2,1)S(1)}, bf16[2,256,128]{2,1,0:T(8,128)(2,1)S(1)}, u32[]{:S(2)}, u32[]{:S(2)}) collective-permute-start(bf16[2,256,128]{2,1,0:T(8,128)(2,1)S(1)} %collective-permute-done.2.refs_3_), channel_id=1, source_target_pairs={{0,1},{1,0},{2,3},{3,2},{4,5},{5,4},{6,7},{7,6},{8,9},{9,8},{10,11... | collective-permute-start | bytes 393224 | tf_op jit(solution)/shard_map/ppermute | solution.py:238
  49.4 1.3 %collective-permute-start.7 = (bf16[2,256,128]{2,1,0:T(8,128)(2,1)S(1)}, bf16[2,256,128]{2,1,0:T(8,128)(2,1)S(1)}, u32[]{:S(2)}, u32[]{:S(2)}) collective-permute-start(bf16[2,256,128]{2,1,0:T(8,128)(2,1)S(1)} %collective-permute-done.3.refs_4_), channel_id=1, source_target_pairs={{0,1},{1,0},{2,3},{3,2},{4,5},{5,4},{6,7},{7,6},{8,9},{9,8},{10,11... | collective-permute-start | bytes 393224 | tf_op jit(solution)/shard_map/ppermute | solution.py:238
  55.4 2.0 %collective-permute-start.8 = (bf16[8,2,2,2,32,128]{5,4,3,2,1,0:T(8,128)(2,1)S(1)}, bf16[8,2,2,2,32,128]{5,4,3,2,1,0:T(8,128)(2,1)S(1)}, u32[]{:S(2)}, u32[]{:S(2)}) collective-permute-start(bf16[8,2,2,2,32,128]{5,4,3,2,1,0:T(8,128)(2,1)S(1)} %slice_bitcast_fusion), channel_id=1, source_target_pairs={{0,1},{1,0},{2,3},{3,2},{4,5},{5,4},{6,7},{7,6},{8,9},{9,8},{10,11... | collective-permute-start | bytes 1572872 | tf_op jit(solution)/shard_map/ppermute | solution.py:260
  56.3 7.7 %copy-start.2 = (s32[16,2]{0,1:T(2,128)S(1)}, s32[16,2]{0,1:T(2,128)}, u32[]{:S(2)}) copy-start(s32[16,2]{0,1:T(2,128)} %param.17) | copy-start | bytes 388
  56.3 7.9 %copy-start.3 = (f32[2,120]{1,0:T(2,128)S(1)}, f32[2,120]{1,0:T(2,128)}, u32[]{:S(2)}) copy-start(f32[2,120]{1,0:T(2,128)} %param.14) | copy-start | bytes 2884
  56.3 7.9 %copy-start.4 = (f32[32]{0:T(128)S(1)}, f32[32]{0:T(128)}, u32[]{:S(2)}) copy-start(f32[32]{0:T(128)} %param.15) | copy-start | bytes 388
  56.3 8.1 %copy-start.5 = (f32[2]{0:T(128)S(1)}, f32[2]{0:T(128)}, u32[]{:S(2)}) copy-start(f32[2]{0:T(128)} %constant.24.clone) | copy-start | bytes 28
  58.3 21.3 %copy-start.1 = (f32[2,2,3600]{2,1,0:T(2,128)S(1)}, f32[2,2,3600]{2,1,0:T(2,128)}, u32[]{:S(2)}) copy-start(f32[2,2,3600]{2,1,0:T(2,128)} %param.13) | copy-start | bytes 172804
  58.3 21.1 %all-to-all-start.1 = ((bf16[16,2,2,32,128]{4,3,2,1,0:T(8,128)(2,1)}), bf16[16,2,2,32,128]{4,3,2,1,0:T(8,128)(2,1)S(1)}, u32[]{:S(2)}, u32[]{:S(2)}) async-start(bf16[16,2,2,32,128]{4,3,2,1,0:T(8,128)(2,1)} %bitcast.13), calls=%async_computation.1 | async-start | bytes 1048576 | tf_op jit(solution)/shard_map/all_to_all | solution.py:267

commit v3 on v2

--- a/solution.py
+++ b/solution.py
@@ -9,6 +9,7 @@
 
 
 LANES = 128
+GROUP = 16
 BF = jnp.bfloat16
 F32 = jnp.float32
 
@@ -21,20 +22,20 @@
     return [(i, i ^ bits) for i in range(count)]
 
 
-def member(aux, sides):
-    return (aux // 2 % 2 if sides[1] == 2 else 0, aux % 2 if sides[0] == 2 else 0)
-
-
 def prep_kernel(n_pair, sides, *refs):
-    inputs, chunks, share_ref = refs[:6], refs[6], refs[7]
-    buffers, (turned, sems) = refs[8:14], refs[14:]
+    inputs, chunks_out, share_out = refs[:6], refs[6], refs[7]
+    buffers, (chunks, share_ref, turned, sems, panel_sems, out_sems) = refs[8:14], refs[14:]
+    panels, amps, lmo, near, ranks, fock = buffers
     copies = [
         pltpu.make_async_copy(src, dst, sems.at[i])
-        for i, (src, dst) in enumerate(zip(inputs, buffers))
+        for i, (src, dst) in enumerate(zip(inputs[1:], buffers[1:]))
     ]
-    for copy in copies:
+    panel_copies = [
+        pltpu.make_async_copy(inputs[0].at[lp], panels.at[lp], panel_sems.at[lp])
+        for lp in range(panels.shape[0])
+    ]
+    for copy in copies + panel_copies:
         copy.start()
-    panels, amps, lmo, near, ranks, fock = buffers
     local, rank, width = panels.shape
     part = width // n_pair
     wide = part // LANES
@@ -42,7 +43,7 @@
     me = lax.axis_index("pair")
     aux = lax.axis_index("aux")
     slots = near.shape[1]
-    for copy in copies[2:]:
+    for copy in copies[1:]:
         copy.wait()
 
     share_rows = share_ref.shape[0]
@@ -67,18 +68,20 @@
     share_ref[share_rows - 16 :, :] = tail.astype(BF)
 
     freqs = amps.shape[1]
-    many, take = local // sides[1], freqs // sides[0]
-    lp_first, s_first = member(aux, sides)
-    copies[1].wait()
-    for i in range(many):
+    take = freqs // sides
+    s_first = aux % 2 if sides == 2 else 0
+    copies[0].wait()
+    for i in range(local):
         for j in range(take):
-            a = amps[lp_first * many + i, s_first * take + j].astype(F32)
+            a = amps[i, s_first * take + j].astype(F32)
             a = jnp.concatenate([a, jnp.zeros((rank, LANES - rank), F32)], axis=1)
             first = (i * take + j) * rank
             share_ref[first : first + rank, :] = a.astype(BF)
 
-    copies[0].wait()
+    sends = [pltpu.make_async_copy(share_ref, share_out, out_sems.at[local])]
+    sends[0].start()
     for lp in range(local):
+        panel_copies[lp].wait()
         keep = lax.broadcasted_iota(jnp.int32, (rank, LANES), 0) < ranks[lp]
         for k in range(n_pair):
             for w in range(wide):
@@ -91,74 +94,97 @@
                 x = panels[lp, :, start : start + LANES].astype(F32)
                 x = jnp.where(keep, x, 0.0)
                 x = jnp.concatenate([x, jnp.zeros((LANES - rank, LANES), F32)], axis=0)
-                turned[t * LANES : (t + 1) * LANES, :] = x.T.astype(BF)
+                turned[lp, t * LANES : (t + 1) * LANES, :] = x.T.astype(BF)
             for k in range(n_pair):
                 start = pl.multiple_of((me ^ k) * rest, 16)
-                chunks[me ^ k, lp, wide * rank :, :] = turned[pl.ds(start, rest), :]
-
-
-def couple_kernel(n_pair, blocks, sides, shape, where, ids_ref, w_ref, *refs):
+                chunks[me ^ k, lp, wide * rank :, :] = turned[lp, pl.ds(start, rest), :]
+        send = pltpu.make_async_copy(chunks.at[:, lp], chunks_out.at[:, lp], out_sems.at[lp])
+        send.start()
+        sends.append(send)
+    for send in sends:
+        send.wait()
+
+
+def mix_kernel(local, where, ids_ref, w_ref, out_ref):
+    n_pair, slots = ids_ref.shape[0], ids_ref.shape[2]
+    me = where[0]
+    side = out_ref.shape[1]
+    group = lax.broadcasted_iota(jnp.int32, (GROUP, side), 1) // GROUP
+    inner = lax.broadcasted_iota(jnp.int32, (GROUP, side), 1) % GROUP
+    diagonal = lax.broadcasted_iota(jnp.int32, (GROUP, side), 0) == inner
+    for k in range(n_pair):
+        for lp in range(local):
+            acc = jnp.zeros((GROUP, side), F32)
+            for j in range(slots):
+                i = ids_ref[k, lp, j]
+                source = ((i // local) ^ me) * local + i % local
+                acc = acc + jnp.where(group == source, w_ref[k, lp, j], 0.0)
+            first = (k * local + lp) * GROUP
+            out_ref[first : first + GROUP, :] = jnp.where(diagonal, acc, 0.0).astype(BF)
+
+
+def couple_kernel(n_pair, blocks, sides, shape, where, panels, mix_ref, *refs):
     half = n_pair // 2
-    members = sides[0] * sides[1]
-    panels, mats = refs[0], refs[1 : 1 + half * members]
-    out_ref, proj, mixed, mat = refs[1 + half * members :]
+    mats = refs[: half * sides]
+    out_ref, proj, mixed, mat = refs[half * sides :]
     local, rank, part, freqs = shape
+    total = n_pair * local
     wide = part // LANES
     rest = part - wide * LANES
     rows = rank // blocks
-    slots = ids_ref.shape[2]
+    lanes = freqs * LANES
     me, aux = where[0], where[1]
-    many, take = local // sides[1], freqs // sides[0]
-    order = list(range(n_pair))
-
-    for k in order:
-        for pair_slot in range(sides[1]):
-            for i in range(many):
-                lp = member(aux ^ (pair_slot * 2), sides)[0] * many + i
-                for s in range(freqs):
-                    slot, inner = s // take, s % take
-                    first = (i * take + inner) * rank
-                    piece = mats[(pair_slot * sides[0] + slot) * half + k % half]
-                    mat[:, s * LANES : (s + 1) * LANES] = piece[k // half, first : first + rank, :]
-                index = k * local + lp
-                for w in range(wide):
-                    proj[index, w * LANES : (w + 1) * LANES, :] = lax.dot_general(
-                        panels[me ^ k, lp, w * rank : (w + 1) * rank, :],
-                        mat[...],
-                        (((0,), (0,)), ((), ())),
-                        preferred_element_type=F32,
-                    )
-                if rest:
-                    proj[index, wide * LANES :, :] = jnp.dot(
-                        panels[me ^ k, lp, wide * rank :, :][:, :rank],
-                        mat[...],
-                        preferred_element_type=F32,
-                    )
-
-    tile = 32 if part % 32 == 0 else 16
-    for k in order:
+    take = freqs // sides
+
+    def keep(first, index, value):
+        count = value.shape[0] // GROUP
+        proj[first // GROUP : first // GROUP + count, index] = value.astype(BF).reshape(
+            count, GROUP, lanes
+        )
+
+    for k in range(n_pair):
         for lp in range(local):
-            source = []
-            for j in range(slots):
-                i = ids_ref[k, lp, j]
-                source.append(((i // local) ^ me) * local + i % local)
-            scale = [w_ref[k, lp, j] for j in range(slots)]
-            for t in range(part // tile):
-                span = slice(t * tile, (t + 1) * tile)
-                acc = scale[0] * proj[source[0], span, :]
-                for j in range(1, slots):
-                    acc = acc + scale[j] * proj[source[j], span, :]
-                mixed[span, :] = acc.astype(BF)
+            index = k * local + lp
+            for s in range(freqs):
+                slot, inner = s // take, s % take
+                first = (lp * take + inner) * rank
+                piece = mats[slot * half + k % half].at[k // half]
+                mat[index, :, s * LANES : (s + 1) * LANES] = piece[first : first + rank, :]
+            for w in range(wide):
+                found = lax.dot_general(
+                    panels[me ^ k, lp, w * rank : (w + 1) * rank, :],
+                    mat[index],
+                    (((0,), (0,)), ((), ())),
+                    preferred_element_type=F32,
+                )
+                keep(w * LANES, index, found)
+            if rest:
+                found = jnp.dot(
+                    panels[me ^ k, lp, wide * rank :, :][:, :rank],
+                    mat[index],
+                    preferred_element_type=F32,
+                )
+                keep(wide * LANES, index, found)
+
+    for g in range(part // GROUP):
+        found = jnp.dot(
+            mix_ref[...], proj[g].reshape(total * GROUP, lanes), preferred_element_type=F32
+        )
+        mixed[:, g * GROUP : (g + 1) * GROUP, :] = found.astype(BF).reshape(total, GROUP, lanes)
+
+    for k in range(n_pair):
+        for lp in range(local):
+            index = k * local + lp
             got = None
             if wide:
                 x = jnp.concatenate(
                     [panels[me ^ k, lp, w * rank : (w + 1) * rank, :] for w in range(wide)], axis=1
                 )
-                got = jnp.dot(x, mixed[: wide * LANES, :], preferred_element_type=F32)
+                got = jnp.dot(x, mixed[index, : wide * LANES, :], preferred_element_type=F32)
             if rest:
                 more = lax.dot_general(
                     panels[me ^ k, lp, wide * rank :, :],
-                    mixed[wide * LANES :, :],
+                    mixed[index, wide * LANES :, :],
                     (((0,), (0,)), ((), ())),
                     preferred_element_type=F32,
                 )[:rank]
@@ -166,7 +192,7 @@
             for h in range(blocks):
                 side = aux % 2 ^ (h % 2) if blocks > 1 else 0
                 for s in range(freqs):
-                    freq = member(aux ^ (s // take), sides)[1] * take + s % take
+                    freq = (s // take ^ (aux % 2)) * take + s % take if sides == 2 else s
                     out_ref[side, me ^ k, h // 2, lp, freq, :rows, :] = got[
                         h * rows : (h + 1) * rows, s * LANES : (s + 1) * LANES
                     ].astype(out_ref.dtype)
@@ -189,15 +215,12 @@
     wide = part // LANES
     rest = part - wide * LANES
     chunk_rows = wide * rank + rest
-    sides = (
-        2 if n_aux % 2 == 0 and freqs % 2 == 0 else 1,
-        1,
-    )
+    sides = 2 if n_aux % 2 == 0 and freqs % 2 == 0 else 1
     where = jnp.stack([me_pair, me_aux]).astype(jnp.int32)
     vmem = pl.BlockSpec(memory_space=pltpu.VMEM)
     smem = pl.BlockSpec(memory_space=pltpu.SMEM)
 
-    share_rows = (local // sides[1]) * (freqs // sides[0]) * rank + 16
+    share_rows = local * (freqs // sides) * rank + 16
     given = (panels, amplitudes, pair_lmo.T, neighbours, pno_ranks, fock_off)
     spaces = [pltpu.VMEM] * 2 + [pltpu.SMEM] * 4
     outs = pl.pallas_call(
@@ -205,11 +228,15 @@
         out_shape=[jax.ShapeDtypeStruct((n_pair, local, chunk_rows, LANES), BF)]
         + [jax.ShapeDtypeStruct((share_rows, LANES), BF)],
         in_specs=[pl.BlockSpec(memory_space=pltpu.HBM)] * 6,
-        out_specs=[vmem] * 2,
+        out_specs=[pl.BlockSpec(memory_space=pltpu.HBM)] * 2,
         scratch_shapes=[space(a.shape, a.dtype) for space, a in zip(spaces, given)]
         + [
-            pltpu.VMEM((max(n_pair * rest, 16), LANES), BF),
-            pltpu.SemaphoreType.DMA((6,)),
+            pltpu.VMEM((n_pair, local, chunk_rows, LANES), BF),
+            pltpu.VMEM((share_rows, LANES), BF),
+            pltpu.VMEM((local, max(n_pair * rest, 16), LANES), BF),
+            pltpu.SemaphoreType.DMA((5,)),
+            pltpu.SemaphoreType.DMA((local,)),
+            pltpu.SemaphoreType.DMA((local + 1,)),
         ],
         cost_estimate=pl.CostEstimate(flops=0, bytes_accessed=4 * 2**20, transcendentals=0),
     )(*given)
@@ -226,16 +253,17 @@
     tail = tail.reshape(n_pair, 16, LANES)
     ids = tail[:, 0, : local * slots].reshape(n_pair, local, slots).astype(jnp.int32)
     scale = tail[:, 1, : local * slots].reshape(n_pair, local, slots).astype(F32)
-    if sides[1] == 2:
+    if sides == 2:
         for k in range(far):
-            pieces.append(lax.ppermute(pieces[k], "aux", flip(n_aux, 2)))
-    if sides[0] == 2:
-        held, pieces = pieces, []
-        for slot in range(sides[1]):
-            block = held[slot * far : (slot + 1) * far]
-            pieces += block
-            for k in range(far):
-                pieces.append(lax.ppermute(block[k], "aux", flip(n_aux, 1)))
+            pieces.append(lax.ppermute(pieces[k], "aux", flip(n_aux, 1)))
+    mix = pl.pallas_call(
+        functools.partial(mix_kernel, local),
+        out_shape=jax.ShapeDtypeStruct((total * GROUP, total * GROUP), BF),
+        in_specs=[smem] * 3,
+        out_specs=vmem,
+        compiler_params=pltpu.CompilerParams(vmem_limit_bytes=8 * 2**20),
+        cost_estimate=pl.CostEstimate(flops=10**6, bytes_accessed=2**17, transcendentals=0),
+    )(where, ids, scale)
 
     out_dims = (2 if even else 1, n_pair, max(blocks // 2, 1), local, freqs, rows_pad, LANES)
     flops = 4 * total * part * rank * freqs * LANES
@@ -244,17 +272,16 @@
             couple_kernel, n_pair, blocks, sides, (local, rank, part, freqs)
         ),
         out_shape=jax.ShapeDtypeStruct(out_dims, BF if even else F32),
-        in_specs=[smem] * 3
-        + [vmem] * (1 + far * sides[0] * sides[1]),
+        in_specs=[smem] + [vmem] * (2 + far * sides),
         out_specs=vmem,
         scratch_shapes=[
-            pltpu.VMEM((total, part, freqs * LANES), F32),
-            pltpu.VMEM((part, freqs * LANES), BF),
-            pltpu.VMEM((rank, freqs * LANES), BF),
+            pltpu.VMEM((part // GROUP, total, GROUP, freqs * LANES), BF),
+            pltpu.VMEM((total, part, freqs * LANES), BF),
+            pltpu.VMEM((total, rank, freqs * LANES), BF),
         ],
         compiler_params=pltpu.CompilerParams(vmem_limit_bytes=40 * 2**20),
         cost_estimate=pl.CostEstimate(flops=flops, bytes_accessed=4 * 2**20, transcendentals=0),
-    )(where, ids, scale, received, *pieces)
+    )(where, received, mix, *pieces)
 
     if even:
         other = lax.ppermute(coupled[1], "aux", flip(n_aux, 1))

time: 80.7 us -> 79.7 us (0.988)
  waiting for transfers between devices: 47.8 us -> 46.6 us
    pallas_call x1, Pallas kernels: 4.56 us -> 2.88 us  [body(): pl.pallas_call(functools.partial(couple_kernel, n_pair, blocks, sides, (l...]
    pallas_call x0 -> x1, Pallas kernels: none -> 1.63 us  [body(): pl.pallas_call(functools.partial(mix_kernel, local), out_shape=jax.ShapeD...]
    ppermute x4, waiting for transfers between devices: 1.07 us -> 0.01 us  [body(): pieces.append(lax.ppermute(pieces[k], 'aux', flip(n_aux, 1)))]
  transfers between devices with their start and end apart: 11 -> 11, of which waited for: 9 -> 6; matrix products, arithmetic and copies ran while one was open for 2% -> 2% of each run, Pallas kernels for 0% -> 2%
where the time goes in v3:
time: 79.7 us; the launch traced here: 79.3 us
  waiting for transfers between devices  46.6 us (58%)
  starting transfers between devices  20.7 us (26%)
  Pallas kernels  7.4 us (9%)
  other arithmetic  3 us (4%)
  between operations  0.85 us (1%)
    ppermute x1, waiting for transfers between devices, body(): other = lax.ppermute(share, 'pair', flip(n_pair, far))  27.1 us
    all_to_all x1, waiting for transfers between devices, body(): lax.all_to_all(mine, ('pair', 'aux'), 0, 0, axis_index_groups=groups, til...  14 us
    all_to_all x1, starting transfers between devices, body(): received = lax.all_to_all(chunks, 'pair', 0, 0, tiled=True)  7.43 us
    all_to_all x1, starting transfers between devices, body(): lax.all_to_all(mine, ('pair', 'aux'), 0, 0, axis_index_groups=groups, til...  5.64 us
    ppermute x3, waiting for transfers between devices, body(): pieces[k] = lax.ppermute(pieces[0], 'pair', flip(n_pair, k))  4.74 us
    ppermute x3, starting transfers between devices, body(): pieces[k] = lax.ppermute(pieces[0], 'pair', flip(n_pair, k))  3.54 us
    ppermute x1, starting transfers between devices, body(): other = lax.ppermute(share, 'pair', flip(n_pair, far))  2.92 us
    pallas_call x1, Pallas kernels, body(): pl.pallas_call(functools.partial(prep_kernel, n_pair, sides), out_shape=[...  2.89 us
  transfers between devices with their start and end apart: 11, of which 6 were waited for; matrix products, arithmetic and copies ran while one was open for 2% of the time, Pallas kernels for 2%

profile of v3, /device:TPU:0, one launch (start us, length us, event | category | flops | bytes accessed | tf_op | source)
XLA Modules:
  0.0 79.3 jit_solution(831362306205724562)
XLA Ops:
  0.0 2.9 %shard_map.109 = (bf16[8,2,272,128]{3,2,1,0:T(8,128)(2,1)}, bf16[256,128]{1,0:T(8,128)(2,1)}) custom-call(bf16[2,120,2304]{2,1,0:T(8,128)(2,1)} %refs_0_.1, bf16[2,2,120,120]{3,2,1,0:T(8,128)(2,1)} %refs_1_.1, s32[2,16]{1,0:T(2,128)} %bitcast.32, s32[2,8]{1,0:T(2,128)} %refs_3_.1, s32[2]{0:T(128)} %refs_4_.1, f32[32,32]{1,0:T(8,128)} %refs_5_.1), custom_call_target="tpu_custom_call" | custom-call | bytes 4194304 | tf_op jit(solution)/shard_map/pallas_call | solution.py:226
  2.9 0.0 copy-start
  2.9 7.4 %all-to-all-start = ((bf16[8,2,272,128]{3,2,1,0:T(8,128)(2,1)}), bf16[8,2,272,128]{3,2,1,0:T(8,128)(2,1)S(1)}, u32[]{:S(2)}, u32[]{:S(2)}) async-start(bf16[8,2,272,128]{3,2,1,0:T(8,128)(2,1)} %get-tuple-element.7), calls=%async_computation | async-start | bytes 2228224 | tf_op jit(solution)/shard_map/all_to_all | solution.py:248
  10.3 2.9 %collective-permute-start = (bf16[256,128]{1,0:T(8,128)(2,1)S(1)}, bf16[256,128]{1,0:T(8,128)(2,1)S(1)}, u32[]{:S(2)}, u32[]{:S(2)}) collective-permute-start(bf16[256,128]{1,0:T(8,128)(2,1)S(1)} %copy-done), channel_id=1, source_target_pairs={{0,16},{4,20},{8,24},{12,28},{16,0},{20,4},{24,8},{28,12},{1,17},{... | collective-permute-start | bytes 196616 | tf_op jit(solution)/shard_map/ppermute | solution.py:246
  13.3 27.1 %collective-permute-done = bf16[256,128]{1,0:T(8,128)(2,1)S(1)} collective-permute-done((bf16[256,128]{1,0:T(8,128)(2,1)S(1)}, bf16[256,128]{1,0:T(8,128)(2,1)S(1)}, u32[]{:S(2)}, u32[]{:S(2)}) %collective-permute-start) | collective-permute-done | bytes 65568 | tf_op jit(solution)/shard_map/ppermute | solution.py:246
  40.3 0.1 collective-permute-start.3
  40.4 0.1 pad_add_fusion.where
  40.5 2.9 %collective-permute-start.2 = (bf16[2,256,128]{2,1,0:T(8,128)(2,1)S(1)}, bf16[2,256,128]{2,1,0:T(8,128)(2,1)S(1)}, u32[]{:S(2)}, u32[]{:S(2)}) collective-permute-start(bf16[2,256,128]{2,1,0:T(8,128)(2,1)S(1)} %pad_maximum_fusion.refs_0_), channel_id=1, source_target_pairs={{0,8},{4,12},{8,0},{12,4},{16,24},{20,28},{24,16},{28,20},{1,9},{5... | collective-permute-start | bytes 393224 | tf_op jit(solution)/shard_map/ppermute | solution.py:251
  43.4 0.6 collective-permute-start.1
  44.0 0.0 collective-permute-start.4
  44.0 3.0 %collective-permute-done.3.refs_3_ = bf16[2,256,128]{2,1,0:T(8,128)(2,1)S(1)} collective-permute-done((bf16[2,256,128]{2,1,0:T(8,128)(2,1)S(1)}, bf16[2,256,128]{2,1,0:T(8,128)(2,1)S(1)}, u32[]{:S(2)}, u32[]{:S(2)}) %collective-permute-start.3) | collective-permute-done | bytes 131104 | tf_op jit(solution)/shard_map/ppermute | solution.py:251
  47.0 1.6 %collective-permute-done.2.refs_2_ = bf16[2,256,128]{2,1,0:T(8,128)(2,1)S(1)} collective-permute-done((bf16[2,256,128]{2,1,0:T(8,128)(2,1)S(1)}, bf16[2,256,128]{2,1,0:T(8,128)(2,1)S(1)}, u32[]{:S(2)}, u32[]{:S(2)}) %collective-permute-start.2) | collective-permute-done | bytes 131104 | tf_op jit(solution)/shard_map/ppermute | solution.py:251
  48.6 0.1 collective-permute-done.1.refs_1_
  48.7 0.1 collective-permute-start.5
  48.8 0.5 collective-permute-start.6
  49.3 0.1 collective-permute-start.7
  49.4 0.1 reshape.31.ids_ref
  49.5 0.1 reshape.32.w_ref
  49.6 1.6 %shard_map.110.mix_ref = bf16[256,256]{1,0:T(8,128)(2,1)S(1)} custom-call(s32[2]{0:T(128)S(1)} %pad_add_fusion.where, s32[8,2,8]{2,1,0:T(2,128)S(1)} %reshape.31.ids_ref, f32[8,2,8]{2,1,0:T(2,128)S(1)} %reshape.32.w_ref), custom_call_target="tpu_custom_call" | custom-call | flops 1000000 | bytes 131072 | tf_op jit(solution)/shard_map/pallas_call | solution.py:259
  51.2 0.0 collective-permute-done.4.refs_4_
  51.2 0.0 collective-permute-done.5.refs_5_
  51.3 0.0 collective-permute-done.6.refs_6_
  51.3 0.0 collective-permute-done.7.refs_7_
  51.3 0.0 all-to-all-done.panels
  51.3 2.9 %shard_map.111 = bf16[2,8,2,2,2,32,128]{6,5,4,3,2,1,0:T(8,128)(2,1)S(1)} custom-call(s32[2]{0:T(128)S(1)} %pad_add_fusion.where, bf16[8,2,272,128]{3,2,1,0:T(8,128)(2,1)S(1)} %all-to-all-done.panels, bf16[256,256]{1,0:T(8,128)(2,1)S(1)} %shard_map.110.mix_ref, bf16[2,256,128]{2,1,0:T(8,128)(2,1)S(1)} %pad_maximum_fusion.refs_0_, ...), custom_call_target="tpu_custom_call" | custom-call | flops 566231040 | bytes 4194304 | tf_op jit(solution)/shard_map/pallas_call | solution.py:270
  54.2 0.5 collective-permute-start.8
  55.4 0.0 copy-start.2
  55.4 0.0 copy-start.3
  55.4 0.0 copy-start.4
  55.4 0.0 copy-start.5
  55.4 0.8 %collective-permute-done.8 = bf16[8,2,2,2,32,128]{5,4,3,2,1,0:T(8,128)(2,1)S(1)} collective-permute-done((bf16[8,2,2,2,32,128]{5,4,3,2,1,0:T(8,128)(2,1)S(1)}, bf16[8,2,2,2,32,128]{5,4,3,2,1,0:T(8,128)(2,1)S(1)}, u32[]{:S(2)}, u32[]{:S(2)}) %collective-permute-start.8) | collective-permute-done | bytes 524320 | tf_op jit(solution)/shard_map/ppermute | solution.py:287
  56.3 1.0 %fusion = bf16[8,2,2,2,32,128]{5,4,3,2,1,0:T(8,128)(2,1)} fusion(bf16[8,2,2,2,32,128]{5,4,3,2,1,0:T(8,128)(2,1)S(1)} %collective-permute-done.8, bf16[2,8,2,2,2,32,128]{6,5,4,3,2,1,0:T(8,128)(2,1)S(1)} %shard_map.111), kind=kLoop, calls=%fused_computation.1 | loop fusion | flops 1048576 | bytes 1572864 | tf_op jit(solution)/shard_map/convert_element_type | solution.py:288
  57.3 5.6 %all-to-all-start.1 = ((bf16[16,2,2,32,128]{4,3,2,1,0:T(8,128)(2,1)}), bf16[16,2,2,32,128]{4,3,2,1,0:T(8,128)(2,1)S(1)}, u32[]{:S(2)}, u32[]{:S(2)}) async-start(bf16[16,2,2,32,128]{4,3,2,1,0:T(8,128)(2,1)} %bitcast.13), calls=%async_computation.1 | async-start | bytes 1048576 | tf_op jit(solution)/shard_map/all_to_all | solution.py:294
  62.9 0.0 copy-done.2
  62.9 0.1 constant_dynamic-slice_fusion
  63.0 0.1 copy.15
  63.1 0.0 copy-done.3
  63.1 0.1 constant_dynamic-slice_fusion.1
  63.2 0.2 fusion.5
  63.3 0.0 copy-done.5
  63.3 0.1 add_subtract_fusion
  63.4 0.9 %convert_multiply_fusion = f32[2,2,30,120]{3,2,1,0:T(8,128)S(1)} fusion(bf16[2,2,120,120]{3,2,1,0:T(8,128)(2,1)} %refs_1_.1, s32[]{:T(128)S(6)} %select_n.7, f32[2]{0:T(128)S(1)} %broadcast_multiply_fusion, f32[2,30,120]{2,1,0:T(8,128)S(1)} %add_subtract_fusion), kind=kLoop, calls=%fused_computation.8 | loop fusion | flops 43200 | bytes 115212 | tf_op jit(solution)/shard_map/mul | solution.py:318
  64.3 0.1 reshape.27
  64.4 14.0 %all-to-all-done.1 = bf16[16,2,2,32,128]{4,3,2,1,0:T(8,128)(2,1)S(1)} async-done(((bf16[16,2,2,32,128]{4,3,2,1,0:T(8,128)(2,1)}), bf16[16,2,2,32,128]{4,3,2,1,0:T(8,128)(2,1)S(1)}, u32[]{:S(2)}, u32[]{:S(2)}) %all-to-all-start.1) | async-done | bytes 524320 | tf_op jit(solution)/shard_map/all_to_all | solution.py:294
  78.4 0.1 convert_reduce_fusion
  78.5 0.1 reshape.30
  78.6 0.0 copy-done.1
  78.6 0.7 add_add_fusion
  (14 shorter events, 0.1 us)
Async XLA Ops:
  2.9 7.4 %copy-start = (bf16[256,128]{1,0:T(8,128)(2,1)S(1)}, bf16[256,128]{1,0:T(8,128)(2,1)}, u32[]{:S(2)}) copy-start(bf16[256,128]{1,0:T(8,128)(2,1)} %get-tuple-element.8) | copy-start | bytes 196612
  2.9 48.4 %all-to-all-start = ((bf16[8,2,272,128]{3,2,1,0:T(8,128)(2,1)}), bf16[8,2,272,128]{3,2,1,0:T(8,128)(2,1)S(1)}, u32[]{:S(2)}, u32[]{:S(2)}) async-start(bf16[8,2,272,128]{3,2,1,0:T(8,128)(2,1)} %get-tuple-element.7), calls=%async_computation | async-start | bytes 2228224 | tf_op jit(solution)/shard_map/all_to_all | solution.py:248
  10.3 30.0 %collective-permute-start = (bf16[256,128]{1,0:T(8,128)(2,1)S(1)}, bf16[256,128]{1,0:T(8,128)(2,1)S(1)}, u32[]{:S(2)}, u32[]{:S(2)}) collective-permute-start(bf16[256,128]{1,0:T(8,128)(2,1)S(1)} %copy-done), channel_id=1, source_target_pairs={{0,16},{4,20},{8,24},{12,28},{16,0},{20,4},{24,8},{28,12},{1,17},{... | collective-permute-start | bytes 196616 | tf_op jit(solution)/shard_map/ppermute | solution.py:246
  40.3 6.6 %collective-permute-start.3 = (bf16[2,256,128]{2,1,0:T(8,128)(2,1)S(1)}, bf16[2,256,128]{2,1,0:T(8,128)(2,1)S(1)}, u32[]{:S(2)}, u32[]{:S(2)}) collective-permute-start(bf16[2,256,128]{2,1,0:T(8,128)(2,1)S(1)} %pad_maximum_fusion.refs_0_), channel_id=1, source_target_pairs={{0,12},{4,8},{8,4},{12,0},{16,28},{20,24},{24,20},{28,16},{1,13},{... | collective-permute-start | bytes 393224 | tf_op jit(solution)/shard_map/ppermute | solution.py:251
  40.5 8.1 %collective-permute-start.2 = (bf16[2,256,128]{2,1,0:T(8,128)(2,1)S(1)}, bf16[2,256,128]{2,1,0:T(8,128)(2,1)S(1)}, u32[]{:S(2)}, u32[]{:S(2)}) collective-permute-start(bf16[2,256,128]{2,1,0:T(8,128)(2,1)S(1)} %pad_maximum_fusion.refs_0_), channel_id=1, source_target_pairs={{0,8},{4,12},{8,0},{12,4},{16,24},{20,28},{24,16},{28,20},{1,9},{5... | collective-permute-start | bytes 393224 | tf_op jit(solution)/shard_map/ppermute | solution.py:251
  43.4 5.4 %collective-permute-start.1 = (bf16[2,256,128]{2,1,0:T(8,128)(2,1)S(1)}, bf16[2,256,128]{2,1,0:T(8,128)(2,1)S(1)}, u32[]{:S(2)}, u32[]{:S(2)}) collective-permute-start(bf16[2,256,128]{2,1,0:T(8,128)(2,1)S(1)} %pad_maximum_fusion.refs_0_), channel_id=1, source_target_pairs={{0,4},{4,0},{8,12},{12,8},{16,20},{20,16},{24,28},{28,24},{1,5},{5... | collective-permute-start | bytes 393224 | tf_op jit(solution)/shard_map/ppermute | solution.py:251
  44.0 7.3 %collective-permute-start.4 = (bf16[2,256,128]{2,1,0:T(8,128)(2,1)S(1)}, bf16[2,256,128]{2,1,0:T(8,128)(2,1)S(1)}, u32[]{:S(2)}, u32[]{:S(2)}) collective-permute-start(bf16[2,256,128]{2,1,0:T(8,128)(2,1)S(1)} %pad_maximum_fusion.refs_0_), channel_id=1, source_target_pairs={{0,1},{1,0},{2,3},{3,2},{4,5},{5,4},{6,7},{7,6},{8,9},{9,8},{10,11... | collective-permute-start | bytes 393224 | tf_op jit(solution)/shard_map/ppermute | solution.py:258
  48.7 2.5 %collective-permute-start.5 = (bf16[2,256,128]{2,1,0:T(8,128)(2,1)S(1)}, bf16[2,256,128]{2,1,0:T(8,128)(2,1)S(1)}, u32[]{:S(2)}, u32[]{:S(2)}) collective-permute-start(bf16[2,256,128]{2,1,0:T(8,128)(2,1)S(1)} %collective-permute-done.1.refs_1_), channel_id=1, source_target_pairs={{0,1},{1,0},{2,3},{3,2},{4,5},{5,4},{6,7},{7,6},{8,9},{9,8},{10,11... | collective-permute-start | bytes 393224 | tf_op jit(solution)/shard_map/ppermute | solution.py:258
  48.8 2.4 %collective-permute-start.6 = (bf16[2,256,128]{2,1,0:T(8,128)(2,1)S(1)}, bf16[2,256,128]{2,1,0:T(8,128)(2,1)S(1)}, u32[]{:S(2)}, u32[]{:S(2)}) collective-permute-start(bf16[2,256,128]{2,1,0:T(8,128)(2,1)S(1)} %collective-permute-done.2.refs_2_), channel_id=1, source_target_pairs={{0,1},{1,0},{2,3},{3,2},{4,5},{5,4},{6,7},{7,6},{8,9},{9,8},{10,11... | collective-permute-start | bytes 393224 | tf_op jit(solution)/shard_map/ppermute | solution.py:258
  49.3 2.0 %collective-permute-start.7 = (bf16[2,256,128]{2,1,0:T(8,128)(2,1)S(1)}, bf16[2,256,128]{2,1,0:T(8,128)(2,1)S(1)}, u32[]{:S(2)}, u32[]{:S(2)}) collective-permute-start(bf16[2,256,128]{2,1,0:T(8,128)(2,1)S(1)} %collective-permute-done.3.refs_3_), channel_id=1, source_target_pairs={{0,1},{1,0},{2,3},{3,2},{4,5},{5,4},{6,7},{7,6},{8,9},{9,8},{10,11... | collective-permute-start | bytes 393224 | tf_op jit(solution)/shard_map/ppermute | solution.py:258
  54.2 2.0 %collective-permute-start.8 = (bf16[8,2,2,2,32,128]{5,4,3,2,1,0:T(8,128)(2,1)S(1)}, bf16[8,2,2,2,32,128]{5,4,3,2,1,0:T(8,128)(2,1)S(1)}, u32[]{:S(2)}, u32[]{:S(2)}) collective-permute-start(bf16[8,2,2,2,32,128]{5,4,3,2,1,0:T(8,128)(2,1)S(1)} %slice_bitcast_fusion), channel_id=1, source_target_pairs={{0,1},{1,0},{2,3},{3,2},{4,5},{5,4},{6,7},{7,6},{8,9},{9,8},{10,11... | collective-permute-start | bytes 1572872 | tf_op jit(solution)/shard_map/ppermute | solution.py:287
  55.4 7.5 %copy-start.2 = (s32[16,2]{0,1:T(2,128)S(1)}, s32[16,2]{0,1:T(2,128)}, u32[]{:S(2)}) copy-start(s32[16,2]{0,1:T(2,128)} %param.17) | copy-start | bytes 388
  55.4 7.7 %copy-start.3 = (f32[2,120]{1,0:T(2,128)S(1)}, f32[2,120]{1,0:T(2,128)}, u32[]{:S(2)}) copy-start(f32[2,120]{1,0:T(2,128)} %param.14) | copy-start | bytes 2884
  55.4 7.8 %copy-start.4 = (f32[32]{0:T(128)S(1)}, f32[32]{0:T(128)}, u32[]{:S(2)}) copy-start(f32[32]{0:T(128)} %param.15) | copy-start | bytes 388
  55.4 7.9 %copy-start.5 = (f32[2]{0:T(128)S(1)}, f32[2]{0:T(128)}, u32[]{:S(2)}) copy-start(f32[2]{0:T(128)} %constant.24.clone) | copy-start | bytes 28
  57.3 21.4 %copy-start.1 = (f32[2,2,3600]{2,1,0:T(2,128)S(1)}, f32[2,2,3600]{2,1,0:T(2,128)}, u32[]{:S(2)}) copy-start(f32[2,2,3600]{2,1,0:T(2,128)} %param.13) | copy-start | bytes 172804
  57.3 21.1 %all-to-all-start.1 = ((bf16[16,2,2,32,128]{4,3,2,1,0:T(8,128)(2,1)}), bf16[16,2,2,32,128]{4,3,2,1,0:T(8,128)(2,1)S(1)}, u32[]{:S(2)}, u32[]{:S(2)}) async-start(bf16[16,2,2,32,128]{4,3,2,1,0:T(8,128)(2,1)} %bitcast.13), calls=%async_computation.1 | async-start | bytes 1048576 | tf_op jit(solution)/shard_map/all_to_all | solution.py:294

commit v4 on v3

--- a/solution.py
+++ b/solution.py
@@ -105,35 +105,17 @@
         send.wait()
 
 
-def mix_kernel(local, where, ids_ref, w_ref, out_ref):
-    n_pair, slots = ids_ref.shape[0], ids_ref.shape[2]
-    me = where[0]
-    side = out_ref.shape[1]
-    group = lax.broadcasted_iota(jnp.int32, (GROUP, side), 1) // GROUP
-    inner = lax.broadcasted_iota(jnp.int32, (GROUP, side), 1) % GROUP
-    diagonal = lax.broadcasted_iota(jnp.int32, (GROUP, side), 0) == inner
-    for k in range(n_pair):
-        for lp in range(local):
-            acc = jnp.zeros((GROUP, side), F32)
-            for j in range(slots):
-                i = ids_ref[k, lp, j]
-                source = ((i // local) ^ me) * local + i % local
-                acc = acc + jnp.where(group == source, w_ref[k, lp, j], 0.0)
-            first = (k * local + lp) * GROUP
-            out_ref[first : first + GROUP, :] = jnp.where(diagonal, acc, 0.0).astype(BF)
-
-
-def couple_kernel(n_pair, blocks, sides, shape, where, panels, mix_ref, *refs):
+def couple_kernel(n_pair, blocks, sides, shape, table, panels, *refs):
     half = n_pair // 2
     mats = refs[: half * sides]
-    out_ref, proj, mixed, mat = refs[half * sides :]
+    out_ref, proj, mixed, mat, mix_ref = refs[half * sides :]
     local, rank, part, freqs = shape
     total = n_pair * local
     wide = part // LANES
     rest = part - wide * LANES
     rows = rank // blocks
     lanes = freqs * LANES
-    me, aux = where[0], where[1]
+    me, aux = lax.axis_index("pair"), lax.axis_index("aux")
     take = freqs // sides
 
     def keep(first, index, value):
@@ -142,9 +124,26 @@
             count, GROUP, lanes
         )
 
+    half_group = GROUP // 2
+    lane = lax.broadcasted_iota(jnp.int32, (half_group, total * GROUP), 1)
+    row = lax.broadcasted_iota(jnp.int32, (half_group, total * GROUP), 0)
+    column = lane % GROUP
+    group = lane // GROUP
+    group = (((group // local) ^ me) * local + group % local).astype(F32)
+    slots = table.shape[2] // local
+
     for k in range(n_pair):
         for lp in range(local):
             index = k * local + lp
+            acc = jnp.zeros((half_group, total * GROUP), F32)
+            for j in range(lp * slots, (lp + 1) * slots):
+                acc = acc + jnp.where(group == table[k, 0, j], table[k, 1, j], 0.0)
+            both = [
+                jnp.where(column == row + shift, acc, 0.0) for shift in (0, half_group)
+            ]
+            mix_ref[index * GROUP : (index + 1) * GROUP, :] = jnp.concatenate(both, axis=0).astype(
+                BF
+            )
             for s in range(freqs):
                 slot, inner = s // take, s % take
                 first = (lp * take + inner) * rank
@@ -216,7 +215,6 @@
     rest = part - wide * LANES
     chunk_rows = wide * rank + rest
     sides = 2 if n_aux % 2 == 0 and freqs % 2 == 0 else 1
-    where = jnp.stack([me_pair, me_aux]).astype(jnp.int32)
     vmem = pl.BlockSpec(memory_space=pltpu.VMEM)
     smem = pl.BlockSpec(memory_space=pltpu.SMEM)
 
@@ -250,21 +248,10 @@
         if k < far:
             pieces[k] = lax.ppermute(pieces[0], "pair", flip(n_pair, k))
     tail = jnp.stack([piece[:, share_rows - 16 :] for piece in pieces], axis=1)
-    tail = tail.reshape(n_pair, 16, LANES)
-    ids = tail[:, 0, : local * slots].reshape(n_pair, local, slots).astype(jnp.int32)
-    scale = tail[:, 1, : local * slots].reshape(n_pair, local, slots).astype(F32)
+    table = tail.reshape(n_pair, 16, LANES)[:, :2, : local * slots].astype(F32)
     if sides == 2:
         for k in range(far):
             pieces.append(lax.ppermute(pieces[k], "aux", flip(n_aux, 1)))
-    mix = pl.pallas_call(
-        functools.partial(mix_kernel, local),
-        out_shape=jax.ShapeDtypeStruct((total * GROUP, total * GROUP), BF),
-        in_specs=[smem] * 3,
-        out_specs=vmem,
-        compiler_params=pltpu.CompilerParams(vmem_limit_bytes=8 * 2**20),
-        cost_estimate=pl.CostEstimate(flops=10**6, bytes_accessed=2**17, transcendentals=0),
-    )(where, ids, scale)
-
     out_dims = (2 if even else 1, n_pair, max(blocks // 2, 1), local, freqs, rows_pad, LANES)
     flops = 4 * total * part * rank * freqs * LANES
     coupled = pl.pallas_call(
@@ -272,16 +259,17 @@
             couple_kernel, n_pair, blocks, sides, (local, rank, part, freqs)
         ),
         out_shape=jax.ShapeDtypeStruct(out_dims, BF if even else F32),
-        in_specs=[smem] + [vmem] * (2 + far * sides),
+        in_specs=[smem] + [vmem] * (1 + far * sides),
         out_specs=vmem,
         scratch_shapes=[
             pltpu.VMEM((part // GROUP, total, GROUP, freqs * LANES), BF),
             pltpu.VMEM((total, part, freqs * LANES), BF),
             pltpu.VMEM((total, rank, freqs * LANES), BF),
+            pltpu.VMEM((total * GROUP, total * GROUP), BF),
         ],
         compiler_params=pltpu.CompilerParams(vmem_limit_bytes=40 * 2**20),
         cost_estimate=pl.CostEstimate(flops=flops, bytes_accessed=4 * 2**20, transcendentals=0),
-    )(where, received, mix, *pieces)
+    )(table, received, *pieces)
 
     if even:
         other = lax.ppermute(coupled[1], "aux", flip(n_aux, 1))

time: 79.7 us -> 79.2 us (level)
  Pallas kernels: 7.4 us -> 5.92 us
  waiting for transfers between devices: 46.6 us -> 48 us
    pallas_call x1 -> x0, Pallas kernels: 1.63 us -> none  [body(): pl.pallas_call(functools.partial(mix_kernel, local), out_shape=jax.ShapeD...]
    ppermute x4, waiting for transfers between devices: 0.01 us -> 1.26 us  [body(): pieces.append(lax.ppermute(pieces[k], 'aux', flip(n_aux, 1)))]
  transfers between devices with their start and end apart: 11 -> 11, of which waited for: 6 -> 9; matrix products, arithmetic and copies ran while one was open for 2% -> 2% of each run, Pallas kernels for 2% -> 0%
where the time goes in v4:
time: 79.2 us; the launch traced here: 78.7 us
  waiting for transfers between devices  48 us (61%)
  starting transfers between devices  20.5 us (26%)
  Pallas kernels  5.92 us (7%)
  other arithmetic  2.9 us (4%)
    ppermute x1, waiting for transfers between devices, body(): other = lax.ppermute(share, 'pair', flip(n_pair, far))  27.1 us
    all_to_all x1, waiting for transfers between devices, body(): lax.all_to_all(mine, ('pair', 'aux'), 0, 0, axis_index_groups=groups, til...  13.9 us
    all_to_all x1, starting transfers between devices, body(): received = lax.all_to_all(chunks, 'pair', 0, 0, tiled=True)  7.43 us
    all_to_all x1, starting transfers between devices, body(): lax.all_to_all(mine, ('pair', 'aux'), 0, 0, axis_index_groups=groups, til...  5.72 us
    ppermute x3, waiting for transfers between devices, body(): pieces[k] = lax.ppermute(pieces[0], 'pair', flip(n_pair, k))  4.74 us
    ppermute x3, starting transfers between devices, body(): pieces[k] = lax.ppermute(pieces[0], 'pair', flip(n_pair, k))  3.55 us
    pallas_call x1, Pallas kernels, body(): pl.pallas_call(functools.partial(couple_kernel, n_pair, blocks, sides, (l...  3.04 us
    ppermute x1, starting transfers between devices, body(): other = lax.ppermute(share, 'pair', flip(n_pair, far))  2.92 us
  transfers between devices with their start and end apart: 11, of which 9 were waited for; matrix products, arithmetic and copies ran while one was open for 2% of the time, Pallas kernels for 0%

profile of v4, /device:TPU:0, one launch (start us, length us, event | category | flops | bytes accessed | tf_op | source)
XLA Modules:
  0.0 78.7 jit_solution(8010903661013051336)
XLA Ops:
  0.0 2.9 %shard_map.109 = (bf16[8,2,272,128]{3,2,1,0:T(8,128)(2,1)}, bf16[256,128]{1,0:T(8,128)(2,1)}) custom-call(bf16[2,120,2304]{2,1,0:T(8,128)(2,1)} %refs_0_.1, bf16[2,2,120,120]{3,2,1,0:T(8,128)(2,1)} %refs_1_.1, s32[2,16]{1,0:T(2,128)} %bitcast.29, s32[2,8]{1,0:T(2,128)} %refs_3_.1, s32[2]{0:T(128)} %refs_4_.1, f32[32,32]{1,0:T(8,128)} %refs_5_.1), custom_call_target="tpu_custom_call" | custom-call | bytes 4194304 | tf_op jit(solution)/shard_map/pallas_call | solution.py:224
  2.9 0.0 copy-start
  2.9 7.4 %all-to-all-start = ((bf16[8,2,272,128]{3,2,1,0:T(8,128)(2,1)}), bf16[8,2,272,128]{3,2,1,0:T(8,128)(2,1)S(1)}, u32[]{:S(2)}, u32[]{:S(2)}) async-start(bf16[8,2,272,128]{3,2,1,0:T(8,128)(2,1)} %get-tuple-element.8), calls=%async_computation | async-start | bytes 2228224 | tf_op jit(solution)/shard_map/all_to_all | solution.py:246
  10.3 0.0 copy-done
  10.3 2.9 %collective-permute-start = (bf16[256,128]{1,0:T(8,128)(2,1)S(1)}, bf16[256,128]{1,0:T(8,128)(2,1)S(1)}, u32[]{:S(2)}, u32[]{:S(2)}) collective-permute-start(bf16[256,128]{1,0:T(8,128)(2,1)S(1)} %copy-done), channel_id=1, source_target_pairs={{0,16},{4,20},{8,24},{12,28},{16,0},{20,4},{24,8},{28,12},{1,17},{... | collective-permute-start | bytes 196616 | tf_op jit(solution)/shard_map/ppermute | solution.py:244
  13.3 27.1 %collective-permute-done = bf16[256,128]{1,0:T(8,128)(2,1)S(1)} collective-permute-done((bf16[256,128]{1,0:T(8,128)(2,1)S(1)}, bf16[256,128]{1,0:T(8,128)(2,1)S(1)}, u32[]{:S(2)}, u32[]{:S(2)}) %collective-permute-start) | collective-permute-done | bytes 65568 | tf_op jit(solution)/shard_map/ppermute | solution.py:244
  40.3 0.1 collective-permute-start.3
  40.4 2.9 %collective-permute-start.2 = (bf16[2,256,128]{2,1,0:T(8,128)(2,1)S(1)}, bf16[2,256,128]{2,1,0:T(8,128)(2,1)S(1)}, u32[]{:S(2)}, u32[]{:S(2)}) collective-permute-start(bf16[2,256,128]{2,1,0:T(8,128)(2,1)S(1)} %pad_maximum_fusion.refs_0_), channel_id=1, source_target_pairs={{0,8},{4,12},{8,0},{12,4},{16,24},{20,28},{24,16},{28,20},{1,9},{5... | collective-permute-start | bytes 393224 | tf_op jit(solution)/shard_map/ppermute | solution.py:249
  43.3 0.6 collective-permute-start.1
  43.9 0.0 collective-permute-start.4
  43.9 3.1 %collective-permute-done.3.refs_3_ = bf16[2,256,128]{2,1,0:T(8,128)(2,1)S(1)} collective-permute-done((bf16[2,256,128]{2,1,0:T(8,128)(2,1)S(1)}, bf16[2,256,128]{2,1,0:T(8,128)(2,1)S(1)}, u32[]{:S(2)}, u32[]{:S(2)}) %collective-permute-start.3) | collective-permute-done | bytes 131104 | tf_op jit(solution)/shard_map/ppermute | solution.py:249
  46.9 1.6 %collective-permute-done.2.refs_2_ = bf16[2,256,128]{2,1,0:T(8,128)(2,1)S(1)} collective-permute-done((bf16[2,256,128]{2,1,0:T(8,128)(2,1)S(1)}, bf16[2,256,128]{2,1,0:T(8,128)(2,1)S(1)}, u32[]{:S(2)}, u32[]{:S(2)}) %collective-permute-start.2) | collective-permute-done | bytes 131104 | tf_op jit(solution)/shard_map/ppermute | solution.py:249
  48.6 0.1 collective-permute-done.1.refs_1_
  48.7 0.1 collective-permute-start.5
  48.7 0.5 collective-permute-start.6
  49.2 0.1 collective-permute-start.7
  49.3 0.0 collective-permute-done.4.refs_4_
  49.3 0.8 collective-permute-done.5.refs_5_
  50.1 0.2 collective-permute-done.6.refs_6_
  50.3 0.3 collective-permute-done.7.refs_7_
  50.6 0.0 all-to-all-done.panels
  50.6 3.0 %shard_map.110 = bf16[2,8,2,2,2,32,128]{6,5,4,3,2,1,0:T(8,128)(2,1)S(1)} custom-call(f32[8,2,16]{2,1,0:T(2,128)S(1)} %slice_convert_fusion.table, bf16[8,2,272,128]{3,2,1,0:T(8,128)(2,1)S(1)} %all-to-all-done.panels, bf16[2,256,128]{2,1,0:T(8,128)(2,1)S(1)} %pad_maximum_fusion.refs_0_, bf16[2,256,128]{2,1,0:T(8,128)(2,1)S(1)} %collective-permute-done.1.refs_1_, ...), custom_call_target="tpu_custom_call" | custom-call | flops 566231040 | bytes 4194304 | tf_op jit(solution)/shard_map/pallas_call | solution.py:257
  53.7 0.3 collective-permute-start.8
  54.6 0.0 copy-start.2
  54.6 0.0 copy-start.3
  54.6 0.0 copy-start.4
  54.6 0.0 copy-start.5
  54.6 1.0 %collective-permute-done.8 = bf16[8,2,2,2,32,128]{5,4,3,2,1,0:T(8,128)(2,1)S(1)} collective-permute-done((bf16[8,2,2,2,32,128]{5,4,3,2,1,0:T(8,128)(2,1)S(1)}, bf16[8,2,2,2,32,128]{5,4,3,2,1,0:T(8,128)(2,1)S(1)}, u32[]{:S(2)}, u32[]{:S(2)}) %collective-permute-start.8) | collective-permute-done | bytes 524320 | tf_op jit(solution)/shard_map/ppermute | solution.py:275
  55.7 1.0 %fusion = bf16[8,2,2,2,32,128]{5,4,3,2,1,0:T(8,128)(2,1)} fusion(bf16[8,2,2,2,32,128]{5,4,3,2,1,0:T(8,128)(2,1)S(1)} %collective-permute-done.8, bf16[2,8,2,2,2,32,128]{6,5,4,3,2,1,0:T(8,128)(2,1)S(1)} %shard_map.110), kind=kLoop, calls=%fused_computation.1 | loop fusion | flops 1048576 | bytes 1572864 | tf_op jit(solution)/shard_map/convert_element_type | solution.py:276
  56.7 0.0 copy-start.1
  56.7 5.7 %all-to-all-start.1 = ((bf16[16,2,2,32,128]{4,3,2,1,0:T(8,128)(2,1)}), bf16[16,2,2,32,128]{4,3,2,1,0:T(8,128)(2,1)S(1)}, u32[]{:S(2)}, u32[]{:S(2)}) async-start(bf16[16,2,2,32,128]{4,3,2,1,0:T(8,128)(2,1)} %bitcast.11), calls=%async_computation.1 | async-start | bytes 1048576 | tf_op jit(solution)/shard_map/all_to_all | solution.py:282
  62.4 0.0 copy-done.2
  62.4 0.1 constant_dynamic-slice_fusion
  62.5 0.1 copy.15
  62.6 0.0 copy-done.3
  62.6 0.1 constant_dynamic-slice_fusion.1
  62.7 0.0 copy-done.4
  62.7 0.2 fusion.3
  62.8 0.0 copy-done.5
  62.8 0.1 add_subtract_fusion
  62.9 0.9 %convert_multiply_fusion = f32[2,2,30,120]{3,2,1,0:T(8,128)S(1)} fusion(bf16[2,2,120,120]{3,2,1,0:T(8,128)(2,1)} %refs_1_.1, s32[]{:T(128)S(6)} %select_n.7, f32[2]{0:T(128)S(1)} %broadcast_multiply_fusion, f32[2,30,120]{2,1,0:T(8,128)S(1)} %add_subtract_fusion), kind=kLoop, calls=%fused_computation.8 | loop fusion | flops 43200 | bytes 115212 | tf_op jit(solution)/shard_map/mul | solution.py:306
  63.8 0.1 reshape.23
  63.9 13.9 %all-to-all-done.1 = bf16[16,2,2,32,128]{4,3,2,1,0:T(8,128)(2,1)S(1)} async-done(((bf16[16,2,2,32,128]{4,3,2,1,0:T(8,128)(2,1)}), bf16[16,2,2,32,128]{4,3,2,1,0:T(8,128)(2,1)S(1)}, u32[]{:S(2)}, u32[]{:S(2)}) %all-to-all-start.1) | async-done | bytes 524320 | tf_op jit(solution)/shard_map/all_to_all | solution.py:282
  77.8 0.1 convert_reduce_fusion
  77.9 0.1 reshape.26
  78.0 0.0 copy-done.1
  78.0 0.7 add_add_fusion
  (10 shorter events, 0.1 us)
Async XLA Ops:
  2.9 7.4 %copy-start = (bf16[256,128]{1,0:T(8,128)(2,1)S(1)}, bf16[256,128]{1,0:T(8,128)(2,1)}, u32[]{:S(2)}) copy-start(bf16[256,128]{1,0:T(8,128)(2,1)} %get-tuple-element.7) | copy-start | bytes 196612
  2.9 47.7 %all-to-all-start = ((bf16[8,2,272,128]{3,2,1,0:T(8,128)(2,1)}), bf16[8,2,272,128]{3,2,1,0:T(8,128)(2,1)S(1)}, u32[]{:S(2)}, u32[]{:S(2)}) async-start(bf16[8,2,272,128]{3,2,1,0:T(8,128)(2,1)} %get-tuple-element.8), calls=%async_computation | async-start | bytes 2228224 | tf_op jit(solution)/shard_map/all_to_all | solution.py:246
  10.3 30.0 %collective-permute-start = (bf16[256,128]{1,0:T(8,128)(2,1)S(1)}, bf16[256,128]{1,0:T(8,128)(2,1)S(1)}, u32[]{:S(2)}, u32[]{:S(2)}) collective-permute-start(bf16[256,128]{1,0:T(8,128)(2,1)S(1)} %copy-done), channel_id=1, source_target_pairs={{0,16},{4,20},{8,24},{12,28},{16,0},{20,4},{24,8},{28,12},{1,17},{... | collective-permute-start | bytes 196616 | tf_op jit(solution)/shard_map/ppermute | solution.py:244
  40.3 6.6 %collective-permute-start.3 = (bf16[2,256,128]{2,1,0:T(8,128)(2,1)S(1)}, bf16[2,256,128]{2,1,0:T(8,128)(2,1)S(1)}, u32[]{:S(2)}, u32[]{:S(2)}) collective-permute-start(bf16[2,256,128]{2,1,0:T(8,128)(2,1)S(1)} %pad_maximum_fusion.refs_0_), channel_id=1, source_target_pairs={{0,12},{4,8},{8,4},{12,0},{16,28},{20,24},{24,20},{28,16},{1,13},{... | collective-permute-start | bytes 393224 | tf_op jit(solution)/shard_map/ppermute | solution.py:249
  40.4 8.2 %collective-permute-start.2 = (bf16[2,256,128]{2,1,0:T(8,128)(2,1)S(1)}, bf16[2,256,128]{2,1,0:T(8,128)(2,1)S(1)}, u32[]{:S(2)}, u32[]{:S(2)}) collective-permute-start(bf16[2,256,128]{2,1,0:T(8,128)(2,1)S(1)} %pad_maximum_fusion.refs_0_), channel_id=1, source_target_pairs={{0,8},{4,12},{8,0},{12,4},{16,24},{20,28},{24,16},{28,20},{1,9},{5... | collective-permute-start | bytes 393224 | tf_op jit(solution)/shard_map/ppermute | solution.py:249
  43.3 5.4 %collective-permute-start.1 = (bf16[2,256,128]{2,1,0:T(8,128)(2,1)S(1)}, bf16[2,256,128]{2,1,0:T(8,128)(2,1)S(1)}, u32[]{:S(2)}, u32[]{:S(2)}) collective-permute-start(bf16[2,256,128]{2,1,0:T(8,128)(2,1)S(1)} %pad_maximum_fusion.refs_0_), channel_id=1, source_target_pairs={{0,4},{4,0},{8,12},{12,8},{16,20},{20,16},{24,28},{28,24},{1,5},{5... | collective-permute-start | bytes 393224 | tf_op jit(solution)/shard_map/ppermute | solution.py:249
  43.9 5.4 %collective-permute-start.4 = (bf16[2,256,128]{2,1,0:T(8,128)(2,1)S(1)}, bf16[2,256,128]{2,1,0:T(8,128)(2,1)S(1)}, u32[]{:S(2)}, u32[]{:S(2)}) collective-permute-start(bf16[2,256,128]{2,1,0:T(8,128)(2,1)S(1)} %pad_maximum_fusion.refs_0_), channel_id=1, source_target_pairs={{0,1},{1,0},{2,3},{3,2},{4,5},{5,4},{6,7},{7,6},{8,9},{9,8},{10,11... | collective-permute-start | bytes 393224 | tf_op jit(solution)/shard_map/ppermute | solution.py:254
  48.7 1.4 %collective-permute-start.5 = (bf16[2,256,128]{2,1,0:T(8,128)(2,1)S(1)}, bf16[2,256,128]{2,1,0:T(8,128)(2,1)S(1)}, u32[]{:S(2)}, u32[]{:S(2)}) collective-permute-start(bf16[2,256,128]{2,1,0:T(8,128)(2,1)S(1)} %collective-permute-done.1.refs_1_), channel_id=1, source_target_pairs={{0,1},{1,0},{2,3},{3,2},{4,5},{5,4},{6,7},{7,6},{8,9},{9,8},{10,11... | collective-permute-start | bytes 393224 | tf_op jit(solution)/shard_map/ppermute | solution.py:254
  48.7 1.5 %collective-permute-start.6 = (bf16[2,256,128]{2,1,0:T(8,128)(2,1)S(1)}, bf16[2,256,128]{2,1,0:T(8,128)(2,1)S(1)}, u32[]{:S(2)}, u32[]{:S(2)}) collective-permute-start(bf16[2,256,128]{2,1,0:T(8,128)(2,1)S(1)} %collective-permute-done.2.refs_2_), channel_id=1, source_target_pairs={{0,1},{1,0},{2,3},{3,2},{4,5},{5,4},{6,7},{7,6},{8,9},{9,8},{10,11... | collective-permute-start | bytes 393224 | tf_op jit(solution)/shard_map/ppermute | solution.py:254
  49.2 1.3 %collective-permute-start.7 = (bf16[2,256,128]{2,1,0:T(8,128)(2,1)S(1)}, bf16[2,256,128]{2,1,0:T(8,128)(2,1)S(1)}, u32[]{:S(2)}, u32[]{:S(2)}) collective-permute-start(bf16[2,256,128]{2,1,0:T(8,128)(2,1)S(1)} %collective-permute-done.3.refs_3_), channel_id=1, source_target_pairs={{0,1},{1,0},{2,3},{3,2},{4,5},{5,4},{6,7},{7,6},{8,9},{9,8},{10,11... | collective-permute-start | bytes 393224 | tf_op jit(solution)/shard_map/ppermute | solution.py:254
  53.7 2.0 %collective-permute-start.8 = (bf16[8,2,2,2,32,128]{5,4,3,2,1,0:T(8,128)(2,1)S(1)}, bf16[8,2,2,2,32,128]{5,4,3,2,1,0:T(8,128)(2,1)S(1)}, u32[]{:S(2)}, u32[]{:S(2)}) collective-permute-start(bf16[8,2,2,2,32,128]{5,4,3,2,1,0:T(8,128)(2,1)S(1)} %slice_bitcast_fusion), channel_id=1, source_target_pairs={{0,1},{1,0},{2,3},{3,2},{4,5},{5,4},{6,7},{7,6},{8,9},{9,8},{10,11... | collective-permute-start | bytes 1572872 | tf_op jit(solution)/shard_map/ppermute | solution.py:275
  54.6 7.8 %copy-start.2 = (s32[16,2]{0,1:T(2,128)S(1)}, s32[16,2]{0,1:T(2,128)}, u32[]{:S(2)}) copy-start(s32[16,2]{0,1:T(2,128)} %param.17) | copy-start | bytes 388
  54.6 8.0 %copy-start.3 = (f32[2,120]{1,0:T(2,128)S(1)}, f32[2,120]{1,0:T(2,128)}, u32[]{:S(2)}) copy-start(f32[2,120]{1,0:T(2,128)} %param.14) | copy-start | bytes 2884
  54.6 8.0 %copy-start.4 = (f32[32]{0:T(128)S(1)}, f32[32]{0:T(128)}, u32[]{:S(2)}) copy-start(f32[32]{0:T(128)} %param.15) | copy-start | bytes 388
  54.6 8.2 %copy-start.5 = (f32[2]{0:T(128)S(1)}, f32[2]{0:T(128)}, u32[]{:S(2)}) copy-start(f32[2]{0:T(128)} %constant.24.clone) | copy-start | bytes 28
  56.7 21.4 %copy-start.1 = (f32[2,2,3600]{2,1,0:T(2,128)S(1)}, f32[2,2,3600]{2,1,0:T(2,128)}, u32[]{:S(2)}) copy-start(f32[2,2,3600]{2,1,0:T(2,128)} %param.13) | copy-start | bytes 172804
  56.7 21.2 %all-to-all-start.1 = ((bf16[16,2,2,32,128]{4,3,2,1,0:T(8,128)(2,1)}), bf16[16,2,2,32,128]{4,3,2,1,0:T(8,128)(2,1)S(1)}, u32[]{:S(2)}, u32[]{:S(2)}) async-start(bf16[16,2,2,32,128]{4,3,2,1,0:T(8,128)(2,1)} %bitcast.11), calls=%async_computation.1 | async-start | bytes 1048576 | tf_op jit(solution)/shard_map/all_to_all | solution.py:282

commit v5 on v4

--- a/solution.py
+++ b/solution.py
@@ -12,10 +12,6 @@
 GROUP = 16
 BF = jnp.bfloat16
 F32 = jnp.float32
-
-
-def round_up(value, unit):
-    return -(-value // unit) * unit
 
 
 def flip(count, bits):
@@ -172,6 +168,7 @@
         mixed[:, g * GROUP : (g + 1) * GROUP, :] = found.astype(BF).reshape(total, GROUP, lanes)
 
     for k in range(n_pair):
+        parts = []
         for lp in range(local):
             index = k * local + lp
             got = None
@@ -188,13 +185,20 @@
                     preferred_element_type=F32,
                 )[:rank]
                 got = more if got is None else got + more
-            for h in range(blocks):
-                side = aux % 2 ^ (h % 2) if blocks > 1 else 0
-                for s in range(freqs):
-                    freq = (s // take ^ (aux % 2)) * take + s % take if sides == 2 else s
-                    out_ref[side, me ^ k, h // 2, lp, freq, :rows, :] = got[
-                        h * rows : (h + 1) * rows, s * LANES : (s + 1) * LANES
-                    ].astype(out_ref.dtype)
+            parts.append(got)
+        for h in range(blocks):
+            side = aux % 2 ^ (h % 2) if blocks > 1 else 0
+            pieces = []
+            for lp in range(local):
+                for f in range(freqs):
+                    here = f * LANES
+                    there = ((f // take ^ 1) * take + f % take) * LANES if sides == 2 else here
+                    block = parts[lp][h * rows : (h + 1) * rows]
+                    value = block[:, here : here + LANES]
+                    if sides == 2:
+                        value = jnp.where(aux % 2 == 0, value, block[:, there : there + LANES])
+                    pieces.append(value)
+            out_ref[side, me ^ k, h // 2] = jnp.concatenate(pieces, axis=0).astype(out_ref.dtype)
 
 
 def body(sizes, panels, amplitudes, drive, pno_energy, occ_energy, frequency, pair_lmo,
@@ -207,7 +211,6 @@
     even = rank % n_aux == 0 and n_aux % 2 == 0
     blocks = n_aux if even else 1
     rows = rank // blocks
-    rows_pad = round_up(rows, 16)
     part = width // n_pair
     me_pair = lax.axis_index("pair")
     me_aux = lax.axis_index("aux")
@@ -252,7 +255,8 @@
     if sides == 2:
         for k in range(far):
             pieces.append(lax.ppermute(pieces[k], "aux", flip(n_aux, 1)))
-    out_dims = (2 if even else 1, n_pair, max(blocks // 2, 1), local, freqs, rows_pad, LANES)
+    packed = local * freqs * rows
+    out_dims = (2 if even else 1, n_pair, max(blocks // 2, 1), packed, LANES)
     flops = 4 * total * part * rank * freqs * LANES
     coupled = pl.pallas_call(
         functools.partial(
@@ -282,11 +286,11 @@
         parts = lax.all_to_all(
             mine, ("pair", "aux"), 0, 0, axis_index_groups=groups, tiled=True
         )
-        coupled_share = jnp.sum(parts.astype(F32), axis=0)[:, :, :rows, :rank].reshape(
+        coupled_share = jnp.sum(parts.astype(F32), axis=0)[:, :rank].reshape(
             local, freqs, rows * rank
         )
     else:
-        flat = coupled.reshape(total, freqs, rows_pad, LANES)[:, :, :rank, :rank]
+        flat = coupled.reshape(total, freqs, rank, LANES)[:, :, :, :rank]
         flat = flat.reshape(total, freqs, rank * rank)
         share_aux = lax.psum_scatter(flat, "aux", scatter_dimension=2, tiled=True)
         coupled_share = lax.psum_scatter(share_aux, "pair", scatter_dimension=0, tiled=True)

time: 79.2 us -> 78.4 us (0.990)
    all_to_all x1, waiting for transfers between devices: 13.9 us -> 12.7 us  [body(): lax.all_to_all(mine, ('pair', 'aux'), 0, 0, axis_index_groups=groups, til...]
where the time goes in v5:
time: 78.4 us; the launch traced here: 78 us
  waiting for transfers between devices  47.4 us (60%)
  starting transfers between devices  20.5 us (26%)
  Pallas kernels  5.91 us (8%)
  other arithmetic  2.8 us (4%)
    ppermute x1, waiting for transfers between devices, body(): other = lax.ppermute(share, 'pair', flip(n_pair, far))  27.1 us
    all_to_all x1, waiting for transfers between devices, body(): lax.all_to_all(mine, ('pair', 'aux'), 0, 0, axis_index_groups=groups, til...  12.7 us
    all_to_all x1, starting transfers between devices, body(): received = lax.all_to_all(chunks, 'pair', 0, 0, tiled=True)  7.43 us
    all_to_all x1, starting transfers between devices, body(): lax.all_to_all(mine, ('pair', 'aux'), 0, 0, axis_index_groups=groups, til...  5.72 us
    ppermute x3, waiting for transfers between devices, body(): pieces[k] = lax.ppermute(pieces[0], 'pair', flip(n_pair, k))  4.74 us
    ppermute x3, starting transfers between devices, body(): pieces[k] = lax.ppermute(pieces[0], 'pair', flip(n_pair, k))  3.55 us
    pallas_call x1, Pallas kernels, body(): pl.pallas_call(functools.partial(couple_kernel, n_pair, blocks, sides, (l...  3.02 us
    ppermute x1, starting transfers between devices, body(): other = lax.ppermute(share, 'pair', flip(n_pair, far))  2.92 us
  transfers between devices with their start and end apart: 11, of which 9 were waited for; matrix products, arithmetic and copies ran while one was open for 2% of the time, Pallas kernels for 0%

profile of v5, /device:TPU:0, one launch (start us, length us, event | category | flops | bytes accessed | tf_op | source)
XLA Modules:
  0.0 78.0 jit_solution(18230846167582599968)
XLA Ops:
  0.0 2.9 %shard_map.109 = (bf16[8,2,272,128]{3,2,1,0:T(8,128)(2,1)}, bf16[256,128]{1,0:T(8,128)(2,1)}) custom-call(bf16[2,120,2304]{2,1,0:T(8,128)(2,1)} %refs_0_.1, bf16[2,2,120,120]{3,2,1,0:T(8,128)(2,1)} %refs_1_.1, s32[2,16]{1,0:T(2,128)} %bitcast.29, s32[2,8]{1,0:T(2,128)} %refs_3_.1, s32[2]{0:T(128)} %refs_4_.1, f32[32,32]{1,0:T(8,128)} %refs_5_.1), custom_call_target="tpu_custom_call" | custom-call | bytes 4194304 | tf_op jit(solution)/shard_map/pallas_call | solution.py:227
  2.9 0.0 copy-start
  2.9 7.4 %all-to-all-start = ((bf16[8,2,272,128]{3,2,1,0:T(8,128)(2,1)}), bf16[8,2,272,128]{3,2,1,0:T(8,128)(2,1)S(1)}, u32[]{:S(2)}, u32[]{:S(2)}) async-start(bf16[8,2,272,128]{3,2,1,0:T(8,128)(2,1)} %get-tuple-element.8), calls=%async_computation | async-start | bytes 2228224 | tf_op jit(solution)/shard_map/all_to_all | solution.py:249
  10.3 0.0 copy-done
  10.3 2.9 %collective-permute-start = (bf16[256,128]{1,0:T(8,128)(2,1)S(1)}, bf16[256,128]{1,0:T(8,128)(2,1)S(1)}, u32[]{:S(2)}, u32[]{:S(2)}) collective-permute-start(bf16[256,128]{1,0:T(8,128)(2,1)S(1)} %copy-done), channel_id=1, source_target_pairs={{0,16},{4,20},{8,24},{12,28},{16,0},{20,4},{24,8},{28,12},{1,17},{... | collective-permute-start | bytes 196616 | tf_op jit(solution)/shard_map/ppermute | solution.py:247
  13.3 27.1 %collective-permute-done = bf16[256,128]{1,0:T(8,128)(2,1)S(1)} collective-permute-done((bf16[256,128]{1,0:T(8,128)(2,1)S(1)}, bf16[256,128]{1,0:T(8,128)(2,1)S(1)}, u32[]{:S(2)}, u32[]{:S(2)}) %collective-permute-start) | collective-permute-done | bytes 65568 | tf_op jit(solution)/shard_map/ppermute | solution.py:247
  40.3 0.1 collective-permute-start.3
  40.4 2.9 %collective-permute-start.2 = (bf16[2,256,128]{2,1,0:T(8,128)(2,1)S(1)}, bf16[2,256,128]{2,1,0:T(8,128)(2,1)S(1)}, u32[]{:S(2)}, u32[]{:S(2)}) collective-permute-start(bf16[2,256,128]{2,1,0:T(8,128)(2,1)S(1)} %pad_maximum_fusion.refs_0_), channel_id=1, source_target_pairs={{0,8},{4,12},{8,0},{12,4},{16,24},{20,28},{24,16},{28,20},{1,9},{5... | collective-permute-start | bytes 393224 | tf_op jit(solution)/shard_map/ppermute | solution.py:252
  43.3 0.6 collective-permute-start.1
  43.9 0.0 collective-permute-start.4
  43.9 3.1 %collective-permute-done.3.refs_3_ = bf16[2,256,128]{2,1,0:T(8,128)(2,1)S(1)} collective-permute-done((bf16[2,256,128]{2,1,0:T(8,128)(2,1)S(1)}, bf16[2,256,128]{2,1,0:T(8,128)(2,1)S(1)}, u32[]{:S(2)}, u32[]{:S(2)}) %collective-permute-start.3) | collective-permute-done | bytes 131104 | tf_op jit(solution)/shard_map/ppermute | solution.py:252
  46.9 1.6 %collective-permute-done.2.refs_2_ = bf16[2,256,128]{2,1,0:T(8,128)(2,1)S(1)} collective-permute-done((bf16[2,256,128]{2,1,0:T(8,128)(2,1)S(1)}, bf16[2,256,128]{2,1,0:T(8,128)(2,1)S(1)}, u32[]{:S(2)}, u32[]{:S(2)}) %collective-permute-start.2) | collective-permute-done | bytes 131104 | tf_op jit(solution)/shard_map/ppermute | solution.py:252
  48.6 0.1 collective-permute-done.1.refs_1_
  48.7 0.1 collective-permute-start.5
  48.7 0.5 collective-permute-start.6
  49.2 0.1 collective-permute-start.7
  49.3 0.0 collective-permute-done.4.refs_4_
  49.3 0.8 collective-permute-done.5.refs_5_
  50.1 0.2 collective-permute-done.6.refs_6_
  50.3 0.3 collective-permute-done.7.refs_7_
  50.6 0.0 all-to-all-done.panels
  50.6 3.0 %shard_map.110 = bf16[2,8,2,120,128]{4,3,2,1,0:T(8,128)(2,1)S(1)} custom-call(f32[8,2,16]{2,1,0:T(2,128)S(1)} %slice_convert_fusion.table, bf16[8,2,272,128]{3,2,1,0:T(8,128)(2,1)S(1)} %all-to-all-done.panels, bf16[2,256,128]{2,1,0:T(8,128)(2,1)S(1)} %pad_maximum_fusion.refs_0_, bf16[2,256,128]{2,1,0:T(8,128)(2,1)S(1)} %collective-permute-done.1.refs_1_, ...), custom_call_target="tpu_custom_call" | custom-call | flops 566231040 | bytes 4194304 | tf_op jit(solution)/shard_map/pallas_call | solution.py:261
  53.7 0.3 collective-permute-start.8
  53.9 0.0 copy-start.2
  53.9 0.0 copy-start.3
  53.9 0.0 copy-start.4
  53.9 0.0 copy-start.5
  53.9 1.7 %collective-permute-done.8 = bf16[8,2,120,128]{3,2,1,0:T(8,128)(2,1)S(1)} collective-permute-done((bf16[8,2,120,128]{3,2,1,0:T(8,128)(2,1)S(1)}, bf16[8,2,120,128]{3,2,1,0:T(8,128)(2,1)S(1)}, u32[]{:S(2)}, u32[]{:S(2)}) %collective-permute-start.8) | collective-permute-done | bytes 491552 | tf_op jit(solution)/shard_map/ppermute | solution.py:279
  55.6 0.9 %fusion = bf16[8,2,120,128]{3,2,1,0:T(8,128)(2,1)} fusion(bf16[8,2,120,128]{3,2,1,0:T(8,128)(2,1)S(1)} %collective-permute-done.8, bf16[2,8,2,120,128]{4,3,2,1,0:T(8,128)(2,1)S(1)} %shard_map.110), kind=kLoop, calls=%fused_computation.1 | loop fusion | flops 983040 | bytes 1474560 | tf_op jit(solution)/shard_map/convert_element_type | solution.py:280
  56.5 0.0 copy-start.1
  56.5 5.7 %all-to-all-start.1 = ((bf16[16,120,128]{2,1,0:T(8,128)(2,1)}), bf16[16,120,128]{2,1,0:T(8,128)(2,1)S(1)}, u32[]{:S(2)}, u32[]{:S(2)}) async-start(bf16[16,120,128]{2,1,0:T(8,128)(2,1)} %bitcast.11), calls=%async_computation.1 | async-start | bytes 983040 | tf_op jit(solution)/shard_map/all_to_all | solution.py:286
  62.2 0.0 copy-done.2
  62.2 0.1 constant_dynamic-slice_fusion
  63.0 0.1 copy.15
  63.1 0.0 copy-done.3
  63.1 0.1 constant_dynamic-slice_fusion.1
  63.1 0.0 copy-done.4
  63.1 0.2 fusion.3
  63.3 0.0 copy-done.5
  63.3 0.1 add_subtract_fusion
  63.4 0.9 %convert_multiply_fusion = f32[2,2,30,120]{3,2,1,0:T(8,128)S(1)} fusion(bf16[2,2,120,120]{3,2,1,0:T(8,128)(2,1)} %refs_1_.1, s32[]{:T(128)S(6)} %select_n.7, f32[2]{0:T(128)S(1)} %broadcast_multiply_fusion, f32[2,30,120]{2,1,0:T(8,128)S(1)} %add_subtract_fusion), kind=kLoop, calls=%fused_computation.8 | loop fusion | flops 43200 | bytes 115212 | tf_op jit(solution)/shard_map/mul | solution.py:310
  64.3 0.1 reshape.23
  64.4 12.7 %all-to-all-done.1 = bf16[16,120,128]{2,1,0:T(8,128)(2,1)S(1)} async-done(((bf16[16,120,128]{2,1,0:T(8,128)(2,1)}), bf16[16,120,128]{2,1,0:T(8,128)(2,1)S(1)}, u32[]{:S(2)}, u32[]{:S(2)}) %all-to-all-start.1) | async-done | bytes 491552 | tf_op jit(solution)/shard_map/all_to_all | solution.py:286
  77.1 0.1 convert_reduce_fusion
  77.2 0.1 reshape.26
  77.3 0.0 copy-done.1
  77.3 0.7 add_add_fusion
  (10 shorter events, 0.1 us)
Async XLA Ops:
  2.9 7.4 %copy-start = (bf16[256,128]{1,0:T(8,128)(2,1)S(1)}, bf16[256,128]{1,0:T(8,128)(2,1)}, u32[]{:S(2)}) copy-start(bf16[256,128]{1,0:T(8,128)(2,1)} %get-tuple-element.7) | copy-start | bytes 196612
  2.9 47.7 %all-to-all-start = ((bf16[8,2,272,128]{3,2,1,0:T(8,128)(2,1)}), bf16[8,2,272,128]{3,2,1,0:T(8,128)(2,1)S(1)}, u32[]{:S(2)}, u32[]{:S(2)}) async-start(bf16[8,2,272,128]{3,2,1,0:T(8,128)(2,1)} %get-tuple-element.8), calls=%async_computation | async-start | bytes 2228224 | tf_op jit(solution)/shard_map/all_to_all | solution.py:249
  10.3 30.0 %collective-permute-start = (bf16[256,128]{1,0:T(8,128)(2,1)S(1)}, bf16[256,128]{1,0:T(8,128)(2,1)S(1)}, u32[]{:S(2)}, u32[]{:S(2)}) collective-permute-start(bf16[256,128]{1,0:T(8,128)(2,1)S(1)} %copy-done), channel_id=1, source_target_pairs={{0,16},{4,20},{8,24},{12,28},{16,0},{20,4},{24,8},{28,12},{1,17},{... | collective-permute-start | bytes 196616 | tf_op jit(solution)/shard_map/ppermute | solution.py:247
  40.3 6.6 %collective-permute-start.3 = (bf16[2,256,128]{2,1,0:T(8,128)(2,1)S(1)}, bf16[2,256,128]{2,1,0:T(8,128)(2,1)S(1)}, u32[]{:S(2)}, u32[]{:S(2)}) collective-permute-start(bf16[2,256,128]{2,1,0:T(8,128)(2,1)S(1)} %pad_maximum_fusion.refs_0_), channel_id=1, source_target_pairs={{0,12},{4,8},{8,4},{12,0},{16,28},{20,24},{24,20},{28,16},{1,13},{... | collective-permute-start | bytes 393224 | tf_op jit(solution)/shard_map/ppermute | solution.py:252
  40.4 8.2 %collective-permute-start.2 = (bf16[2,256,128]{2,1,0:T(8,128)(2,1)S(1)}, bf16[2,256,128]{2,1,0:T(8,128)(2,1)S(1)}, u32[]{:S(2)}, u32[]{:S(2)}) collective-permute-start(bf16[2,256,128]{2,1,0:T(8,128)(2,1)S(1)} %pad_maximum_fusion.refs_0_), channel_id=1, source_target_pairs={{0,8},{4,12},{8,0},{12,4},{16,24},{20,28},{24,16},{28,20},{1,9},{5... | collective-permute-start | bytes 393224 | tf_op jit(solution)/shard_map/ppermute | solution.py:252
  43.3 5.4 %collective-permute-start.1 = (bf16[2,256,128]{2,1,0:T(8,128)(2,1)S(1)}, bf16[2,256,128]{2,1,0:T(8,128)(2,1)S(1)}, u32[]{:S(2)}, u32[]{:S(2)}) collective-permute-start(bf16[2,256,128]{2,1,0:T(8,128)(2,1)S(1)} %pad_maximum_fusion.refs_0_), channel_id=1, source_target_pairs={{0,4},{4,0},{8,12},{12,8},{16,20},{20,16},{24,28},{28,24},{1,5},{5... | collective-permute-start | bytes 393224 | tf_op jit(solution)/shard_map/ppermute | solution.py:252
  43.9 5.4 %collective-permute-start.4 = (bf16[2,256,128]{2,1,0:T(8,128)(2,1)S(1)}, bf16[2,256,128]{2,1,0:T(8,128)(2,1)S(1)}, u32[]{:S(2)}, u32[]{:S(2)}) collective-permute-start(bf16[2,256,128]{2,1,0:T(8,128)(2,1)S(1)} %pad_maximum_fusion.refs_0_), channel_id=1, source_target_pairs={{0,1},{1,0},{2,3},{3,2},{4,5},{5,4},{6,7},{7,6},{8,9},{9,8},{10,11... | collective-permute-start | bytes 393224 | tf_op jit(solution)/shard_map/ppermute | solution.py:257
  48.7 1.4 %collective-permute-start.5 = (bf16[2,256,128]{2,1,0:T(8,128)(2,1)S(1)}, bf16[2,256,128]{2,1,0:T(8,128)(2,1)S(1)}, u32[]{:S(2)}, u32[]{:S(2)}) collective-permute-start(bf16[2,256,128]{2,1,0:T(8,128)(2,1)S(1)} %collective-permute-done.1.refs_1_), channel_id=1, source_target_pairs={{0,1},{1,0},{2,3},{3,2},{4,5},{5,4},{6,7},{7,6},{8,9},{9,8},{10,11... | collective-permute-start | bytes 393224 | tf_op jit(solution)/shard_map/ppermute | solution.py:257
  48.7 1.5 %collective-permute-start.6 = (bf16[2,256,128]{2,1,0:T(8,128)(2,1)S(1)}, bf16[2,256,128]{2,1,0:T(8,128)(2,1)S(1)}, u32[]{:S(2)}, u32[]{:S(2)}) collective-permute-start(bf16[2,256,128]{2,1,0:T(8,128)(2,1)S(1)} %collective-permute-done.2.refs_2_), channel_id=1, source_target_pairs={{0,1},{1,0},{2,3},{3,2},{4,5},{5,4},{6,7},{7,6},{8,9},{9,8},{10,11... | collective-permute-start | bytes 393224 | tf_op jit(solution)/shard_map/ppermute | solution.py:257
  49.2 1.3 %collective-permute-start.7 = (bf16[2,256,128]{2,1,0:T(8,128)(2,1)S(1)}, bf16[2,256,128]{2,1,0:T(8,128)(2,1)S(1)}, u32[]{:S(2)}, u32[]{:S(2)}) collective-permute-start(bf16[2,256,128]{2,1,0:T(8,128)(2,1)S(1)} %collective-permute-done.3.refs_3_), channel_id=1, source_target_pairs={{0,1},{1,0},{2,3},{3,2},{4,5},{5,4},{6,7},{7,6},{8,9},{9,8},{10,11... | collective-permute-start | bytes 393224 | tf_op jit(solution)/shard_map/ppermute | solution.py:257
  53.7 1.9 %collective-permute-start.8 = (bf16[8,2,120,128]{3,2,1,0:T(8,128)(2,1)S(1)}, bf16[8,2,120,128]{3,2,1,0:T(8,128)(2,1)S(1)}, u32[]{:S(2)}, u32[]{:S(2)}) collective-permute-start(bf16[8,2,120,128]{3,2,1,0:T(8,128)(2,1)S(1)} %slice_bitcast_fusion), channel_id=1, source_target_pairs={{0,1},{1,0},{2,3},{3,2},{4,5},{5,4},{6,7},{7,6},{8,9},{9,8},{10,11... | collective-permute-start | bytes 1474568 | tf_op jit(solution)/shard_map/ppermute | solution.py:279
  53.9 8.3 %copy-start.2 = (s32[16,2]{0,1:T(2,128)S(1)}, s32[16,2]{0,1:T(2,128)}, u32[]{:S(2)}) copy-start(s32[16,2]{0,1:T(2,128)} %param.17) | copy-start | bytes 388
  53.9 9.2 %copy-start.3 = (f32[2,120]{1,0:T(2,128)S(1)}, f32[2,120]{1,0:T(2,128)}, u32[]{:S(2)}) copy-start(f32[2,120]{1,0:T(2,128)} %param.14) | copy-start | bytes 2884
  53.9 9.2 %copy-start.4 = (f32[32]{0:T(128)S(1)}, f32[32]{0:T(128)}, u32[]{:S(2)}) copy-start(f32[32]{0:T(128)} %param.15) | copy-start | bytes 388
  53.9 9.4 %copy-start.5 = (f32[2]{0:T(128)S(1)}, f32[2]{0:T(128)}, u32[]{:S(2)}) copy-start(f32[2]{0:T(128)} %constant.24.clone) | copy-start | bytes 28
  56.5 20.8 %copy-start.1 = (f32[2,2,3600]{2,1,0:T(2,128)S(1)}, f32[2,2,3600]{2,1,0:T(2,128)}, u32[]{:S(2)}) copy-start(f32[2,2,3600]{2,1,0:T(2,128)} %param.13) | copy-start | bytes 172804
  56.5 20.6 %all-to-all-start.1 = ((bf16[16,120,128]{2,1,0:T(8,128)(2,1)}), bf16[16,120,128]{2,1,0:T(8,128)(2,1)S(1)}, u32[]{:S(2)}, u32[]{:S(2)}) async-start(bf16[16,120,128]{2,1,0:T(8,128)(2,1)} %bitcast.11), calls=%async_computation.1 | async-start | bytes 983040 | tf_op jit(solution)/shard_map/all_to_all | solution.py:286

commit v6 on v5

--- a/solution.py
+++ b/solution.py
@@ -79,11 +79,12 @@
     for lp in range(local):
         panel_copies[lp].wait()
         keep = lax.broadcasted_iota(jnp.int32, (rank, LANES), 0) < ranks[lp]
+        kept = jnp.where(keep, 1.0, 0.0).astype(BF)
         for k in range(n_pair):
             for w in range(wide):
                 start = pl.multiple_of(((me ^ k) * wide + w) * LANES, LANES)
-                x = panels[lp, :, pl.ds(start, LANES)].astype(F32)
-                chunks[me ^ k, lp, w * rank : (w + 1) * rank, :] = jnp.where(keep, x, 0.0).astype(BF)
+                x = panels[lp, :, pl.ds(start, LANES)]
+                chunks[me ^ k, lp, w * rank : (w + 1) * rank, :] = x * kept
         if rest:
             for t in range(n_pair * rest // LANES):
                 start = n_pair * wide * LANES + t * LANES

time: 78.4 us -> 78.4 us (level)
  no operation moved by 1% of the time
where the time goes in v6:
time: 78.4 us; the launch traced here: 78 us
  waiting for transfers between devices  47.4 us (60%)
  starting transfers between devices  20.5 us (26%)
  Pallas kernels  5.87 us (7%)
  other arithmetic  2.8 us (4%)
    ppermute x1, waiting for transfers between devices, body(): other = lax.ppermute(share, 'pair', flip(n_pair, far))  27.1 us
    all_to_all x1, waiting for transfers between devices, body(): lax.all_to_all(mine, ('pair', 'aux'), 0, 0, axis_index_groups=groups, til...  12.7 us
    all_to_all x1, starting transfers between devices, body(): received = lax.all_to_all(chunks, 'pair', 0, 0, tiled=True)  7.43 us
    all_to_all x1, starting transfers between devices, body(): lax.all_to_all(mine, ('pair', 'aux'), 0, 0, axis_index_groups=groups, til...  5.73 us
    ppermute x3, waiting for transfers between devices, body(): pieces[k] = lax.ppermute(pieces[0], 'pair', flip(n_pair, k))  4.74 us
    ppermute x3, starting transfers between devices, body(): pieces[k] = lax.ppermute(pieces[0], 'pair', flip(n_pair, k))  3.55 us
    pallas_call x1, Pallas kernels, body(): pl.pallas_call(functools.partial(couple_kernel, n_pair, blocks, sides, (l...  3.02 us
    ppermute x1, starting transfers between devices, body(): other = lax.ppermute(share, 'pair', flip(n_pair, far))  2.92 us
  transfers between devices with their start and end apart: 11, of which 9 were waited for; matrix products, arithmetic and copies ran while one was open for 2% of the time, Pallas kernels for 0%

profile of v6, /device:TPU:0, one launch (start us, length us, event | category | flops | bytes accessed | tf_op | source)
XLA Modules:
  0.0 78.0 jit_solution(12611532032770730361)
XLA Ops:
  0.0 2.8 %shard_map.109 = (bf16[8,2,272,128]{3,2,1,0:T(8,128)(2,1)}, bf16[256,128]{1,0:T(8,128)(2,1)}) custom-call(bf16[2,120,2304]{2,1,0:T(8,128)(2,1)} %refs_0_.1, bf16[2,2,120,120]{3,2,1,0:T(8,128)(2,1)} %refs_1_.1, s32[2,16]{1,0:T(2,128)} %bitcast.29, s32[2,8]{1,0:T(2,128)} %refs_3_.1, s32[2]{0:T(128)} %refs_4_.1, f32[32,32]{1,0:T(8,128)} %refs_5_.1), custom_call_target="tpu_custom_call" | custom-call | bytes 4194304 | tf_op jit(solution)/shard_map/pallas_call | solution.py:228
  2.9 0.0 copy-start
  2.9 7.4 %all-to-all-start = ((bf16[8,2,272,128]{3,2,1,0:T(8,128)(2,1)}), bf16[8,2,272,128]{3,2,1,0:T(8,128)(2,1)S(1)}, u32[]{:S(2)}, u32[]{:S(2)}) async-start(bf16[8,2,272,128]{3,2,1,0:T(8,128)(2,1)} %get-tuple-element.8), calls=%async_computation | async-start | bytes 2228224 | tf_op jit(solution)/shard_map/all_to_all | solution.py:250
  10.3 0.0 copy-done
  10.3 2.9 %collective-permute-start = (bf16[256,128]{1,0:T(8,128)(2,1)S(1)}, bf16[256,128]{1,0:T(8,128)(2,1)S(1)}, u32[]{:S(2)}, u32[]{:S(2)}) collective-permute-start(bf16[256,128]{1,0:T(8,128)(2,1)S(1)} %copy-done), channel_id=1, source_target_pairs={{0,16},{4,20},{8,24},{12,28},{16,0},{20,4},{24,8},{28,12},{1,17},{... | collective-permute-start | bytes 196616 | tf_op jit(solution)/shard_map/ppermute | solution.py:248
  13.2 27.1 %collective-permute-done = bf16[256,128]{1,0:T(8,128)(2,1)S(1)} collective-permute-done((bf16[256,128]{1,0:T(8,128)(2,1)S(1)}, bf16[256,128]{1,0:T(8,128)(2,1)S(1)}, u32[]{:S(2)}, u32[]{:S(2)}) %collective-permute-start) | collective-permute-done | bytes 65568 | tf_op jit(solution)/shard_map/ppermute | solution.py:248
  40.3 0.1 collective-permute-start.3
  40.4 2.9 %collective-permute-start.2 = (bf16[2,256,128]{2,1,0:T(8,128)(2,1)S(1)}, bf16[2,256,128]{2,1,0:T(8,128)(2,1)S(1)}, u32[]{:S(2)}, u32[]{:S(2)}) collective-permute-start(bf16[2,256,128]{2,1,0:T(8,128)(2,1)S(1)} %pad_maximum_fusion.refs_0_), channel_id=1, source_target_pairs={{0,8},{4,12},{8,0},{12,4},{16,24},{20,28},{24,16},{28,20},{1,9},{5... | collective-permute-start | bytes 393224 | tf_op jit(solution)/shard_map/ppermute | solution.py:253
  43.2 0.6 collective-permute-start.1
  43.8 0.0 collective-permute-start.4
  43.9 3.1 %collective-permute-done.3.refs_3_ = bf16[2,256,128]{2,1,0:T(8,128)(2,1)S(1)} collective-permute-done((bf16[2,256,128]{2,1,0:T(8,128)(2,1)S(1)}, bf16[2,256,128]{2,1,0:T(8,128)(2,1)S(1)}, u32[]{:S(2)}, u32[]{:S(2)}) %collective-permute-start.3) | collective-permute-done | bytes 131104 | tf_op jit(solution)/shard_map/ppermute | solution.py:253
  46.9 1.6 %collective-permute-done.2.refs_2_ = bf16[2,256,128]{2,1,0:T(8,128)(2,1)S(1)} collective-permute-done((bf16[2,256,128]{2,1,0:T(8,128)(2,1)S(1)}, bf16[2,256,128]{2,1,0:T(8,128)(2,1)S(1)}, u32[]{:S(2)}, u32[]{:S(2)}) %collective-permute-start.2) | collective-permute-done | bytes 131104 | tf_op jit(solution)/shard_map/ppermute | solution.py:253
  48.5 0.1 collective-permute-done.1.refs_1_
  48.6 0.1 collective-permute-start.5
  48.7 0.5 collective-permute-start.6
  49.2 0.1 collective-permute-start.7
  49.3 0.0 collective-permute-done.4.refs_4_
  49.3 0.8 collective-permute-done.5.refs_5_
  50.0 0.2 collective-permute-done.6.refs_6_
  50.2 0.3 collective-permute-done.7.refs_7_
  50.5 0.0 all-to-all-done.panels
  50.6 3.0 %shard_map.110 = bf16[2,8,2,120,128]{4,3,2,1,0:T(8,128)(2,1)S(1)} custom-call(f32[8,2,16]{2,1,0:T(2,128)S(1)} %slice_convert_fusion.table, bf16[8,2,272,128]{3,2,1,0:T(8,128)(2,1)S(1)} %all-to-all-done.panels, bf16[2,256,128]{2,1,0:T(8,128)(2,1)S(1)} %pad_maximum_fusion.refs_0_, bf16[2,256,128]{2,1,0:T(8,128)(2,1)S(1)} %collective-permute-done.1.refs_1_, ...), custom_call_target="tpu_custom_call" | custom-call | flops 566231040 | bytes 4194304 | tf_op jit(solution)/shard_map/pallas_call | solution.py:262
  53.6 0.3 collective-permute-start.8
  53.9 0.0 copy-start.2
  53.9 0.0 copy-start.3
  53.9 0.0 copy-start.4
  53.9 0.0 copy-start.5
  53.9 1.7 %collective-permute-done.8 = bf16[8,2,120,128]{3,2,1,0:T(8,128)(2,1)S(1)} collective-permute-done((bf16[8,2,120,128]{3,2,1,0:T(8,128)(2,1)S(1)}, bf16[8,2,120,128]{3,2,1,0:T(8,128)(2,1)S(1)}, u32[]{:S(2)}, u32[]{:S(2)}) %collective-permute-start.8) | collective-permute-done | bytes 491552 | tf_op jit(solution)/shard_map/ppermute | solution.py:280
  55.6 0.9 %fusion = bf16[8,2,120,128]{3,2,1,0:T(8,128)(2,1)} fusion(bf16[8,2,120,128]{3,2,1,0:T(8,128)(2,1)S(1)} %collective-permute-done.8, bf16[2,8,2,120,128]{4,3,2,1,0:T(8,128)(2,1)S(1)} %shard_map.110), kind=kLoop, calls=%fused_computation.1 | loop fusion | flops 983040 | bytes 1474560 | tf_op jit(solution)/shard_map/convert_element_type | solution.py:281
  56.5 0.0 copy-start.1
  56.5 5.7 %all-to-all-start.1 = ((bf16[16,120,128]{2,1,0:T(8,128)(2,1)}), bf16[16,120,128]{2,1,0:T(8,128)(2,1)S(1)}, u32[]{:S(2)}, u32[]{:S(2)}) async-start(bf16[16,120,128]{2,1,0:T(8,128)(2,1)} %bitcast.11), calls=%async_computation.1 | async-start | bytes 983040 | tf_op jit(solution)/shard_map/all_to_all | solution.py:287
  62.2 0.0 copy-done.2
  62.2 0.1 constant_dynamic-slice_fusion
  63.0 0.1 copy.15
  63.0 0.0 copy-done.3
  63.0 0.1 constant_dynamic-slice_fusion.1
  63.1 0.0 copy-done.4
  63.1 0.2 fusion.3
  63.3 0.0 copy-done.5
  63.3 0.1 add_subtract_fusion
  63.4 0.9 %convert_multiply_fusion = f32[2,2,30,120]{3,2,1,0:T(8,128)S(1)} fusion(bf16[2,2,120,120]{3,2,1,0:T(8,128)(2,1)} %refs_1_.1, s32[]{:T(128)S(6)} %select_n.7, f32[2]{0:T(128)S(1)} %broadcast_multiply_fusion, f32[2,30,120]{2,1,0:T(8,128)S(1)} %add_subtract_fusion), kind=kLoop, calls=%fused_computation.8 | loop fusion | flops 43200 | bytes 115212 | tf_op jit(solution)/shard_map/mul | solution.py:311
  64.2 0.1 reshape.23
  64.4 12.7 %all-to-all-done.1 = bf16[16,120,128]{2,1,0:T(8,128)(2,1)S(1)} async-done(((bf16[16,120,128]{2,1,0:T(8,128)(2,1)}), bf16[16,120,128]{2,1,0:T(8,128)(2,1)S(1)}, u32[]{:S(2)}, u32[]{:S(2)}) %all-to-all-start.1) | async-done | bytes 491552 | tf_op jit(solution)/shard_map/all_to_all | solution.py:287
  77.1 0.1 convert_reduce_fusion
  77.1 0.1 reshape.26
  77.3 0.0 copy-done.1
  77.3 0.7 add_add_fusion
  (10 shorter events, 0.1 us)
Async XLA Ops:
  2.9 7.4 %copy-start = (bf16[256,128]{1,0:T(8,128)(2,1)S(1)}, bf16[256,128]{1,0:T(8,128)(2,1)}, u32[]{:S(2)}) copy-start(bf16[256,128]{1,0:T(8,128)(2,1)} %get-tuple-element.7) | copy-start | bytes 196612
  2.9 47.7 %all-to-all-start = ((bf16[8,2,272,128]{3,2,1,0:T(8,128)(2,1)}), bf16[8,2,272,128]{3,2,1,0:T(8,128)(2,1)S(1)}, u32[]{:S(2)}, u32[]{:S(2)}) async-start(bf16[8,2,272,128]{3,2,1,0:T(8,128)(2,1)} %get-tuple-element.8), calls=%async_computation | async-start | bytes 2228224 | tf_op jit(solution)/shard_map/all_to_all | solution.py:250
  10.3 30.0 %collective-permute-start = (bf16[256,128]{1,0:T(8,128)(2,1)S(1)}, bf16[256,128]{1,0:T(8,128)(2,1)S(1)}, u32[]{:S(2)}, u32[]{:S(2)}) collective-permute-start(bf16[256,128]{1,0:T(8,128)(2,1)S(1)} %copy-done), channel_id=1, source_target_pairs={{0,16},{4,20},{8,24},{12,28},{16,0},{20,4},{24,8},{28,12},{1,17},{... | collective-permute-start | bytes 196616 | tf_op jit(solution)/shard_map/ppermute | solution.py:248
  40.3 6.6 %collective-permute-start.3 = (bf16[2,256,128]{2,1,0:T(8,128)(2,1)S(1)}, bf16[2,256,128]{2,1,0:T(8,128)(2,1)S(1)}, u32[]{:S(2)}, u32[]{:S(2)}) collective-permute-start(bf16[2,256,128]{2,1,0:T(8,128)(2,1)S(1)} %pad_maximum_fusion.refs_0_), channel_id=1, source_target_pairs={{0,12},{4,8},{8,4},{12,0},{16,28},{20,24},{24,20},{28,16},{1,13},{... | collective-permute-start | bytes 393224 | tf_op jit(solution)/shard_map/ppermute | solution.py:253
  40.4 8.2 %collective-permute-start.2 = (bf16[2,256,128]{2,1,0:T(8,128)(2,1)S(1)}, bf16[2,256,128]{2,1,0:T(8,128)(2,1)S(1)}, u32[]{:S(2)}, u32[]{:S(2)}) collective-permute-start(bf16[2,256,128]{2,1,0:T(8,128)(2,1)S(1)} %pad_maximum_fusion.refs_0_), channel_id=1, source_target_pairs={{0,8},{4,12},{8,0},{12,4},{16,24},{20,28},{24,16},{28,20},{1,9},{5... | collective-permute-start | bytes 393224 | tf_op jit(solution)/shard_map/ppermute | solution.py:253
  43.2 5.4 %collective-permute-start.1 = (bf16[2,256,128]{2,1,0:T(8,128)(2,1)S(1)}, bf16[2,256,128]{2,1,0:T(8,128)(2,1)S(1)}, u32[]{:S(2)}, u32[]{:S(2)}) collective-permute-start(bf16[2,256,128]{2,1,0:T(8,128)(2,1)S(1)} %pad_maximum_fusion.refs_0_), channel_id=1, source_target_pairs={{0,4},{4,0},{8,12},{12,8},{16,20},{20,16},{24,28},{28,24},{1,5},{5... | collective-permute-start | bytes 393224 | tf_op jit(solution)/shard_map/ppermute | solution.py:253
  43.8 5.4 %collective-permute-start.4 = (bf16[2,256,128]{2,1,0:T(8,128)(2,1)S(1)}, bf16[2,256,128]{2,1,0:T(8,128)(2,1)S(1)}, u32[]{:S(2)}, u32[]{:S(2)}) collective-permute-start(bf16[2,256,128]{2,1,0:T(8,128)(2,1)S(1)} %pad_maximum_fusion.refs_0_), channel_id=1, source_target_pairs={{0,1},{1,0},{2,3},{3,2},{4,5},{5,4},{6,7},{7,6},{8,9},{9,8},{10,11... | collective-permute-start | bytes 393224 | tf_op jit(solution)/shard_map/ppermute | solution.py:258
  48.6 1.4 %collective-permute-start.5 = (bf16[2,256,128]{2,1,0:T(8,128)(2,1)S(1)}, bf16[2,256,128]{2,1,0:T(8,128)(2,1)S(1)}, u32[]{:S(2)}, u32[]{:S(2)}) collective-permute-start(bf16[2,256,128]{2,1,0:T(8,128)(2,1)S(1)} %collective-permute-done.1.refs_1_), channel_id=1, source_target_pairs={{0,1},{1,0},{2,3},{3,2},{4,5},{5,4},{6,7},{7,6},{8,9},{9,8},{10,11... | collective-permute-start | bytes 393224 | tf_op jit(solution)/shard_map/ppermute | solution.py:258
  48.7 1.5 %collective-permute-start.6 = (bf16[2,256,128]{2,1,0:T(8,128)(2,1)S(1)}, bf16[2,256,128]{2,1,0:T(8,128)(2,1)S(1)}, u32[]{:S(2)}, u32[]{:S(2)}) collective-permute-start(bf16[2,256,128]{2,1,0:T(8,128)(2,1)S(1)} %collective-permute-done.2.refs_2_), channel_id=1, source_target_pairs={{0,1},{1,0},{2,3},{3,2},{4,5},{5,4},{6,7},{7,6},{8,9},{9,8},{10,11... | collective-permute-start | bytes 393224 | tf_op jit(solution)/shard_map/ppermute | solution.py:258
  49.2 1.3 %collective-permute-start.7 = (bf16[2,256,128]{2,1,0:T(8,128)(2,1)S(1)}, bf16[2,256,128]{2,1,0:T(8,128)(2,1)S(1)}, u32[]{:S(2)}, u32[]{:S(2)}) collective-permute-start(bf16[2,256,128]{2,1,0:T(8,128)(2,1)S(1)} %collective-permute-done.3.refs_3_), channel_id=1, source_target_pairs={{0,1},{1,0},{2,3},{3,2},{4,5},{5,4},{6,7},{7,6},{8,9},{9,8},{10,11... | collective-permute-start | bytes 393224 | tf_op jit(solution)/shard_map/ppermute | solution.py:258
  53.6 1.9 %collective-permute-start.8 = (bf16[8,2,120,128]{3,2,1,0:T(8,128)(2,1)S(1)}, bf16[8,2,120,128]{3,2,1,0:T(8,128)(2,1)S(1)}, u32[]{:S(2)}, u32[]{:S(2)}) collective-permute-start(bf16[8,2,120,128]{3,2,1,0:T(8,128)(2,1)S(1)} %slice_bitcast_fusion), channel_id=1, source_target_pairs={{0,1},{1,0},{2,3},{3,2},{4,5},{5,4},{6,7},{7,6},{8,9},{9,8},{10,11... | collective-permute-start | bytes 1474568 | tf_op jit(solution)/shard_map/ppermute | solution.py:280
  53.9 8.3 %copy-start.2 = (s32[16,2]{0,1:T(2,128)S(1)}, s32[16,2]{0,1:T(2,128)}, u32[]{:S(2)}) copy-start(s32[16,2]{0,1:T(2,128)} %param.17) | copy-start | bytes 388
  53.9 9.2 %copy-start.3 = (f32[2,120]{1,0:T(2,128)S(1)}, f32[2,120]{1,0:T(2,128)}, u32[]{:S(2)}) copy-start(f32[2,120]{1,0:T(2,128)} %param.14) | copy-start | bytes 2884
  53.9 9.2 %copy-start.4 = (f32[32]{0:T(128)S(1)}, f32[32]{0:T(128)}, u32[]{:S(2)}) copy-start(f32[32]{0:T(128)} %param.15) | copy-start | bytes 388
  53.9 9.4 %copy-start.5 = (f32[2]{0:T(128)S(1)}, f32[2]{0:T(128)}, u32[]{:S(2)}) copy-start(f32[2]{0:T(128)} %constant.24.clone) | copy-start | bytes 28
  56.5 20.8 %copy-start.1 = (f32[2,2,3600]{2,1,0:T(2,128)S(1)}, f32[2,2,3600]{2,1,0:T(2,128)}, u32[]{:S(2)}) copy-start(f32[2,2,3600]{2,1,0:T(2,128)} %param.13) | copy-start | bytes 172804
  56.5 20.6 %all-to-all-start.1 = ((bf16[16,120,128]{2,1,0:T(8,128)(2,1)}), bf16[16,120,128]{2,1,0:T(8,128)(2,1)S(1)}, u32[]{:S(2)}, u32[]{:S(2)}) async-start(bf16[16,120,128]{2,1,0:T(8,128)(2,1)} %bitcast.11), calls=%async_computation.1 | async-start | bytes 983040 | tf_op jit(solution)/shard_map/all_to_all | solution.py:287
